TPU v7x, 128 devices: a whole 4x4x4 slice. The times are simulated.
128 devices in a mesh: tm: 4 (over z_hi, core), ent: 8 (over y, z_lo), batch: 4 (over x).
Axes of the slice: x: 4, y: 4, z: 4 (z_hi: 2, z_lo: 2; z = z_hi * 2 + z_lo), core: 2. Of those that a mesh axis runs over, the one named last changes fastest.
Arguments:
- init_state: float32 [4, 4096, 256], P('batch', 'ent'), may hold values from -6 to 6
- tiles: float32 [4, 4, 16, 512, 512], P('batch', 'tm', 'ent'), may hold values from -0.25 to 0.25
- dst_block: int32 [4, 4, 16], P('batch', 'tm', 'ent'), may hold values from 0 to 7
- rel_id: int32 [4, 4, 16], P('batch', 'tm', 'ent'), may hold values from 0 to 255
- cotangent: float32 [4, 4, 4096, 256], P('batch', 'tm', 'ent'), may hold values from -0.0625 to 0.0625
- rel_emb: float32 [256, 256], replicated, may hold values from -6 to 6
- w_neigh: float32 [256, 256], replicated, may hold values from -0.1875 to 0.1875
- w_self: float32 [256, 256], replicated, may hold values from -0.375 to 0.375
- w_gate: float32 [256, 256], replicated, may hold values from -0.375 to 0.375
- b_gate: float32 [256], replicated, may hold values from -2 to 2
Outputs:
- states: float32 [4, 4, 4096, 256], P('batch', 'tm', 'ent')
- grad_rel: float32 [256, 256], replicated
- grad_neigh: float32 [256, 256], replicated
- grad_self: float32 [256, 256], replicated
- grad_gate: float32 [256, 256], replicated
- grad_bias: float32 [256], replicated
All inputs are finite; a program needn't handle non-finite values.
Results may differ from a plain program's by a relative error of at most 0.00012.
Values sent between devices are 32-bit elements; how exact they have to be, the bound alone decides.
No kernel may reach another device: no remote copies, remote signals or barrier semaphores. Data moves between devices by JAX's collectives and lax.ppermute only.
A program may use at most 64 MiB of HBM per device.

v0:
```python
import functools
import math

import jax
import jax.numpy as jnp
from jax import lax
from jax.experimental import pallas as pl
from jax.experimental.pallas import tpu as pltpu
from jax.sharding import Mesh
from jax.sharding import PartitionSpec as P


INTERPRET = False
VMEM_LIMIT = 16 * 1024 * 1024

AXES = ("zh", "c", "y", "zl", "b")
TM = ("zh", "c")
ENT = ("y", "zl")
Z = ("zh", "zl")
highest = lax.Precision.HIGHEST
F32 = jnp.float32


def product(left, right, dims=((1,), (0,))):
    return lax.dot_general(left, right, (dims, ((), ())), precision=highest, preferred_element_type=F32)


def along(value, axis, steps):
    count = lax.axis_size(axis)
    return lax.ppermute(value, axis, [(i, (i + steps) % count) for i in range(count)])


def swap(value):
    return along(value, "c", 1)


def order(value, after):
    return lax.optimization_barrier((value, after))[0]


def local(kernel, tables, arrays, outs, scratch=(), flops=1_000_000):
    vmem, smem = pl.BlockSpec(memory_space=pltpu.VMEM), pl.BlockSpec(memory_space=pltpu.SMEM)
    size = sum(a.size for a in arrays) + sum(math.prod(o) for o in outs if not isinstance(o, int))
    return pl.pallas_call(
        kernel,
        out_shape=[
            jax.ShapeDtypeStruct((o,), jnp.int32) if isinstance(o, int) else jax.ShapeDtypeStruct(o, F32)
            for o in outs
        ],
        in_specs=[smem] * len(tables) + [vmem] * len(arrays),
        out_specs=[smem if isinstance(o, int) else vmem for o in outs],
        scratch_shapes=[pltpu.VMEM(s, F32) for s in scratch],
        cost_estimate=pl.CostEstimate(flops=flops, bytes_accessed=4 * size, transcendentals=0),
        compiler_params=pltpu.CompilerParams(vmem_limit_bytes=VMEM_LIMIT),
        interpret=INTERPRET,
    )(*tables, *arrays)


def ahead(z, s):
    return lax.rem(z + s, 4)


def behind(z, s):
    return lax.rem(z + 4 - s, 4)


def row(i, step):
    return pl.multiple_of(i * step, step)


def give_tiles(place, dst, rel, own, init, cot, out, half):
    c = place[1]
    rows = own.shape[1] // 8
    lane = lax.broadcasted_iota(jnp.int32, (8, own.shape[2]), 1) // 128
    codes = jnp.zeros(lane.shape, F32)
    for j in range(2):
        codes = jnp.where(lane == 2 * j, dst[j].astype(F32), codes)
        codes = jnp.where(lane == 2 * j + 1, rel[j].astype(F32), codes)
    for to in range(4):
        for j in range(2):
            out[to, j * rows : (j + 1) * rows, :] = own[j, pl.ds(row(to * 2 + 1 - c, rows), rows), :]
        out[to, 2 * rows : 2 * rows + 8, :] = codes
        lines = cot[pl.ds(row(to * 2 + 1 - c, rows), rows), :]
        out[to, 2 * rows + 8 :, 0 : cot.shape[1]] = lines[0 : rows // 2]
        out[to, 2 * rows + 8 :, cot.shape[1] :] = lines[rows // 2 :]
    half[...] = init[pl.ds(row(c, half.shape[0]), half.shape[0]), :]


def cut_tiles(core, place, dst, rel, own, got, *outs):
    z, c = place[0], place[1]
    rows = own.shape[1] // 8
    lane = lax.broadcasted_iota(jnp.int32, (8, own.shape[2]), 1) // 128

    @pl.when(c == core)
    def _():
        codes = jnp.zeros(lane.shape, F32)
        for j in range(2):
            codes = jnp.where(lane == 2 * j, dst[j].astype(F32), codes)
            codes = jnp.where(lane == 2 * j + 1, rel[j].astype(F32), codes)
        for s in range(4):
            to = ahead(z, s)
            for j in range(2):
                outs[s][j * rows : (j + 1) * rows, :] = own[j, pl.ds(row(to * 2 + c, rows), rows), :]
            outs[s][2 * rows :, :] = codes

    @pl.when(c != core)
    def _():
        for s in range(4):
            outs[s][...] = got[ahead(z, s), 0 : 2 * rows + 8, :]


def join_tiles(place, p0, p1, p2, p3, early, late, early_ids, late_ids):
    z, y = place[0], place[3]
    rows = early.shape[1]
    for s, piece in enumerate((p0, p1, p2, p3)):
        from_z = behind(z, s)
        b = lax.rem(from_z, 2)

        def write(tiles, ids):
            tiles[b] = piece[0:rows, :]
            for j in range(2):
                dst, rel = (
                    jnp.max(piece[rows : rows + 8, (2 * j + i) * 128 : (2 * j + i + 1) * 128]).astype(jnp.int32)
                    for i in range(2)
                )
                ids[2 * b + j] = lax.rem(lax.div(dst, 2) + 4 - y, 4) * 2 + lax.rem(dst, 2)
                ids[4 + 2 * b + j] = rel

        pl.when(from_z < 2)(functools.partial(write, early, early_ids))
        pl.when(from_z >= 2)(functools.partial(write, late, late_ids))


def spread(ids, tiles, rel_emb, full, slots):
    rows = tiles.shape[1] // 2
    slots[...] = jnp.zeros_like(slots)

    def step(b, carry):
        block = tiles[b]
        part = product(block, full[b])
        sums = jnp.sum(block, axis=1, keepdims=True)
        for j in range(2):
            line = rel_emb[pl.ds(ids[4 + 2 * b + j], 1), :]
            slots[ids[2 * b + j]] += part[j * rows : (j + 1) * rows] + sums[j * rows : (j + 1) * rows] * line
        return carry

    lax.fori_loop(0, 2, step, 0)


def spread_first(place, ids, tiles, rel_emb, init, near, far, o0, o1, o2, o3, own, full, slots):
    z, c, zl = place[0], place[1], place[2]
    half = near.shape[0]
    rows = tiles.shape[1] // 2
    full[zl] = init[...]
    full[1 - zl, pl.ds(row(c, half), half), :] = near[...]
    full[1 - zl, pl.ds(row(1 - c, half), half), :] = far[...]
    at = row(z * 2 + c, rows)
    for b in range(2):
        own[b * rows : (b + 1) * rows, :] = full[b, pl.ds(at, rows), :]
    spread(ids, tiles, rel_emb, full, slots)
    ones = jnp.ones((8, tiles.shape[2]), F32)
    lane = lax.broadcasted_iota(jnp.int32, (1, o0.shape[1]), 1)
    for s, out in enumerate((o0, o1, o2, o3)):
        out[0 : 2 * rows, :] = slots[2 * s : 2 * s + 2].reshape(2 * rows, -1)
        out[2 * rows :, :] = jnp.full((8, out.shape[1]), -1.0, F32)
    for b in range(2):
        sums = product(ones, tiles[b], ((1,), (1,)))
        for j in range(2):
            k = 2 * b + j
            line = jnp.where(lane == rows, ids[k].astype(F32), ids[4 + k].astype(F32))
            for out in (o0, o1, o2, o3):
                out[2 * rows + k : 2 * rows + k + 1, :] = line
                out[2 * rows + k : 2 * rows + k + 1, 0:rows] = sums[0:1, j * rows : (j + 1) * rows]


def pack_ring(place, p0, p1, p2, p3, out):
    rows = out.shape[1]
    for s, piece in enumerate((p0, p1, p2, p3)):
        out[s] = piece[0:rows, :]


def spread_next(place, ids, tiles, rel_emb, p0, p1, p2, p3, other, o0, o1, o2, o3, full, slots):
    z, c = place[0], place[1]
    rows = tiles.shape[1] // 2
    for s, piece in enumerate((p0, p1, p2, p3)):
        from_z = behind(z, s)
        for b in range(2):
            part = slice(b * rows, (b + 1) * rows)
            full[b, pl.ds(row(from_z * 2 + c, rows), rows), :] = piece[part, :]
            full[b, pl.ds(row(from_z * 2 + 1 - c, rows), rows), :] = other[s, part, :]
    spread(ids, tiles, rel_emb, full, slots)
    for s, out in enumerate((o0, o1, o2, o3)):
        out[...] = slots[2 * s : 2 * s + 2].reshape(2 * rows, -1)


def gates(place, state, w_self, w_gate, b_gate, update, self_part):
    held = state[...]
    update[...] = jax.nn.sigmoid(product(held, w_gate[...]) + b_gate[...])
    self_part[...] = product(held, w_self[...])


def advance(place, a0, a1, a2, a3, state, update, self_part, w_neigh, new, agg, candidate):
    rows = state.shape[0]
    total = (a0[0:rows, :] + a1[0:rows, :]) + (a2[0:rows, :] + a3[0:rows, :])
    agg[...] = total
    cand = jnp.tanh(product(total, w_neigh[...]) + self_part[...])
    candidate[...] = cand
    gate = update[...]
    new[...] = gate * cand + (1.0 - gate) * state[...]


def advance_with(place, a0, a1, a2, a3, state, update, self_part, w_neigh, c1, c2, c3, new, agg, candidate, n1, n2, n3):
    advance(place, a0, a1, a2, a3, state, update, self_part, w_neigh, new, agg, candidate)
    rows = new.shape[0]
    for piece, out in ((c1, n1), (c2, n2), (c3, n3)):
        out[0:rows, :] = new[...]
        out[rows:, :] = piece[...].reshape(rows, -1)


def retreat_math(d_new, state, update, candidate, w_neigh, d_pre, d_gate, d_agg, d_keep):
    gate, cand = update[...], candidate[...]
    rest = 1.0 - gate
    pre = d_new * gate * (1.0 - cand * cand)
    d_pre[...] = pre
    d_gate[...] = d_new * (cand - state[...]) * gate * rest
    d_agg[...] = product(pre, w_neigh[...], ((1,), (1,))).reshape(d_agg.shape)
    if d_keep is not None:
        d_keep[...] = d_new * rest


def retreat_last(place, cot, state, update, candidate, w_neigh, d_pre, d_gate, d_agg, d_keep):
    d_new = cot[...].reshape(state.shape)
    retreat_math(d_new, state, update, candidate, w_neigh, d_pre, d_gate, d_agg, d_keep)


def retreat(place, d0, d1, d2, d3, d_prev, cot, state, update, candidate, w_neigh, d_pre, d_gate, d_agg, d_keep):
    came = ((d0[0:2] + d1[0:2]) + (d2[0:2] + d3[0:2]) + cot[...]).reshape(state.shape)
    retreat_math(came + d_prev[...], state, update, candidate, w_neigh, d_pre, d_gate, d_agg, d_keep)


def before(place, d_keep, d_pre, d_gate, w_self, w_gate, d_prev):
    d_prev[...] = (
        d_keep[...]
        + product(d_pre[...], w_self[...], ((1,), (1,)))
        + product(d_gate[...], w_gate[...], ((1,), (1,)))
    )


def gather_back(place, ids, tiles, g0, g1, g2, g3, other, mine, rel_rows, held, res, full):
    z, c = place[0], place[1]
    rows = g0.shape[1]
    for s, piece in enumerate((g0, g1, g2, g3)):
        held[2 * s : 2 * s + 2] = piece[...]

    def step(b, carry):
        block = tiles[b]
        sums = jnp.sum(block, axis=1, keepdims=True)
        for j in range(2):
            value = held[ids[2 * b + j]]
            res[j * rows : (j + 1) * rows, :] = value
            total = jnp.sum(sums[j * rows : (j + 1) * rows] * value, axis=0, keepdims=True)
            rel_rows[2 * b + j] = jnp.broadcast_to(total, rel_rows.shape[1:])
        full[...] = product(block, res[...], ((0,), (0,)))
        for s in range(4):
            to = ahead(z, s)
            mine[s, b] = full[pl.ds(row(to * 2 + c, rows), rows), :]
            other[s, b] = full[pl.ds(row(to * 2 + 1 - c, rows), rows), :]
        return carry

    lax.fori_loop(0, 2, step, 0)


def gather_back_with(place, ids, tiles, g0, g1, g2, g3, s0, s1, s2, s3, other, mine, rel_rows, states, held, res, full):
    c = place[1]
    gather_back(place, ids, tiles, g0, g1, g2, g3, other, mine, rel_rows, held, res, full)
    for s, piece in enumerate((s0, s1, s2, s3)):
        states[s] = piece[2 + c]
        other[4 + s // 2, s % 2] = piece[2 + 1 - c]


def add_pairs(place, mine, got, n0, n1, n2, n3):
    for s, out in enumerate((n0, n1, n2, n3)):
        out[...] = mine[s] + got[s]


def add_pairs_with(place, mine, got, s0, s1, s2, s3, n0, n1, n2, n3):
    for s, (piece, out) in enumerate(((s0, n0), (s1, n1), (s2, n2), (s3, n3))):
        out[0:2] = mine[s] + got[s]
        out[2:4] = piece[...]


def cut_rows(place, own, got, *outs):
    z, c = place[0], place[1]
    rows, width = own.shape[0] // 8, own.shape[1]
    for s in range(4):
        to = ahead(z, s)
        outs[s][c] = own[pl.ds(row(to * 2 + c, rows), rows), :]
        outs[s][1 - c, 0 : rows // 2] = got[to, 2 * rows + 8 :, 0:width]
        outs[s][1 - c, rows // 2 :] = got[to, 2 * rows + 8 :, width:]


def join_rows(place, p0, p1, p2, p3, *refs):
    outs, stack = refs[:4], refs[4]
    z = place[0]
    rows = outs[0].shape[1]
    stack[z] = p0[...]
    for s, piece in enumerate((p1, p2, p3)):
        for core in range(2):
            stack[behind(z, s + 1), core] = piece[(2 + core) * rows : (3 + core) * rows, :]
    for t in range(4):
        for b in range(2):
            outs[t][b] = stack[(t // 2) * 2 + b, t % 2]


def cut_states(place, n0, n1, n2, n3, *refs):
    outs, stack = refs[:4], refs[4]
    z = place[0]
    rows = outs[0].shape[1]
    for t, state in enumerate((n0, n1, n2, n3)):
        for b in range(2):
            stack[(t // 2) * 2 + b, t % 2] = state[b * rows : (b + 1) * rows, :]
    for s in range(4):
        outs[s][...] = stack[ahead(z, s)]


def join_states(place, mine, got, out):
    z, c = place[0], place[1]
    rows = mine.shape[1]
    for s in range(4):
        from_z = behind(z, s)
        out[pl.ds(row(from_z * 2 + c, rows), rows), :] = mine[s]
        out[pl.ds(row(from_z * 2 + 1 - c, rows), rows), :] = got[4 + s // 2, s % 2]


def dense_grads(state, agg, pre, gate_in):
    pairs = ((agg, pre), (state, pre), (state, gate_in))
    return [product(a, b, ((0,), (0,))) for a, b in pairs], jnp.sum(gate_in, axis=0, keepdims=True)


def later_grads(count, place, *refs):
    tables, refs = refs[:count], refs[count:]
    lines, outs, stack = refs[4 * count : 5 * count], refs[5 * count : 5 * count + 5], refs[-1]
    for kind in range(4):
        for i in range(count):
            stack[kind, i] = refs[kind * count + i][...]
    for out in outs:
        out[...] = jnp.zeros_like(out)

    def step(i, carry):
        total, bias = dense_grads(stack[0, i], stack[1, i], stack[2, i], stack[3, i])
        for out, value in zip(outs[1:4], total):
            out[...] += value
        outs[4][...] += jnp.broadcast_to(bias, outs[4].shape)
        return carry

    lax.fori_loop(0, count, step, 0)
    for ids, line in zip(tables, lines):
        for k in range(4):
            outs[0][pl.ds(ids[4 + k], 1), :] += line[k, 0:1, :]


def weight_grads(place, state, agg, pre, gate_in, d_agg, l0, l1, l2, l3, *refs):
    later, d_bias, keep, give = refs[:4], refs[4], refs[5], refs[6]
    c = place[1]
    rows, width = d_agg.shape[1:]
    total, bias = dense_grads(state[...], agg[...], pre[...], gate_in[...])
    d_rel = later[0][...]
    relation = lax.broadcasted_iota(jnp.int32, (8, width), 1).astype(F32)
    for s, piece in enumerate((l0, l1, l2, l3)):
        line = piece[2 * rows :, 0:128]
        slot, rel, sums = line[:, rows : rows + 1], line[:, rows + 1 : rows + 2], line[:, 0:rows]
        found = sum(
            product(jnp.where(slot == float(2 * s + b), sums, 0.0), d_agg[b]) for b in range(2)
        )
        d_rel = d_rel + product((rel == relation).astype(F32), found, ((0,), (0,)))
    total = [d_rel] + [a + b[...] for a, b in zip(total, later[1:])]
    bias = bias + d_bias[0:1, :]
    parts = keep.shape[0]
    chunk = 2 * width // parts
    for out, own_half in ((keep, c == 0), (give, c != 0)):
        for i in range(2):
            value = jnp.where(own_half, total[i], total[2 + i])
            out[i * parts // 2 : (i + 1) * parts // 2, 0:chunk, :] = value.reshape(parts // 2, chunk, width)
        out[:, chunk:, :] = jnp.zeros((parts, out.shape[1] - chunk, width), F32)
        out[0, chunk : chunk + 1, :] = bias


def on_device(
    init_state, tiles, dst_block, rel_id, cotangent, rel_emb, w_neigh, w_self, w_gate, b_gate
):
    z, c, y, zl = lax.axis_index(Z), lax.axis_index("c"), lax.axis_index("y"), lax.axis_index("zl")
    snaps = 4
    tile, width = init_state.shape[1:]
    rows = tile // 8
    bias_row = b_gate.reshape(1, width)
    pair = (2, rows, width)
    flat = (2 * rows, width)

    own_tiles, own_cot, init = tiles[0, 0], cotangent[0, 0], init_state[0]
    here = jnp.stack([z, c, zl, y]).astype(jnp.int32)
    codes = (here, dst_block.reshape(2), rel_id.reshape(2))
    piece = (2 * rows + 8, tile)
    give, half = local(give_tiles, codes, (own_tiles, init, own_cot), [(4, piece[0] + rows // 2, tile), (tile // 2, width)])
    got_tiles = swap(give)
    held, ids = [None] * snaps, [None] * snaps
    part = [local(functools.partial(cut_tiles, core), codes, (own_tiles, got_tiles), [piece] * 4) for core in range(2)]
    ring = [part[0][0]] + [along(part[0][s], Z, s) for s in range(1, 4)]
    near = along(order(half, part[0][1]), "zl", 1)
    far = swap(near)
    cut_cot = local(cut_rows, (here,), (own_cot, got_tiles), [pair] * 4)
    ring, part[1], cut_cot = lax.optimization_barrier((ring, part[1], cut_cot))

    def join(core, ring):
        held[core], held[2 + core], ids[core], ids[2 + core] = local(
            join_tiles, (here,), ring, [(2, 2 * rows, tile)] * 2 + [8, 8]
        )

    join(0, ring)
    work = [(2, tile, width), (8, rows, width)]
    stored, states = [], []
    state = lines = carried = None
    for t in range(snaps):
        if t == 0:
            *to_y, state = local(
                spread_first,
                (here, ids[0]),
                (held[0], rel_emb, init, near, far),
                [(2 * rows + 8, width)] * 4 + [flat],
                work,
            )
        else:
            ring = [state] + [along(carried[s - 1] if carried else state, Z, s) for s in range(1, 4)]
            if carried:
                cots = local(join_rows, (here,), [cut_cot[0]] + ring[1:], [pair] * 4, [(4, 2, rows, width)])
                carried = None
            (packed,) = local(pack_ring, (here,), ring, [(4, *flat)])
            to_y = local(spread_next, (here, ids[t]), [held[t], rel_emb] + ring + [swap(packed)], [flat] * 4, work)
        came_y = [to_y[0]] + [along(to_y[s], "y", s) for s in range(1, 4)]
        if t == 0:
            lines = came_y
            late = [along(part[1][s], Z, s) for s in range(1, 4)]
            join(1, [part[1][0]] + late)
        update, self_part = local(gates, (here,), (state, w_self, w_gate, bias_row), [flat] * 2)
        terms = came_y + [state, update, self_part, w_neigh]
        if t == 1:
            new, agg, candidate, *carried = local(
                advance_with, (here,), terms + list(cut_cot[1:]), [flat] * 3 + [(4 * rows, width)] * 3
            )
        else:
            new, agg, candidate = local(advance, (here,), terms, [flat] * 3)
        stored.append((state, agg, update, candidate))
        states.append(new)
        state = new

    cut = local(cut_states, (here,), states, [pair] * 4, [(4, 2, rows, width)])

    d_prev = d_in = None
    pres, gates_in, rel_lines = [None] * snaps, [None] * snaps, []
    for t in reversed(range(snaps)):
        held_state, agg, update, candidate = stored[t]
        tail = (cots[t], held_state, update, candidate, w_neigh)
        outs = [flat, flat, pair, flat]
        if d_in is None:
            d_pre, d_gate, d_agg, d_keep = local(retreat_last, (here,), tail, outs)
        else:
            d_pre, d_gate, d_agg, d_keep = local(retreat, (here,), (*d_in, d_prev, *tail), outs)
        pres[t], gates_in[t] = d_pre, d_gate
        if t == 0:
            break
        pieces = [d_agg] + [along(d_agg, "y", -s) for s in range(1, 4)]
        (d_prev,) = local(before, (here,), (d_keep, d_pre, d_gate, w_self, w_gate), [flat])
        second = t == snaps - 2
        other, mine_rows, rel_rows, *mine_states = local(
            gather_back_with if second else gather_back,
            (here, ids[t]),
            [held[t]] + pieces + (list(d_in) if second else []),
            [(6 if second else 4, *pair), (4, *pair), (4, 8, width)] + [(4, rows, width)] * second,
            [(8, rows, width), flat, (tile, width)],
        )
        got = swap(other)
        if second:
            (state_out,) = local(join_states, (here,), (*mine_states, got), [(tile, width)])
        rel_lines.append(rel_rows)
        if t == 1:
            square = (width, width)
            later = local(
                functools.partial(later_grads, snaps - 1),
                (here, *ids[1:]),
                [s[0] for s in stored[1:]]
                + [s[1] for s in stored[1:]]
                + pres[1:]
                + gates_in[1:]
                + rel_lines[::-1],
                [square] * 4 + [(8, width)],
                [(4, snaps - 1, *flat)],
                flops=20_000_000_000,
            )
        if t == snaps - 1:
            parts = local(add_pairs_with, (here,), [mine_rows, got] + list(cut), [(4, rows, width)] * 4)
        else:
            parts = local(add_pairs, (here,), (mine_rows, got), [pair] * 4)
        d_in = [parts[0]] + [along(parts[s], Z, s) for s in range(1, 4)]

    parts = 16
    chunk = 2 * width // parts
    size = (parts, chunk + 8, width)
    keep, give = local(
        weight_grads, (here,), (stored[0][0], stored[0][1], d_pre, d_gate, d_agg, *lines, *later), [size] * 2
    )
    plane = ("zh", "zl", "y")
    summed = jnp.sum(lax.all_to_all(keep + swap(give), plane, 0, 0, tiled=True), axis=0)
    summed = (summed + along(summed, "b", 2)) + (along(summed, "b", 1) + along(summed, "b", 3))
    mine_sum = lax.all_to_all(jnp.broadcast_to(summed[None], size), plane, 0, 0, tiled=True)
    other_sum = swap(mine_sum)
    halves = (jnp.where(c == 0, mine_sum, other_sum), jnp.where(c == 0, other_sum, mine_sum))
    grads = [h[:, :chunk].reshape(2, width, width)[i] for h in halves for i in range(2)]
    return (state_out.reshape(1, 1, tile, width), *grads, mine_sum[0, chunk])


def solution(mesh):
    torus = Mesh(mesh.devices.reshape(2, 2, 4, 2, mesh.shape["batch"]), AXES)
    return jax.shard_map(
        on_device,
        mesh=torus,
        in_specs=(
            P("b", ENT, None),
            P("b", TM, ENT, None, None),
            P("b", TM, ENT),
            P("b", TM, ENT),
            P("b", TM, ENT, None),
            P(),
            P(),
            P(),
            P(),
            P(),
        ),
        out_specs=(P("b", TM, ENT, None), P(), P(), P(), P(), P()),
        check_vma=False,
    )
```

profile of v0, /device:TPU:1, one launch (start us, length us, event | category | flops | bytes accessed | tf_op | source)
XLA Modules:
  0.0 282.1 jit_solution(17227084673024643219)
XLA Ops:
  7.8 2.8 collective-permute-done.got
  13.1 3.3 %collective-permute-start.2 = (f32[136,512]{1,0:T(8,128)S(1)}, f32[136,512]{1,0:T(8,128)S(1)}, u32[]{:S(2)}, u32[]{:S(2)}) collective-permute-start(f32[136,512]{1,0:T(8,128)S(1)} %get-tuple-element.136), channel_id=1, source_target_pairs={{0,64},{4,68},{64,0},{68,4},{1,65},{5,69},{65,1},{69,5},{2,66},{6,... | collective-permute-start | bytes 835592 | tf_op jit(solution)/shard_map/ppermute | solution.py:30
  22.2 6.3 %collective-permute-done.2.p2 = f32[136,512]{1,0:T(8,128)S(1)} collective-permute-done((f32[136,512]{1,0:T(8,128)S(1)}, f32[136,512]{1,0:T(8,128)S(1)}, u32[]{:S(2)}, u32[]{:S(2)}) %collective-permute-start.2) | collective-permute-done | bytes 278560 | tf_op jit(solution)/shard_map/ppermute | solution.py:30
  28.4 2.9 %collective-permute-done.3.p3 = f32[136,512]{1,0:T(8,128)S(1)} collective-permute-done((f32[136,512]{1,0:T(8,128)S(1)}, f32[136,512]{1,0:T(8,128)S(1)}, u32[]{:S(2)}, u32[]{:S(2)}) %collective-permute-start.3) | collective-permute-done | bytes 278560 | tf_op jit(solution)/shard_map/ppermute | solution.py:30
  33.2 2.2 shard_map.151
  36.5 2.6 collective-permute-start.10
  41.2 3.0 %collective-permute-done.10.a2.l2 = f32[136,256]{1,0:T(8,128)S(1)} collective-permute-done((f32[136,256]{1,0:T(8,128)S(1)}, f32[136,256]{1,0:T(8,128)S(1)}, u32[]{:S(2)}, u32[]{:S(2)}) %collective-permute-start.10) | collective-permute-done | bytes 139296 | tf_op jit(solution)/shard_map/ppermute | solution.py:30
  45.7 3.5 %collective-permute-start.14 = (f32[128,256]{1,0:T(8,128)S(1)}, f32[128,256]{1,0:T(8,128)S(1)}, u32[]{:S(2)}, u32[]{:S(2)}) collective-permute-start(f32[128,256]{1,0:T(8,128)S(1)} %get-tuple-element.172.p0.state.n0.refs_3_), channel_id=1, source_target_pairs={{0,68},{4,0},{64,4},{68,64},{1,69},{5,1},{65,5},{69,65},{2,70},{6,... | collective-permute-start | bytes 393224 | tf_op jit(solution)/shard_map/ppermute | solution.py:30
  49.9 2.0 collective-permute-done.14.p3
  51.9 2.7 collective-permute-done.13.p2
  56.6 3.1 %collective-permute-start.15 = (f32[4,128,256]{2,1,0:T(8,128)S(1)}, f32[4,128,256]{2,1,0:T(8,128)S(1)}, u32[]{:S(2)}, u32[]{:S(2)}) collective-permute-start(f32[4,128,256]{2,1,0:T(8,128)S(1)} %shard_map.154), channel_id=1, source_target_pairs={{0,32},{32,0},{1,33},{33,1},{2,34},{34,2},{3,35},{35,3},{4,36},{36... | collective-permute-start | bytes 1572872 | tf_op jit(solution)/shard_map/ppermute | solution.py:30
  62.4 12.6 %collective-permute-done.4.p1 = f32[136,512]{1,0:T(8,128)S(1)} collective-permute-done((f32[136,512]{1,0:T(8,128)S(1)}, f32[136,512]{1,0:T(8,128)S(1)}, u32[]{:S(2)}, u32[]{:S(2)}) %collective-permute-start.4) | collective-permute-done | bytes 278560 | tf_op jit(solution)/shard_map/ppermute | solution.py:30
  79.8 2.9 %collective-permute-start.17 = (f32[128,256]{1,0:T(8,128)S(1)}, f32[128,256]{1,0:T(8,128)S(1)}, u32[]{:S(2)}, u32[]{:S(2)}) collective-permute-start(f32[128,256]{1,0:T(8,128)S(1)} %get-tuple-element.175), channel_id=1, source_target_pairs={{0,16},{8,24},{16,0},{24,8},{1,17},{9,25},{17,1},{25,9},{2,18},{10... | collective-permute-start | bytes 393224 | tf_op jit(solution)/shard_map/ppermute | solution.py:30
  84.0 3.5 %collective-permute-done.17.a2 = f32[128,256]{1,0:T(8,128)S(1)} collective-permute-done((f32[128,256]{1,0:T(8,128)S(1)}, f32[128,256]{1,0:T(8,128)S(1)}, u32[]{:S(2)}, u32[]{:S(2)}) %collective-permute-start.17) | collective-permute-done | bytes 131104 | tf_op jit(solution)/shard_map/ppermute | solution.py:30
  90.2 2.7 collective-permute-start.20
  92.9 3.5 %collective-permute-done.19.p1 = f32[256,256]{1,0:T(8,128)S(1)} collective-permute-done((f32[256,256]{1,0:T(8,128)S(1)}, f32[256,256]{1,0:T(8,128)S(1)}, u32[]{:S(2)}, u32[]{:S(2)}) %collective-permute-start.19) | collective-permute-done | bytes 262176 | tf_op jit(solution)/shard_map/ppermute | solution.py:30
  96.4 6.8 %collective-permute-done.20.p2 = f32[256,256]{1,0:T(8,128)S(1)} collective-permute-done((f32[256,256]{1,0:T(8,128)S(1)}, f32[256,256]{1,0:T(8,128)S(1)}, u32[]{:S(2)}, u32[]{:S(2)}) %collective-permute-start.20) | collective-permute-done | bytes 262176 | tf_op jit(solution)/shard_map/ppermute | solution.py:30
  104.3 2.3 collective-permute-start.22
  109.8 2.0 collective-permute-start.23
  115.7 3.9 %collective-permute-done.24.a2 = f32[128,256]{1,0:T(8,128)S(1)} collective-permute-done((f32[128,256]{1,0:T(8,128)S(1)}, f32[128,256]{1,0:T(8,128)S(1)}, u32[]{:S(2)}, u32[]{:S(2)}) %collective-permute-start.24) | collective-permute-done | bytes 131104 | tf_op jit(solution)/shard_map/ppermute | solution.py:30
  120.5 1.9 collective-permute-start.28
  123.0 2.3 collective-permute-done.28.p3
  125.4 2.4 collective-permute-done.27.p2
  127.8 3.5 %collective-permute-done.26.p1 = f32[128,256]{1,0:T(8,128)S(1)} collective-permute-done((f32[128,256]{1,0:T(8,128)S(1)}, f32[128,256]{1,0:T(8,128)S(1)}, u32[]{:S(2)}, u32[]{:S(2)}) %collective-permute-start.26) | collective-permute-done | bytes 131104 | tf_op jit(solution)/shard_map/ppermute | solution.py:30
  137.9 2.2 collective-permute-start.31
  142.3 3.9 %collective-permute-done.31.a2 = f32[128,256]{1,0:T(8,128)S(1)} collective-permute-done((f32[128,256]{1,0:T(8,128)S(1)}, f32[128,256]{1,0:T(8,128)S(1)}, u32[]{:S(2)}, u32[]{:S(2)}) %collective-permute-start.31) | collective-permute-done | bytes 131104 | tf_op jit(solution)/shard_map/ppermute | solution.py:30
  149.6 2.1 collective-permute-start.34
  153.0 4.5 %collective-permute-done.34.g2 = f32[2,64,256]{2,1,0:T(8,128)S(1)} collective-permute-done((f32[2,64,256]{2,1,0:T(8,128)S(1)}, f32[2,64,256]{2,1,0:T(8,128)S(1)}, u32[]{:S(2)}, u32[]{:S(2)}) %collective-permute-start.34) | collective-permute-done | bytes 131104 | tf_op jit(solution)/shard_map/ppermute | solution.py:30
  167.1 10.5 %collective-permute-done.37.d1.s1 = f32[4,64,256]{2,1,0:T(8,128)S(1)} collective-permute-done((f32[4,64,256]{2,1,0:T(8,128)S(1)}, f32[4,64,256]{2,1,0:T(8,128)S(1)}, u32[]{:S(2)}, u32[]{:S(2)}) %collective-permute-start.37) | collective-permute-done | bytes 262176 | tf_op jit(solution)/shard_map/ppermute | solution.py:30
  179.9 2.2 collective-permute-start.41
  184.0 2.7 collective-permute-done.41.g2
  186.9 1.9 shard_map.173
  188.8 2.7 collective-permute-start.43
  191.5 1.9 collective-permute-done.43.got
  195.3 3.0 %collective-permute-start.45 = (f32[2,64,256]{2,1,0:T(8,128)S(1)}, f32[2,64,256]{2,1,0:T(8,128)S(1)}, u32[]{:S(2)}, u32[]{:S(2)}) collective-permute-start(f32[2,64,256]{2,1,0:T(8,128)S(1)} %get-tuple-element.225), channel_id=1, source_target_pairs={{0,64},{4,68},{64,0},{68,4},{1,65},{5,69},{65,1},{69,5},{2,66},{6,... | collective-permute-start | bytes 393224 | tf_op jit(solution)/shard_map/ppermute | solution.py:30
  200.4 3.9 %collective-permute-done.45.d2 = f32[2,64,256]{2,1,0:T(8,128)S(1)} collective-permute-done((f32[2,64,256]{2,1,0:T(8,128)S(1)}, f32[2,64,256]{2,1,0:T(8,128)S(1)}, u32[]{:S(2)}, u32[]{:S(2)}) %collective-permute-start.45) | collective-permute-done | bytes 131104 | tf_op jit(solution)/shard_map/ppermute | solution.py:30
  206.2 2.7 collective-permute-start.48
  210.4 3.4 %collective-permute-done.48.g2 = f32[2,64,256]{2,1,0:T(8,128)S(1)} collective-permute-done((f32[2,64,256]{2,1,0:T(8,128)S(1)}, f32[2,64,256]{2,1,0:T(8,128)S(1)}, u32[]{:S(2)}, u32[]{:S(2)}) %collective-permute-start.48) | collective-permute-done | bytes 131104 | tf_op jit(solution)/shard_map/ppermute | solution.py:30
  215.9 2.4 collective-permute-start.50
  221.2 3.0 %collective-permute-start.52 = (f32[2,64,256]{2,1,0:T(8,128)S(1)}, f32[2,64,256]{2,1,0:T(8,128)S(1)}, u32[]{:S(2)}, u32[]{:S(2)}) collective-permute-start(f32[2,64,256]{2,1,0:T(8,128)S(1)} %get-tuple-element.237), channel_id=1, source_target_pairs={{0,64},{4,68},{64,0},{68,4},{1,65},{5,69},{65,1},{69,5},{2,66},{6,... | collective-permute-start | bytes 393224 | tf_op jit(solution)/shard_map/ppermute | solution.py:30
  224.2 3.2 %shard_map.182 = (f32[256,256]{1,0:T(8,128)S(1)}, f32[256,256]{1,0:T(8,128)S(1)}, f32[256,256]{1,0:T(8,128)S(1)}, f32[256,256]{1,0:T(8,128)S(1)}, f32[8,256]{1,0:T(8,128)S(1)}) custom-call(s32[4]{0:T(128)S(1)} %pad_add_fusion.place, s32[8]{0:T(128)S(1)} %get-tuple-element.159.ids.refs_0_, s32[8]{0:T(128)S(1)} %get-tuple-element.150.ids.refs_1_, ...), custom_call_target="tpu_custom_call" | custom-call | flops 20000000000 | bytes 2727936 | tf_op jit(solution)/shard_map/pallas_call | solution.py:44
  227.4 2.8 collective-permute-done.52.d2
  231.6 2.8 %shard_map.183 = (f32[16,40,256]{2,1,0:T(8,128)S(1)}, f32[16,40,256]{2,1,0:T(8,128)S(1)}) custom-call(s32[4]{0:T(128)S(1)} %pad_add_fusion.place, f32[128,256]{1,0:T(8,128)S(1)} %get-tuple-element.169.state, f32[128,256]{1,0:T(8,128)S(1)} %get-tuple-element.221.agg, f32[128,256]{1,0:T(8,128)S(1)} %get-tuple-element.244.pre, ...), custom_call_target="tpu_custom_call" | custom-call | flops 1000000 | bytes 3579904 | tf_op jit(solution)/shard_map/pallas_call | solution.py:44
  237.5 17.3 %all_to_all.10 = f32[16,40,256]{2,1,0:T(8,128)S(1)} all-to-all(f32[16,40,256]{2,1,0:T(8,128)S(1)} %add.16), channel_id=1, replica_groups=mesh['zh'=2,'c'=2,'y'=4,'zl'=2,'b'=4] {'zh','zl','y'}, dimensions={0} | all-to-all | bytes 1310720 | tf_op jit(solution)/shard_map/all_to_all | solution.py:510
  254.8 2.6 collective-permute-start.57
  259.1 2.8 collective-permute-done.56
  262.0 13.4 %all_to_all.11 = f32[16,40,256]{2,1,0:T(8,128)S(1)} all-to-all(f32[16,40,256]{2,1,0:T(8,128)S(1)} %broadcast_in_dim.2), channel_id=1, replica_groups=mesh['zh'=2,'c'=2,'y'=4,'zl'=2,'b'=4] {'zh','zl','y'}, dimensions={0} | all-to-all | bytes 1310720 | tf_op jit(solution)/shard_map/all_to_all | solution.py:512
  275.4 3.6 %collective-permute-start.58 = (f32[16,40,256]{2,1,0:T(8,128)S(1)}, f32[16,40,256]{2,1,0:T(8,128)S(1)}, u32[]{:S(2)}, u32[]{:S(2)}) collective-permute-start(f32[16,40,256]{2,1,0:T(8,128)S(1)} %all_to_all.11), channel_id=1, source_target_pairs={{0,32},{32,0},{1,33},{33,1},{2,34},{34,2},{3,35},{35,3},{4,36},{36... | collective-permute-start | bytes 1966088 | tf_op jit(solution)/shard_map/ppermute | solution.py:30
  (143 shorter events, 94.6 us)
Async XLA Ops:
  11.2 8.1 %collective-permute-start.7 = (f32[256,256]{1,0:T(8,128)S(1)}, f32[256,256]{1,0:T(8,128)S(1)}, u32[]{:S(2)}, u32[]{:S(2)}) collective-permute-start(f32[256,256]{1,0:T(8,128)S(1)} %get-tuple-element.164), channel_id=1, source_target_pairs={{0,4},{4,0},{1,5},{5,1},{2,6},{6,2},{3,7},{7,3},{8,12},{12,8},{9,1... | collective-permute-start | bytes 786440 | tf_op jit(solution)/shard_map/ppermute | solution.py:30
  13.1 15.3 %collective-permute-start.2 = (f32[136,512]{1,0:T(8,128)S(1)}, f32[136,512]{1,0:T(8,128)S(1)}, u32[]{:S(2)}, u32[]{:S(2)}) collective-permute-start(f32[136,512]{1,0:T(8,128)S(1)} %get-tuple-element.136), channel_id=1, source_target_pairs={{0,64},{4,68},{64,0},{68,4},{1,65},{5,69},{65,1},{69,5},{2,66},{6,... | collective-permute-start | bytes 835592 | tf_op jit(solution)/shard_map/ppermute | solution.py:30
  16.4 15.0 %collective-permute-start.3 = (f32[136,512]{1,0:T(8,128)S(1)}, f32[136,512]{1,0:T(8,128)S(1)}, u32[]{:S(2)}, u32[]{:S(2)}) collective-permute-start(f32[136,512]{1,0:T(8,128)S(1)} %get-tuple-element.137), channel_id=1, source_target_pairs={{0,68},{4,0},{64,4},{68,64},{1,69},{5,1},{65,5},{69,65},{2,70},{6,... | collective-permute-start | bytes 835592 | tf_op jit(solution)/shard_map/ppermute | solution.py:30
  16.4 15.0 %collective-permute-start.1 = (f32[136,512]{1,0:T(8,128)S(1)}, f32[136,512]{1,0:T(8,128)S(1)}, u32[]{:S(2)}, u32[]{:S(2)}) collective-permute-start(f32[136,512]{1,0:T(8,128)S(1)} %get-tuple-element.135), channel_id=1, source_target_pairs={{0,4},{4,64},{64,68},{68,0},{1,5},{5,65},{65,69},{69,1},{2,6},{6,6... | collective-permute-start | bytes 835592 | tf_op jit(solution)/shard_map/ppermute | solution.py:30
  19.4 13.7 %collective-permute-start.8 = (f32[256,256]{1,0:T(8,128)S(1)}, f32[256,256]{1,0:T(8,128)S(1)}, u32[]{:S(2)}, u32[]{:S(2)}) collective-permute-start(f32[256,256]{1,0:T(8,128)S(1)} %collective-permute-done.7.near), channel_id=1, source_target_pairs={{0,32},{32,0},{1,33},{33,1},{2,34},{34,2},{3,35},{35,3},{4,36},{36... | collective-permute-start | bytes 786440 | tf_op jit(solution)/shard_map/ppermute | solution.py:30
  35.3 5.9 %collective-permute-start.9 = (f32[136,256]{1,0:T(8,128)S(1)}, f32[136,256]{1,0:T(8,128)S(1)}, u32[]{:S(2)}, u32[]{:S(2)}) collective-permute-start(f32[136,256]{1,0:T(8,128)S(1)} %get-tuple-element.166), channel_id=1, source_target_pairs={{0,8},{8,16},{16,24},{24,0},{1,9},{9,17},{17,25},{25,1},{2,10},{10... | collective-permute-start | bytes 417800 | tf_op jit(solution)/shard_map/ppermute | solution.py:30
  36.5 7.7 %collective-permute-start.10 = (f32[136,256]{1,0:T(8,128)S(1)}, f32[136,256]{1,0:T(8,128)S(1)}, u32[]{:S(2)}, u32[]{:S(2)}) collective-permute-start(f32[136,256]{1,0:T(8,128)S(1)} %get-tuple-element.167), channel_id=1, source_target_pairs={{0,16},{8,24},{16,0},{24,8},{1,17},{9,25},{17,1},{25,9},{2,18},{10... | collective-permute-start | bytes 417800 | tf_op jit(solution)/shard_map/ppermute | solution.py:30
  39.2 5.7 %collective-permute-start.11 = (f32[136,256]{1,0:T(8,128)S(1)}, f32[136,256]{1,0:T(8,128)S(1)}, u32[]{:S(2)}, u32[]{:S(2)}) collective-permute-start(f32[136,256]{1,0:T(8,128)S(1)} %get-tuple-element.168), channel_id=1, source_target_pairs={{0,24},{8,0},{16,8},{24,16},{1,25},{9,1},{17,9},{25,17},{2,26},{10... | collective-permute-start | bytes 417800 | tf_op jit(solution)/shard_map/ppermute | solution.py:30
  45.7 6.2 %collective-permute-start.14 = (f32[128,256]{1,0:T(8,128)S(1)}, f32[128,256]{1,0:T(8,128)S(1)}, u32[]{:S(2)}, u32[]{:S(2)}) collective-permute-start(f32[128,256]{1,0:T(8,128)S(1)} %get-tuple-element.172.p0.state.n0.refs_3_), channel_id=1, source_target_pairs={{0,68},{4,0},{64,4},{68,64},{1,69},{5,1},{65,5},{69,65},{2,70},{6,... | collective-permute-start | bytes 393224 | tf_op jit(solution)/shard_map/ppermute | solution.py:30
  49.2 5.4 %collective-permute-start.13 = (f32[128,256]{1,0:T(8,128)S(1)}, f32[128,256]{1,0:T(8,128)S(1)}, u32[]{:S(2)}, u32[]{:S(2)}) collective-permute-start(f32[128,256]{1,0:T(8,128)S(1)} %get-tuple-element.172.p0.state.n0.refs_3_), channel_id=1, source_target_pairs={{0,64},{4,68},{64,0},{68,4},{1,65},{5,69},{65,1},{69,5},{2,66},{6,... | collective-permute-start | bytes 393224 | tf_op jit(solution)/shard_map/ppermute | solution.py:30
  49.2 6.9 %collective-permute-start.12 = (f32[128,256]{1,0:T(8,128)S(1)}, f32[128,256]{1,0:T(8,128)S(1)}, u32[]{:S(2)}, u32[]{:S(2)}) collective-permute-start(f32[128,256]{1,0:T(8,128)S(1)} %get-tuple-element.172.p0.state.n0.refs_3_), channel_id=1, source_target_pairs={{0,4},{4,64},{64,68},{68,0},{1,5},{5,65},{65,69},{69,1},{2,6},{6,6... | collective-permute-start | bytes 393224 | tf_op jit(solution)/shard_map/ppermute | solution.py:30
  56.6 20.5 %collective-permute-start.15 = (f32[4,128,256]{2,1,0:T(8,128)S(1)}, f32[4,128,256]{2,1,0:T(8,128)S(1)}, u32[]{:S(2)}, u32[]{:S(2)}) collective-permute-start(f32[4,128,256]{2,1,0:T(8,128)S(1)} %shard_map.154), channel_id=1, source_target_pairs={{0,32},{32,0},{1,33},{33,1},{2,34},{34,2},{3,35},{35,3},{4,36},{36... | collective-permute-start | bytes 1572872 | tf_op jit(solution)/shard_map/ppermute | solution.py:30
  59.8 15.3 %collective-permute-start.4 = (f32[136,512]{1,0:T(8,128)S(1)}, f32[136,512]{1,0:T(8,128)S(1)}, u32[]{:S(2)}, u32[]{:S(2)}) collective-permute-start(f32[136,512]{1,0:T(8,128)S(1)} %get-tuple-element.153), channel_id=1, source_target_pairs={{0,4},{4,64},{64,68},{68,0},{1,5},{5,65},{65,69},{69,1},{2,6},{6,6... | collective-permute-start | bytes 835592 | tf_op jit(solution)/shard_map/ppermute | solution.py:30
  59.8 15.3 %collective-permute-start.5 = (f32[136,512]{1,0:T(8,128)S(1)}, f32[136,512]{1,0:T(8,128)S(1)}, u32[]{:S(2)}, u32[]{:S(2)}) collective-permute-start(f32[136,512]{1,0:T(8,128)S(1)} %get-tuple-element.154), channel_id=1, source_target_pairs={{0,64},{4,68},{64,0},{68,4},{1,65},{5,69},{65,1},{69,5},{2,66},{6,... | collective-permute-start | bytes 835592 | tf_op jit(solution)/shard_map/ppermute | solution.py:30
  61.6 13.8 %collective-permute-start.6 = (f32[136,512]{1,0:T(8,128)S(1)}, f32[136,512]{1,0:T(8,128)S(1)}, u32[]{:S(2)}, u32[]{:S(2)}) collective-permute-start(f32[136,512]{1,0:T(8,128)S(1)} %get-tuple-element.155), channel_id=1, source_target_pairs={{0,68},{4,0},{64,4},{68,64},{1,69},{5,1},{65,5},{69,65},{2,70},{6,... | collective-permute-start | bytes 835592 | tf_op jit(solution)/shard_map/ppermute | solution.py:30
  78.8 5.3 %collective-permute-start.16 = (f32[128,256]{1,0:T(8,128)S(1)}, f32[128,256]{1,0:T(8,128)S(1)}, u32[]{:S(2)}, u32[]{:S(2)}) collective-permute-start(f32[128,256]{1,0:T(8,128)S(1)} %get-tuple-element.174), channel_id=1, source_target_pairs={{0,8},{8,16},{16,24},{24,0},{1,9},{9,17},{17,25},{25,1},{2,10},{10... | collective-permute-start | bytes 393224 | tf_op jit(solution)/shard_map/ppermute | solution.py:30
  79.8 7.8 %collective-permute-start.17 = (f32[128,256]{1,0:T(8,128)S(1)}, f32[128,256]{1,0:T(8,128)S(1)}, u32[]{:S(2)}, u32[]{:S(2)}) collective-permute-start(f32[128,256]{1,0:T(8,128)S(1)} %get-tuple-element.175), channel_id=1, source_target_pairs={{0,16},{8,24},{16,0},{24,8},{1,17},{9,25},{17,1},{25,9},{2,18},{10... | collective-permute-start | bytes 393224 | tf_op jit(solution)/shard_map/ppermute | solution.py:30
  82.7 5.5 %collective-permute-start.18 = (f32[128,256]{1,0:T(8,128)S(1)}, f32[128,256]{1,0:T(8,128)S(1)}, u32[]{:S(2)}, u32[]{:S(2)}) collective-permute-start(f32[128,256]{1,0:T(8,128)S(1)} %get-tuple-element.176), channel_id=1, source_target_pairs={{0,24},{8,0},{16,8},{24,16},{1,25},{9,1},{17,9},{25,17},{2,26},{10... | collective-permute-start | bytes 393224 | tf_op jit(solution)/shard_map/ppermute | solution.py:30
  89.0 7.4 %collective-permute-start.19 = (f32[256,256]{1,0:T(8,128)S(1)}, f32[256,256]{1,0:T(8,128)S(1)}, u32[]{:S(2)}, u32[]{:S(2)}) collective-permute-start(f32[256,256]{1,0:T(8,128)S(1)} %get-tuple-element.182), channel_id=1, source_target_pairs={{0,4},{4,64},{64,68},{68,0},{1,5},{5,65},{65,69},{69,1},{2,6},{6,6... | collective-permute-start | bytes 786440 | tf_op jit(solution)/shard_map/ppermute | solution.py:30
  90.2 13.1 %collective-permute-start.20 = (f32[256,256]{1,0:T(8,128)S(1)}, f32[256,256]{1,0:T(8,128)S(1)}, u32[]{:S(2)}, u32[]{:S(2)}) collective-permute-start(f32[256,256]{1,0:T(8,128)S(1)} %get-tuple-element.183), channel_id=1, source_target_pairs={{0,64},{4,68},{64,0},{68,4},{1,65},{5,69},{65,1},{69,5},{2,66},{6,... | collective-permute-start | bytes 786440 | tf_op jit(solution)/shard_map/ppermute | solution.py:30
  92.9 10.8 %collective-permute-start.21 = (f32[256,256]{1,0:T(8,128)S(1)}, f32[256,256]{1,0:T(8,128)S(1)}, u32[]{:S(2)}, u32[]{:S(2)}) collective-permute-start(f32[256,256]{1,0:T(8,128)S(1)} %get-tuple-element.184), channel_id=1, source_target_pairs={{0,68},{4,0},{64,4},{68,64},{1,69},{5,1},{65,5},{69,65},{2,70},{6,... | collective-permute-start | bytes 786440 | tf_op jit(solution)/shard_map/ppermute | solution.py:30
  109.8 6.0 %collective-permute-start.23 = (f32[128,256]{1,0:T(8,128)S(1)}, f32[128,256]{1,0:T(8,128)S(1)}, u32[]{:S(2)}, u32[]{:S(2)}) collective-permute-start(f32[128,256]{1,0:T(8,128)S(1)} %get-tuple-element.188), channel_id=1, source_target_pairs={{0,8},{8,16},{16,24},{24,0},{1,9},{9,17},{17,25},{25,1},{2,10},{10... | collective-permute-start | bytes 393224 | tf_op jit(solution)/shard_map/ppermute | solution.py:30
  111.8 7.8 %collective-permute-start.24 = (f32[128,256]{1,0:T(8,128)S(1)}, f32[128,256]{1,0:T(8,128)S(1)}, u32[]{:S(2)}, u32[]{:S(2)}) collective-permute-start(f32[128,256]{1,0:T(8,128)S(1)} %get-tuple-element.189), channel_id=1, source_target_pairs={{0,16},{8,24},{16,0},{24,8},{1,17},{9,25},{17,1},{25,9},{2,18},{10... | collective-permute-start | bytes 393224 | tf_op jit(solution)/shard_map/ppermute | solution.py:30
  113.6 6.0 %collective-permute-start.25 = (f32[128,256]{1,0:T(8,128)S(1)}, f32[128,256]{1,0:T(8,128)S(1)}, u32[]{:S(2)}, u32[]{:S(2)}) collective-permute-start(f32[128,256]{1,0:T(8,128)S(1)} %get-tuple-element.190), channel_id=1, source_target_pairs={{0,24},{8,0},{16,8},{24,16},{1,25},{9,1},{17,9},{25,17},{2,26},{10... | collective-permute-start | bytes 393224 | tf_op jit(solution)/shard_map/ppermute | solution.py:30
  120.5 4.9 %collective-permute-start.28 = (f32[128,256]{1,0:T(8,128)S(1)}, f32[128,256]{1,0:T(8,128)S(1)}, u32[]{:S(2)}, u32[]{:S(2)}) collective-permute-start(f32[128,256]{1,0:T(8,128)S(1)} %get-tuple-element.193.state.p0.n2.refs_5_), channel_id=1, source_target_pairs={{0,68},{4,0},{64,4},{68,64},{1,69},{5,1},{65,5},{69,65},{2,70},{6,... | collective-permute-start | bytes 393224 | tf_op jit(solution)/shard_map/ppermute | solution.py:30
  122.4 5.4 %collective-permute-start.27 = (f32[128,256]{1,0:T(8,128)S(1)}, f32[128,256]{1,0:T(8,128)S(1)}, u32[]{:S(2)}, u32[]{:S(2)}) collective-permute-start(f32[128,256]{1,0:T(8,128)S(1)} %get-tuple-element.193.state.p0.n2.refs_5_), channel_id=1, source_target_pairs={{0,64},{4,68},{64,0},{68,4},{1,65},{5,69},{65,1},{69,5},{2,66},{6,... | collective-permute-start | bytes 393224 | tf_op jit(solution)/shard_map/ppermute | solution.py:30
  122.5 8.8 %collective-permute-start.26 = (f32[128,256]{1,0:T(8,128)S(1)}, f32[128,256]{1,0:T(8,128)S(1)}, u32[]{:S(2)}, u32[]{:S(2)}) collective-permute-start(f32[128,256]{1,0:T(8,128)S(1)} %get-tuple-element.193.state.p0.n2.refs_5_), channel_id=1, source_target_pairs={{0,4},{4,64},{64,68},{68,0},{1,5},{5,65},{65,69},{69,1},{2,6},{6,6... | collective-permute-start | bytes 393224 | tf_op jit(solution)/shard_map/ppermute | solution.py:30
  136.3 6.0 %collective-permute-start.30 = (f32[128,256]{1,0:T(8,128)S(1)}, f32[128,256]{1,0:T(8,128)S(1)}, u32[]{:S(2)}, u32[]{:S(2)}) collective-permute-start(f32[128,256]{1,0:T(8,128)S(1)} %get-tuple-element.196), channel_id=1, source_target_pairs={{0,8},{8,16},{16,24},{24,0},{1,9},{9,17},{17,25},{25,1},{2,10},{10... | collective-permute-start | bytes 393224 | tf_op jit(solution)/shard_map/ppermute | solution.py:30
  137.9 8.2 %collective-permute-start.31 = (f32[128,256]{1,0:T(8,128)S(1)}, f32[128,256]{1,0:T(8,128)S(1)}, u32[]{:S(2)}, u32[]{:S(2)}) collective-permute-start(f32[128,256]{1,0:T(8,128)S(1)} %get-tuple-element.197), channel_id=1, source_target_pairs={{0,16},{8,24},{16,0},{24,8},{1,17},{9,25},{17,1},{25,9},{2,18},{10... | collective-permute-start | bytes 393224 | tf_op jit(solution)/shard_map/ppermute | solution.py:30
  140.1 6.0 %collective-permute-start.32 = (f32[128,256]{1,0:T(8,128)S(1)}, f32[128,256]{1,0:T(8,128)S(1)}, u32[]{:S(2)}, u32[]{:S(2)}) collective-permute-start(f32[128,256]{1,0:T(8,128)S(1)} %get-tuple-element.198), channel_id=1, source_target_pairs={{0,24},{8,0},{16,8},{24,16},{1,25},{9,1},{17,9},{25,17},{2,26},{10... | collective-permute-start | bytes 393224 | tf_op jit(solution)/shard_map/ppermute | solution.py:30
  147.9 5.1 %collective-permute-start.35 = (f32[2,64,256]{2,1,0:T(8,128)S(1)}, f32[2,64,256]{2,1,0:T(8,128)S(1)}, u32[]{:S(2)}, u32[]{:S(2)}) collective-permute-start(f32[2,64,256]{2,1,0:T(8,128)S(1)} %get-tuple-element.201.g0), channel_id=1, source_target_pairs={{0,8},{8,16},{16,24},{24,0},{1,9},{9,17},{17,25},{25,1},{2,10},{10... | collective-permute-start | bytes 393224 | tf_op jit(solution)/shard_map/ppermute | solution.py:30
  149.6 7.9 %collective-permute-start.34 = (f32[2,64,256]{2,1,0:T(8,128)S(1)}, f32[2,64,256]{2,1,0:T(8,128)S(1)}, u32[]{:S(2)}, u32[]{:S(2)}) collective-permute-start(f32[2,64,256]{2,1,0:T(8,128)S(1)} %get-tuple-element.201.g0), channel_id=1, source_target_pairs={{0,16},{8,24},{16,0},{24,8},{1,17},{9,25},{17,1},{25,9},{2,18},{10... | collective-permute-start | bytes 393224 | tf_op jit(solution)/shard_map/ppermute | solution.py:30
  151.7 5.8 %collective-permute-start.33 = (f32[2,64,256]{2,1,0:T(8,128)S(1)}, f32[2,64,256]{2,1,0:T(8,128)S(1)}, u32[]{:S(2)}, u32[]{:S(2)}) collective-permute-start(f32[2,64,256]{2,1,0:T(8,128)S(1)} %get-tuple-element.201.g0), channel_id=1, source_target_pairs={{0,24},{8,0},{16,8},{24,16},{1,25},{9,1},{17,9},{25,17},{2,26},{10... | collective-permute-start | bytes 393224 | tf_op jit(solution)/shard_map/ppermute | solution.py:30
  163.2 14.4 %collective-permute-start.37 = (f32[4,64,256]{2,1,0:T(8,128)S(1)}, f32[4,64,256]{2,1,0:T(8,128)S(1)}, u32[]{:S(2)}, u32[]{:S(2)}) collective-permute-start(f32[4,64,256]{2,1,0:T(8,128)S(1)} %get-tuple-element.210), channel_id=1, source_target_pairs={{0,4},{4,64},{64,68},{68,0},{1,5},{5,65},{65,69},{69,1},{2,6},{6,6... | collective-permute-start | bytes 786440 | tf_op jit(solution)/shard_map/ppermute | solution.py:30
  163.3 14.3 %collective-permute-start.38 = (f32[4,64,256]{2,1,0:T(8,128)S(1)}, f32[4,64,256]{2,1,0:T(8,128)S(1)}, u32[]{:S(2)}, u32[]{:S(2)}) collective-permute-start(f32[4,64,256]{2,1,0:T(8,128)S(1)} %get-tuple-element.211), channel_id=1, source_target_pairs={{0,64},{4,68},{64,0},{68,4},{1,65},{5,69},{65,1},{69,5},{2,66},{6,... | collective-permute-start | bytes 786440 | tf_op jit(solution)/shard_map/ppermute | solution.py:30
  164.8 13.2 %collective-permute-start.39 = (f32[4,64,256]{2,1,0:T(8,128)S(1)}, f32[4,64,256]{2,1,0:T(8,128)S(1)}, u32[]{:S(2)}, u32[]{:S(2)}) collective-permute-start(f32[4,64,256]{2,1,0:T(8,128)S(1)} %get-tuple-element.212), channel_id=1, source_target_pairs={{0,68},{4,0},{64,4},{68,64},{1,69},{5,1},{65,5},{69,65},{2,70},{6,... | collective-permute-start | bytes 786440 | tf_op jit(solution)/shard_map/ppermute | solution.py:30
  178.9 5.1 %collective-permute-start.42 = (f32[2,64,256]{2,1,0:T(8,128)S(1)}, f32[2,64,256]{2,1,0:T(8,128)S(1)}, u32[]{:S(2)}, u32[]{:S(2)}) collective-permute-start(f32[2,64,256]{2,1,0:T(8,128)S(1)} %get-tuple-element.218.g0), channel_id=1, source_target_pairs={{0,8},{8,16},{16,24},{24,0},{1,9},{9,17},{17,25},{25,1},{2,10},{10... | collective-permute-start | bytes 393224 | tf_op jit(solution)/shard_map/ppermute | solution.py:30
  179.9 6.8 %collective-permute-start.41 = (f32[2,64,256]{2,1,0:T(8,128)S(1)}, f32[2,64,256]{2,1,0:T(8,128)S(1)}, u32[]{:S(2)}, u32[]{:S(2)}) collective-permute-start(f32[2,64,256]{2,1,0:T(8,128)S(1)} %get-tuple-element.218.g0), channel_id=1, source_target_pairs={{0,16},{8,24},{16,0},{24,8},{1,17},{9,25},{17,1},{25,9},{2,18},{10... | collective-permute-start | bytes 393224 | tf_op jit(solution)/shard_map/ppermute | solution.py:30
  194.1 6.3 %collective-permute-start.44 = (f32[2,64,256]{2,1,0:T(8,128)S(1)}, f32[2,64,256]{2,1,0:T(8,128)S(1)}, u32[]{:S(2)}, u32[]{:S(2)}) collective-permute-start(f32[2,64,256]{2,1,0:T(8,128)S(1)} %get-tuple-element.224), channel_id=1, source_target_pairs={{0,4},{4,64},{64,68},{68,0},{1,5},{5,65},{65,69},{69,1},{2,6},{6,6... | collective-permute-start | bytes 393224 | tf_op jit(solution)/shard_map/ppermute | solution.py:30
  195.3 9.0 %collective-permute-start.45 = (f32[2,64,256]{2,1,0:T(8,128)S(1)}, f32[2,64,256]{2,1,0:T(8,128)S(1)}, u32[]{:S(2)}, u32[]{:S(2)}) collective-permute-start(f32[2,64,256]{2,1,0:T(8,128)S(1)} %get-tuple-element.225), channel_id=1, source_target_pairs={{0,64},{4,68},{64,0},{68,4},{1,65},{5,69},{65,1},{69,5},{2,66},{6,... | collective-permute-start | bytes 393224 | tf_op jit(solution)/shard_map/ppermute | solution.py:30
  198.3 6.0 %collective-permute-start.46 = (f32[2,64,256]{2,1,0:T(8,128)S(1)}, f32[2,64,256]{2,1,0:T(8,128)S(1)}, u32[]{:S(2)}, u32[]{:S(2)}) collective-permute-start(f32[2,64,256]{2,1,0:T(8,128)S(1)} %get-tuple-element.226), channel_id=1, source_target_pairs={{0,68},{4,0},{64,4},{68,64},{1,69},{5,1},{65,5},{69,65},{2,70},{6,... | collective-permute-start | bytes 393224 | tf_op jit(solution)/shard_map/ppermute | solution.py:30
  205.3 5.1 %collective-permute-start.49 = (f32[2,64,256]{2,1,0:T(8,128)S(1)}, f32[2,64,256]{2,1,0:T(8,128)S(1)}, u32[]{:S(2)}, u32[]{:S(2)}) collective-permute-start(f32[2,64,256]{2,1,0:T(8,128)S(1)} %get-tuple-element.232.g0), channel_id=1, source_target_pairs={{0,8},{8,16},{16,24},{24,0},{1,9},{9,17},{17,25},{25,1},{2,10},{10... | collective-permute-start | bytes 393224 | tf_op jit(solution)/shard_map/ppermute | solution.py:30
  206.2 7.6 %collective-permute-start.48 = (f32[2,64,256]{2,1,0:T(8,128)S(1)}, f32[2,64,256]{2,1,0:T(8,128)S(1)}, u32[]{:S(2)}, u32[]{:S(2)}) collective-permute-start(f32[2,64,256]{2,1,0:T(8,128)S(1)} %get-tuple-element.232.g0), channel_id=1, source_target_pairs={{0,16},{8,24},{16,0},{24,8},{1,17},{9,25},{17,1},{25,9},{2,18},{10... | collective-permute-start | bytes 393224 | tf_op jit(solution)/shard_map/ppermute | solution.py:30
  208.9 5.0 %collective-permute-start.47 = (f32[2,64,256]{2,1,0:T(8,128)S(1)}, f32[2,64,256]{2,1,0:T(8,128)S(1)}, u32[]{:S(2)}, u32[]{:S(2)}) collective-permute-start(f32[2,64,256]{2,1,0:T(8,128)S(1)} %get-tuple-element.232.g0), channel_id=1, source_target_pairs={{0,24},{8,0},{16,8},{24,16},{1,25},{9,1},{17,9},{25,17},{2,26},{10... | collective-permute-start | bytes 393224 | tf_op jit(solution)/shard_map/ppermute | solution.py:30
  220.4 7.1 %collective-permute-start.51 = (f32[2,64,256]{2,1,0:T(8,128)S(1)}, f32[2,64,256]{2,1,0:T(8,128)S(1)}, u32[]{:S(2)}, u32[]{:S(2)}) collective-permute-start(f32[2,64,256]{2,1,0:T(8,128)S(1)} %get-tuple-element.236), channel_id=1, source_target_pairs={{0,4},{4,64},{64,68},{68,0},{1,5},{5,65},{65,69},{69,1},{2,6},{6,6... | collective-permute-start | bytes 393224 | tf_op jit(solution)/shard_map/ppermute | solution.py:30
  221.2 9.0 %collective-permute-start.52 = (f32[2,64,256]{2,1,0:T(8,128)S(1)}, f32[2,64,256]{2,1,0:T(8,128)S(1)}, u32[]{:S(2)}, u32[]{:S(2)}) collective-permute-start(f32[2,64,256]{2,1,0:T(8,128)S(1)} %get-tuple-element.237), channel_id=1, source_target_pairs={{0,64},{4,68},{64,0},{68,4},{1,65},{5,69},{65,1},{69,5},{2,66},{6,... | collective-permute-start | bytes 393224 | tf_op jit(solution)/shard_map/ppermute | solution.py:30
  224.2 6.0 %collective-permute-start.53 = (f32[2,64,256]{2,1,0:T(8,128)S(1)}, f32[2,64,256]{2,1,0:T(8,128)S(1)}, u32[]{:S(2)}, u32[]{:S(2)}) collective-permute-start(f32[2,64,256]{2,1,0:T(8,128)S(1)} %get-tuple-element.238), channel_id=1, source_target_pairs={{0,68},{4,0},{64,4},{68,64},{1,69},{5,1},{65,5},{69,65},{2,70},{6,... | collective-permute-start | bytes 393224 | tf_op jit(solution)/shard_map/ppermute | solution.py:30
  275.4 5.6 %collective-permute-start.58 = (f32[16,40,256]{2,1,0:T(8,128)S(1)}, f32[16,40,256]{2,1,0:T(8,128)S(1)}, u32[]{:S(2)}, u32[]{:S(2)}) collective-permute-start(f32[16,40,256]{2,1,0:T(8,128)S(1)} %all_to_all.11), channel_id=1, source_target_pairs={{0,32},{32,0},{1,33},{33,1},{2,34},{34,2},{3,35},{35,3},{4,36},{36... | collective-permute-start | bytes 1966088 | tf_op jit(solution)/shard_map/ppermute | solution.py:30
  (23 other events, 120.5 us)
where the time goes:
time: 282 us
  waiting for transfers between devices  112 us (40%)
  starting transfers between devices  85.4 us (30%)
  Pallas kernels  45.9 us (16%)
  blocking collectives  30.7 us (11%)
  local copies, waits for them, and re-layouts  6.63 us (2%)
    ppermute x59, waiting for transfers between devices, along(): lax.ppermute(value, axis, [(i, (i + steps) % count) for i in range(count)])  112 us
    ppermute x59, starting transfers between devices, along(): lax.ppermute(value, axis, [(i, (i + steps) % count) for i in range(count)])  85.4 us
    pallas_call x39, Pallas kernels, local(): pl.pallas_call(kernel, out_shape=[jax.ShapeDtypeStruct((o,), jnp.int32) i...  45.9 us
    all_to_all x1, blocking collectives, on_device(): lax.all_to_all(keep + swap(give), plane, 0, 0, tiled=True)  17.3 us
    all_to_all x1, blocking collectives, on_device(): lax.all_to_all(jnp.broadcast_to(summed[None], size), plane, 0, 0, tiled=T...  13.4 us
  transfers between devices with their start and end apart: 59, of which 43 were waited for; matrix products, arithmetic and copies ran while one was open for 0% of the time, Pallas kernels for 6%

commit v1 on v0

--- a/solution.py
+++ b/solution.py
@@ -17,12 +17,19 @@
 TM = ("zh", "c")
 ENT = ("y", "zl")
 Z = ("zh", "zl")
-highest = lax.Precision.HIGHEST
 F32 = jnp.float32
+BF16 = jnp.bfloat16
+
+
+def halves(value):
+    high = value.astype(BF16)
+    return high, (value - high.astype(F32)).astype(BF16)
 
 
 def product(left, right, dims=((1,), (0,))):
-    return lax.dot_general(left, right, (dims, ((), ())), precision=highest, preferred_element_type=F32)
+    (a, b), (c, d) = halves(left), halves(right)
+    dot = lambda p, q: lax.dot_general(p, q, (dims, ((), ())), preferred_element_type=F32)
+    return dot(a, c) + (dot(a, d) + dot(b, c))
 
 
 def along(value, axis, steps):
@@ -112,17 +119,18 @@
 def join_tiles(place, p0, p1, p2, p3, early, late, early_ids, late_ids):
     z, y = place[0], place[3]
     rows = early.shape[1]
-    for s, piece in enumerate((p0, p1, p2, p3)):
+    pieces = (p0, p1, p2, p3)
+    codes = [
+        [jnp.max(piece[rows : rows + 8, q * 128 : (q + 1) * 128]).astype(jnp.int32) for q in range(4)] for piece in pieces
+    ]
+    for s, piece in enumerate(pieces):
         from_z = behind(z, s)
         b = lax.rem(from_z, 2)
 
         def write(tiles, ids):
             tiles[b] = piece[0:rows, :]
             for j in range(2):
-                dst, rel = (
-                    jnp.max(piece[rows : rows + 8, (2 * j + i) * 128 : (2 * j + i + 1) * 128]).astype(jnp.int32)
-                    for i in range(2)
-                )
+                dst, rel = codes[s][2 * j], codes[s][2 * j + 1]
                 ids[2 * b + j] = lax.rem(lax.div(dst, 2) + 4 - y, 4) * 2 + lax.rem(dst, 2)
                 ids[4 + 2 * b + j] = rel
 
@@ -208,14 +216,6 @@
     new[...] = gate * cand + (1.0 - gate) * state[...]
 
 
-def advance_with(place, a0, a1, a2, a3, state, update, self_part, w_neigh, c1, c2, c3, new, agg, candidate, n1, n2, n3):
-    advance(place, a0, a1, a2, a3, state, update, self_part, w_neigh, new, agg, candidate)
-    rows = new.shape[0]
-    for piece, out in ((c1, n1), (c2, n2), (c3, n3)):
-        out[0:rows, :] = new[...]
-        out[rows:, :] = piece[...].reshape(rows, -1)
-
-
 def retreat_math(d_new, state, update, candidate, w_neigh, d_pre, d_gate, d_agg, d_keep):
     gate, cand = update[...], candidate[...]
     rest = 1.0 - gate
@@ -273,19 +273,13 @@
     c = place[1]
     gather_back(place, ids, tiles, g0, g1, g2, g3, other, mine, rel_rows, held, res, full)
     for s, piece in enumerate((s0, s1, s2, s3)):
-        states[s] = piece[2 + c]
-        other[4 + s // 2, s % 2] = piece[2 + 1 - c]
+        states[s] = piece[c]
+        other[4 + s // 2, s % 2] = piece[1 - c]
 
 
 def add_pairs(place, mine, got, n0, n1, n2, n3):
     for s, out in enumerate((n0, n1, n2, n3)):
         out[...] = mine[s] + got[s]
-
-
-def add_pairs_with(place, mine, got, s0, s1, s2, s3, n0, n1, n2, n3):
-    for s, (piece, out) in enumerate(((s0, n0), (s1, n1), (s2, n2), (s3, n3))):
-        out[0:2] = mine[s] + got[s]
-        out[2:4] = piece[...]
 
 
 def cut_rows(place, own, got, *outs):
@@ -301,11 +295,8 @@
 def join_rows(place, p0, p1, p2, p3, *refs):
     outs, stack = refs[:4], refs[4]
     z = place[0]
-    rows = outs[0].shape[1]
-    stack[z] = p0[...]
-    for s, piece in enumerate((p1, p2, p3)):
-        for core in range(2):
-            stack[behind(z, s + 1), core] = piece[(2 + core) * rows : (3 + core) * rows, :]
+    for s, piece in enumerate((p0, p1, p2, p3)):
+        stack[behind(z, s)] = piece[...]
     for t in range(4):
         for b in range(2):
             outs[t][b] = stack[(t // 2) * 2 + b, t % 2]
@@ -417,7 +408,7 @@
     join(0, ring)
     work = [(2, tile, width), (8, rows, width)]
     stored, states = [], []
-    state = lines = carried = None
+    state = lines = None
     for t in range(snaps):
         if t == 0:
             *to_y, state = local(
@@ -428,10 +419,7 @@
                 work,
             )
         else:
-            ring = [state] + [along(carried[s - 1] if carried else state, Z, s) for s in range(1, 4)]
-            if carried:
-                cots = local(join_rows, (here,), [cut_cot[0]] + ring[1:], [pair] * 4, [(4, 2, rows, width)])
-                carried = None
+            ring = [state] + [along(state, Z, s) for s in range(1, 4)]
             (packed,) = local(pack_ring, (here,), ring, [(4, *flat)])
             to_y = local(spread_next, (here, ids[t]), [held[t], rel_emb] + ring + [swap(packed)], [flat] * 4, work)
         came_y = [to_y[0]] + [along(to_y[s], "y", s) for s in range(1, 4)]
@@ -442,16 +430,15 @@
         update, self_part = local(gates, (here,), (state, w_self, w_gate, bias_row), [flat] * 2)
         terms = came_y + [state, update, self_part, w_neigh]
         if t == 1:
-            new, agg, candidate, *carried = local(
-                advance_with, (here,), terms + list(cut_cot[1:]), [flat] * 3 + [(4 * rows, width)] * 3
-            )
-        else:
-            new, agg, candidate = local(advance, (here,), terms, [flat] * 3)
+            ring = [cut_cot[0]] + [along(cut_cot[s], Z, s) for s in range(1, 4)]
+            cots = local(join_rows, (here,), ring, [pair] * 4, [(4, 2, rows, width)])
+        new, agg, candidate = local(advance, (here,), terms, [flat] * 3)
         stored.append((state, agg, update, candidate))
         states.append(new)
         state = new
 
     cut = local(cut_states, (here,), states, [pair] * 4, [(4, 2, rows, width)])
+    cut = [cut[0]] + [along(cut[s], Z, s) for s in range(1, 4)]
 
     d_prev = d_in = None
     pres, gates_in, rel_lines = [None] * snaps, [None] * snaps, []
@@ -472,7 +459,7 @@
         other, mine_rows, rel_rows, *mine_states = local(
             gather_back_with if second else gather_back,
             (here, ids[t]),
-            [held[t]] + pieces + (list(d_in) if second else []),
+            [held[t]] + pieces + (cut if second else []),
             [(6 if second else 4, *pair), (4, *pair), (4, 8, width)] + [(4, rows, width)] * second,
             [(8, rows, width), flat, (tile, width)],
         )
@@ -494,10 +481,7 @@
                 [(4, snaps - 1, *flat)],
                 flops=20_000_000_000,
             )
-        if t == snaps - 1:
-            parts = local(add_pairs_with, (here,), [mine_rows, got] + list(cut), [(4, rows, width)] * 4)
-        else:
-            parts = local(add_pairs, (here,), (mine_rows, got), [pair] * 4)
+        parts = local(add_pairs, (here,), (mine_rows, got), [pair] * 4)
         d_in = [parts[0]] + [along(parts[s], Z, s) for s in range(1, 4)]
 
     parts = 16

time: 282 us -> 269 us (0.954)
  waiting for transfers between devices: 112 us -> 99.3 us
  Pallas kernels: 45.9 us -> 38.9 us
  starting transfers between devices: 85.4 us -> 92.2 us
    ppermute x59 -> x65, waiting for transfers between devices: 112 us -> 99.3 us  [along(): lax.ppermute(value, axis, [(i, (i + steps) % count) for i in range(count)])]
    pallas_call x39, Pallas kernels: 45.9 us -> 38.9 us  [local(): pl.pallas_call(kernel, out_shape=[jax.ShapeDtypeStruct((o,), jnp.int32) i...]
    ppermute x59 -> x65, starting transfers between devices: 85.4 us -> 92.2 us  [along(): lax.ppermute(value, axis, [(i, (i + steps) % count) for i in range(count)])]
  transfers between devices with their start and end apart: 59 -> 65, of which waited for: 43 -> 43; matrix products, arithmetic and copies ran while one was open for 0% -> 0% of each run, Pallas kernels for 6% -> 6%
where the time goes in v1:
time: 269 us
  waiting for transfers between devices  99.3 us (37%)
  starting transfers between devices  92.2 us (34%)
  Pallas kernels  38.9 us (14%)
  blocking collectives  30.8 us (11%)
  local copies, waits for them, and re-layouts  6.63 us (2%)
    ppermute x65, waiting for transfers between devices, along(): lax.ppermute(value, axis, [(i, (i + steps) % count) for i in range(count)])  99.3 us
    ppermute x65, starting transfers between devices, along(): lax.ppermute(value, axis, [(i, (i + steps) % count) for i in range(count)])  92.2 us
    pallas_call x39, Pallas kernels, local(): pl.pallas_call(kernel, out_shape=[jax.ShapeDtypeStruct((o,), jnp.int32) i...  38.9 us
    all_to_all x1, blocking collectives, on_device(): lax.all_to_all(keep + swap(give), plane, 0, 0, tiled=True)  17.3 us
    all_to_all x1, blocking collectives, on_device(): lax.all_to_all(jnp.broadcast_to(summed[None], size), plane, 0, 0, tiled=T...  13.4 us
  transfers between devices with their start and end apart: 65, of which 43 were waited for; matrix products, arithmetic and copies ran while one was open for 0% of the time, Pallas kernels for 6%

profile of v1, /device:TPU:1, one launch (start us, length us, event | category | flops | bytes accessed | tf_op | source)
XLA Modules:
  0.0 269.2 jit_solution(16123300342156939082)
XLA Ops:
  7.8 2.8 %collective-permute-done.got = f32[4,168,512]{2,1,0:T(8,128)S(1)} collective-permute-done((f32[4,168,512]{2,1,0:T(8,128)S(1)}, f32[4,168,512]{2,1,0:T(8,128)S(1)}, u32[]{:S(2)}, u32[]{:S(2)}) %collective-permute-start) | collective-permute-done | bytes 1376288 | tf_op jit(solution)/shard_map/ppermute | solution.py:37
  13.1 3.3 %collective-permute-start.2 = (f32[136,512]{1,0:T(8,128)S(1)}, f32[136,512]{1,0:T(8,128)S(1)}, u32[]{:S(2)}, u32[]{:S(2)}) collective-permute-start(f32[136,512]{1,0:T(8,128)S(1)} %get-tuple-element.133), channel_id=1, source_target_pairs={{0,64},{4,68},{64,0},{68,4},{1,65},{5,69},{65,1},{69,5},{2,66},{6,... | collective-permute-start | bytes 835592 | tf_op jit(solution)/shard_map/ppermute | solution.py:37
  22.2 6.3 %collective-permute-done.2.p2 = f32[136,512]{1,0:T(8,128)S(1)} collective-permute-done((f32[136,512]{1,0:T(8,128)S(1)}, f32[136,512]{1,0:T(8,128)S(1)}, u32[]{:S(2)}, u32[]{:S(2)}) %collective-permute-start.2) | collective-permute-done | bytes 278560 | tf_op jit(solution)/shard_map/ppermute | solution.py:37
  28.4 2.9 %collective-permute-done.3.p3 = f32[136,512]{1,0:T(8,128)S(1)} collective-permute-done((f32[136,512]{1,0:T(8,128)S(1)}, f32[136,512]{1,0:T(8,128)S(1)}, u32[]{:S(2)}, u32[]{:S(2)}) %collective-permute-start.3) | collective-permute-done | bytes 278560 | tf_op jit(solution)/shard_map/ppermute | solution.py:37
  35.7 2.6 collective-permute-start.13
  40.2 3.2 %collective-permute-done.13.a2.l2 = f32[136,256]{1,0:T(8,128)S(1)} collective-permute-done((f32[136,256]{1,0:T(8,128)S(1)}, f32[136,256]{1,0:T(8,128)S(1)}, u32[]{:S(2)}, u32[]{:S(2)}) %collective-permute-start.13) | collective-permute-done | bytes 139296 | tf_op jit(solution)/shard_map/ppermute | solution.py:37
  44.8 3.5 %collective-permute-start.17 = (f32[128,256]{1,0:T(8,128)S(1)}, f32[128,256]{1,0:T(8,128)S(1)}, u32[]{:S(2)}, u32[]{:S(2)}) collective-permute-start(f32[128,256]{1,0:T(8,128)S(1)} %get-tuple-element.173.p0.state.n0.refs_3_), channel_id=1, source_target_pairs={{0,68},{4,0},{64,4},{68,64},{1,69},{5,1},{65,5},{69,65},{2,70},{6,... | collective-permute-start | bytes 393224 | tf_op jit(solution)/shard_map/ppermute | solution.py:37
  49.0 2.0 collective-permute-done.17.p3
  51.0 2.7 collective-permute-done.16.p2
  55.7 3.1 %collective-permute-start.18 = (f32[4,128,256]{2,1,0:T(8,128)S(1)}, f32[4,128,256]{2,1,0:T(8,128)S(1)}, u32[]{:S(2)}, u32[]{:S(2)}) collective-permute-start(f32[4,128,256]{2,1,0:T(8,128)S(1)} %shard_map.155), channel_id=1, source_target_pairs={{0,32},{32,0},{1,33},{33,1},{2,34},{34,2},{3,35},{35,3},{4,36},{36... | collective-permute-start | bytes 1572872 | tf_op jit(solution)/shard_map/ppermute | solution.py:37
  61.5 12.6 %collective-permute-done.4.p1 = f32[136,512]{1,0:T(8,128)S(1)} collective-permute-done((f32[136,512]{1,0:T(8,128)S(1)}, f32[136,512]{1,0:T(8,128)S(1)}, u32[]{:S(2)}, u32[]{:S(2)}) %collective-permute-start.4) | collective-permute-done | bytes 278560 | tf_op jit(solution)/shard_map/ppermute | solution.py:37
  78.2 2.9 %collective-permute-start.20 = (f32[128,256]{1,0:T(8,128)S(1)}, f32[128,256]{1,0:T(8,128)S(1)}, u32[]{:S(2)}, u32[]{:S(2)}) collective-permute-start(f32[128,256]{1,0:T(8,128)S(1)} %get-tuple-element.176), channel_id=1, source_target_pairs={{0,16},{8,24},{16,0},{24,8},{1,17},{9,25},{17,1},{25,9},{2,18},{10... | collective-permute-start | bytes 393224 | tf_op jit(solution)/shard_map/ppermute | solution.py:37
  82.3 3.6 %collective-permute-done.20.a2 = f32[128,256]{1,0:T(8,128)S(1)} collective-permute-done((f32[128,256]{1,0:T(8,128)S(1)}, f32[128,256]{1,0:T(8,128)S(1)}, u32[]{:S(2)}, u32[]{:S(2)}) %collective-permute-start.20) | collective-permute-done | bytes 131104 | tf_op jit(solution)/shard_map/ppermute | solution.py:37
  87.4 2.7 collective-permute-start.24
  90.7 2.9 %collective-permute-done.24.p3 = f32[128,256]{1,0:T(8,128)S(1)} collective-permute-done((f32[128,256]{1,0:T(8,128)S(1)}, f32[128,256]{1,0:T(8,128)S(1)}, u32[]{:S(2)}, u32[]{:S(2)}) %collective-permute-start.24) | collective-permute-done | bytes 131104 | tf_op jit(solution)/shard_map/ppermute | solution.py:37
  93.6 1.9 collective-permute-done.23.p2
  95.5 3.4 %collective-permute-done.22.p1 = f32[128,256]{1,0:T(8,128)S(1)} collective-permute-done((f32[128,256]{1,0:T(8,128)S(1)}, f32[128,256]{1,0:T(8,128)S(1)}, u32[]{:S(2)}, u32[]{:S(2)}) %collective-permute-start.22) | collective-permute-done | bytes 131104 | tf_op jit(solution)/shard_map/ppermute | solution.py:37
  103.7 1.8 collective-permute-start.26
  105.6 1.9 collective-permute-start.27
  109.7 3.8 %collective-permute-done.27.a2 = f32[128,256]{1,0:T(8,128)S(1)} collective-permute-done((f32[128,256]{1,0:T(8,128)S(1)}, f32[128,256]{1,0:T(8,128)S(1)}, u32[]{:S(2)}, u32[]{:S(2)}) %collective-permute-start.27) | collective-permute-done | bytes 131104 | tf_op jit(solution)/shard_map/ppermute | solution.py:37
  115.8 2.3 collective-permute-done.31.p3
  118.1 2.0 collective-permute-done.30.p2
  120.2 3.6 %collective-permute-done.29.p1 = f32[128,256]{1,0:T(8,128)S(1)} collective-permute-done((f32[128,256]{1,0:T(8,128)S(1)}, f32[128,256]{1,0:T(8,128)S(1)}, u32[]{:S(2)}, u32[]{:S(2)}) %collective-permute-start.29) | collective-permute-done | bytes 131104 | tf_op jit(solution)/shard_map/ppermute | solution.py:37
  131.1 2.2 collective-permute-start.34
  134.6 2.4 collective-permute-start.35
  141.9 3.4 %collective-permute-start.37 = (f32[2,64,256]{2,1,0:T(8,128)S(1)}, f32[2,64,256]{2,1,0:T(8,128)S(1)}, u32[]{:S(2)}, u32[]{:S(2)}) collective-permute-start(f32[2,64,256]{2,1,0:T(8,128)S(1)} %get-tuple-element.195.g0), channel_id=1, source_target_pairs={{0,16},{8,24},{16,0},{24,8},{1,17},{9,25},{17,1},{25,9},{2,18},{10... | collective-permute-start | bytes 393224 | tf_op jit(solution)/shard_map/ppermute | solution.py:37
  146.4 3.1 %collective-permute-done.37.g2 = f32[2,64,256]{2,1,0:T(8,128)S(1)} collective-permute-done((f32[2,64,256]{2,1,0:T(8,128)S(1)}, f32[2,64,256]{2,1,0:T(8,128)S(1)}, u32[]{:S(2)}, u32[]{:S(2)}) %collective-permute-start.37) | collective-permute-done | bytes 131104 | tf_op jit(solution)/shard_map/ppermute | solution.py:37
  151.7 2.5 collective-permute-start.39
  157.7 2.0 collective-permute-start.42
  163.1 1.9 collective-permute-done.40.d1
  166.8 2.9 %collective-permute-start.44 = (f32[2,64,256]{2,1,0:T(8,128)S(1)}, f32[2,64,256]{2,1,0:T(8,128)S(1)}, u32[]{:S(2)}, u32[]{:S(2)}) collective-permute-start(f32[2,64,256]{2,1,0:T(8,128)S(1)} %get-tuple-element.207.g0), channel_id=1, source_target_pairs={{0,16},{8,24},{16,0},{24,8},{1,17},{9,25},{17,1},{25,9},{2,18},{10... | collective-permute-start | bytes 393224 | tf_op jit(solution)/shard_map/ppermute | solution.py:37
  173.6 2.6 collective-permute-done.43.g1
  177.7 1.9 collective-permute-start.49
  179.5 1.9 collective-permute-done.49.got
  183.6 3.0 %collective-permute-start.51 = (f32[2,64,256]{2,1,0:T(8,128)S(1)}, f32[2,64,256]{2,1,0:T(8,128)S(1)}, u32[]{:S(2)}, u32[]{:S(2)}) collective-permute-start(f32[2,64,256]{2,1,0:T(8,128)S(1)} %get-tuple-element.219), channel_id=1, source_target_pairs={{0,64},{4,68},{64,0},{68,4},{1,65},{5,69},{65,1},{69,5},{2,66},{6,... | collective-permute-start | bytes 393224 | tf_op jit(solution)/shard_map/ppermute | solution.py:37
  188.9 3.7 %collective-permute-done.51.d2 = f32[2,64,256]{2,1,0:T(8,128)S(1)} collective-permute-done((f32[2,64,256]{2,1,0:T(8,128)S(1)}, f32[2,64,256]{2,1,0:T(8,128)S(1)}, u32[]{:S(2)}, u32[]{:S(2)}) %collective-permute-start.51) | collective-permute-done | bytes 131104 | tf_op jit(solution)/shard_map/ppermute | solution.py:37
  193.9 3.1 %collective-permute-start.54 = (f32[2,64,256]{2,1,0:T(8,128)S(1)}, f32[2,64,256]{2,1,0:T(8,128)S(1)}, u32[]{:S(2)}, u32[]{:S(2)}) collective-permute-start(f32[2,64,256]{2,1,0:T(8,128)S(1)} %get-tuple-element.226.g0), channel_id=1, source_target_pairs={{0,16},{8,24},{16,0},{24,8},{1,17},{9,25},{17,1},{25,9},{2,18},{10... | collective-permute-start | bytes 393224 | tf_op jit(solution)/shard_map/ppermute | solution.py:37
  198.6 3.3 %collective-permute-done.54.g2 = f32[2,64,256]{2,1,0:T(8,128)S(1)} collective-permute-done((f32[2,64,256]{2,1,0:T(8,128)S(1)}, f32[2,64,256]{2,1,0:T(8,128)S(1)}, u32[]{:S(2)}, u32[]{:S(2)}) %collective-permute-start.54) | collective-permute-done | bytes 131104 | tf_op jit(solution)/shard_map/ppermute | solution.py:37
  203.4 2.5 collective-permute-start.56
  208.6 3.3 %collective-permute-start.58 = (f32[2,64,256]{2,1,0:T(8,128)S(1)}, f32[2,64,256]{2,1,0:T(8,128)S(1)}, u32[]{:S(2)}, u32[]{:S(2)}) collective-permute-start(f32[2,64,256]{2,1,0:T(8,128)S(1)} %get-tuple-element.231), channel_id=1, source_target_pairs={{0,64},{4,68},{64,0},{68,4},{1,65},{5,69},{65,1},{69,5},{2,66},{6,... | collective-permute-start | bytes 393224 | tf_op jit(solution)/shard_map/ppermute | solution.py:37
  211.9 2.3 shard_map.182
  214.2 3.7 %collective-permute-done.58.d2 = f32[2,64,256]{2,1,0:T(8,128)S(1)} collective-permute-done((f32[2,64,256]{2,1,0:T(8,128)S(1)}, f32[2,64,256]{2,1,0:T(8,128)S(1)}, u32[]{:S(2)}, u32[]{:S(2)}) %collective-permute-start.58) | collective-permute-done | bytes 131104 | tf_op jit(solution)/shard_map/ppermute | solution.py:37
  219.2 2.2 shard_map.183
  224.6 17.3 %all_to_all.10 = f32[16,40,256]{2,1,0:T(8,128)S(1)} all-to-all(f32[16,40,256]{2,1,0:T(8,128)S(1)} %add.16), channel_id=1, replica_groups=mesh['zh'=2,'c'=2,'y'=4,'zl'=2,'b'=4] {'zh','zl','y'}, dimensions={0} | all-to-all | bytes 1310720 | tf_op jit(solution)/shard_map/all_to_all | solution.py:494
  241.9 2.5 collective-permute-start.63
  246.2 2.8 %collective-permute-done.62 = f32[40,256]{1,0:T(8,128)S(1)} collective-permute-done((f32[40,256]{1,0:T(8,128)S(1)}, f32[40,256]{1,0:T(8,128)S(1)}, u32[]{:S(2)}, u32[]{:S(2)}) %collective-permute-start.62) | collective-permute-done | bytes 40992 | tf_op jit(solution)/shard_map/ppermute | solution.py:37
  249.1 13.4 %all_to_all.11 = f32[16,40,256]{2,1,0:T(8,128)S(1)} all-to-all(f32[16,40,256]{2,1,0:T(8,128)S(1)} %broadcast_in_dim.2), channel_id=1, replica_groups=mesh['zh'=2,'c'=2,'y'=4,'zl'=2,'b'=4] {'zh','zl','y'}, dimensions={0} | all-to-all | bytes 1310720 | tf_op jit(solution)/shard_map/all_to_all | solution.py:496
  262.5 3.6 %collective-permute-start.64 = (f32[16,40,256]{2,1,0:T(8,128)S(1)}, f32[16,40,256]{2,1,0:T(8,128)S(1)}, u32[]{:S(2)}, u32[]{:S(2)}) collective-permute-start(f32[16,40,256]{2,1,0:T(8,128)S(1)} %all_to_all.11), channel_id=1, source_target_pairs={{0,32},{32,0},{1,33},{33,1},{2,34},{34,2},{3,35},{35,3},{4,36},{36... | collective-permute-start | bytes 1966088 | tf_op jit(solution)/shard_map/ppermute | solution.py:37
  (155 shorter events, 96.7 us)
Async XLA Ops:
  11.2 8.1 %collective-permute-start.10 = (f32[256,256]{1,0:T(8,128)S(1)}, f32[256,256]{1,0:T(8,128)S(1)}, u32[]{:S(2)}, u32[]{:S(2)}) collective-permute-start(f32[256,256]{1,0:T(8,128)S(1)} %get-tuple-element.165), channel_id=1, source_target_pairs={{0,4},{4,0},{1,5},{5,1},{2,6},{6,2},{3,7},{7,3},{8,12},{12,8},{9,1... | collective-permute-start | bytes 786440 | tf_op jit(solution)/shard_map/ppermute | solution.py:37
  13.1 15.3 %collective-permute-start.2 = (f32[136,512]{1,0:T(8,128)S(1)}, f32[136,512]{1,0:T(8,128)S(1)}, u32[]{:S(2)}, u32[]{:S(2)}) collective-permute-start(f32[136,512]{1,0:T(8,128)S(1)} %get-tuple-element.133), channel_id=1, source_target_pairs={{0,64},{4,68},{64,0},{68,4},{1,65},{5,69},{65,1},{69,5},{2,66},{6,... | collective-permute-start | bytes 835592 | tf_op jit(solution)/shard_map/ppermute | solution.py:37
  16.4 15.0 %collective-permute-start.3 = (f32[136,512]{1,0:T(8,128)S(1)}, f32[136,512]{1,0:T(8,128)S(1)}, u32[]{:S(2)}, u32[]{:S(2)}) collective-permute-start(f32[136,512]{1,0:T(8,128)S(1)} %get-tuple-element.134), channel_id=1, source_target_pairs={{0,68},{4,0},{64,4},{68,64},{1,69},{5,1},{65,5},{69,65},{2,70},{6,... | collective-permute-start | bytes 835592 | tf_op jit(solution)/shard_map/ppermute | solution.py:37
  16.4 15.0 %collective-permute-start.1 = (f32[136,512]{1,0:T(8,128)S(1)}, f32[136,512]{1,0:T(8,128)S(1)}, u32[]{:S(2)}, u32[]{:S(2)}) collective-permute-start(f32[136,512]{1,0:T(8,128)S(1)} %get-tuple-element.132), channel_id=1, source_target_pairs={{0,4},{4,64},{64,68},{68,0},{1,5},{5,65},{65,69},{69,1},{2,6},{6,6... | collective-permute-start | bytes 835592 | tf_op jit(solution)/shard_map/ppermute | solution.py:37
  19.4 13.4 %collective-permute-start.11 = (f32[256,256]{1,0:T(8,128)S(1)}, f32[256,256]{1,0:T(8,128)S(1)}, u32[]{:S(2)}, u32[]{:S(2)}) collective-permute-start(f32[256,256]{1,0:T(8,128)S(1)} %collective-permute-done.10.near), channel_id=1, source_target_pairs={{0,32},{32,0},{1,33},{33,1},{2,34},{34,2},{3,35},{35,3},{4,36},{36... | collective-permute-start | bytes 786440 | tf_op jit(solution)/shard_map/ppermute | solution.py:37
  34.5 5.8 %collective-permute-start.12 = (f32[136,256]{1,0:T(8,128)S(1)}, f32[136,256]{1,0:T(8,128)S(1)}, u32[]{:S(2)}, u32[]{:S(2)}) collective-permute-start(f32[136,256]{1,0:T(8,128)S(1)} %get-tuple-element.167), channel_id=1, source_target_pairs={{0,8},{8,16},{16,24},{24,0},{1,9},{9,17},{17,25},{25,1},{2,10},{10... | collective-permute-start | bytes 417800 | tf_op jit(solution)/shard_map/ppermute | solution.py:37
  35.7 7.7 %collective-permute-start.13 = (f32[136,256]{1,0:T(8,128)S(1)}, f32[136,256]{1,0:T(8,128)S(1)}, u32[]{:S(2)}, u32[]{:S(2)}) collective-permute-start(f32[136,256]{1,0:T(8,128)S(1)} %get-tuple-element.168), channel_id=1, source_target_pairs={{0,16},{8,24},{16,0},{24,8},{1,17},{9,25},{17,1},{25,9},{2,18},{10... | collective-permute-start | bytes 417800 | tf_op jit(solution)/shard_map/ppermute | solution.py:37
  38.3 5.7 %collective-permute-start.14 = (f32[136,256]{1,0:T(8,128)S(1)}, f32[136,256]{1,0:T(8,128)S(1)}, u32[]{:S(2)}, u32[]{:S(2)}) collective-permute-start(f32[136,256]{1,0:T(8,128)S(1)} %get-tuple-element.169), channel_id=1, source_target_pairs={{0,24},{8,0},{16,8},{24,16},{1,25},{9,1},{17,9},{25,17},{2,26},{10... | collective-permute-start | bytes 417800 | tf_op jit(solution)/shard_map/ppermute | solution.py:37
  44.8 6.2 %collective-permute-start.17 = (f32[128,256]{1,0:T(8,128)S(1)}, f32[128,256]{1,0:T(8,128)S(1)}, u32[]{:S(2)}, u32[]{:S(2)}) collective-permute-start(f32[128,256]{1,0:T(8,128)S(1)} %get-tuple-element.173.p0.state.n0.refs_3_), channel_id=1, source_target_pairs={{0,68},{4,0},{64,4},{68,64},{1,69},{5,1},{65,5},{69,65},{2,70},{6,... | collective-permute-start | bytes 393224 | tf_op jit(solution)/shard_map/ppermute | solution.py:37
  48.2 5.4 %collective-permute-start.16 = (f32[128,256]{1,0:T(8,128)S(1)}, f32[128,256]{1,0:T(8,128)S(1)}, u32[]{:S(2)}, u32[]{:S(2)}) collective-permute-start(f32[128,256]{1,0:T(8,128)S(1)} %get-tuple-element.173.p0.state.n0.refs_3_), channel_id=1, source_target_pairs={{0,64},{4,68},{64,0},{68,4},{1,65},{5,69},{65,1},{69,5},{2,66},{6,... | collective-permute-start | bytes 393224 | tf_op jit(solution)/shard_map/ppermute | solution.py:37
  48.2 6.9 %collective-permute-start.15 = (f32[128,256]{1,0:T(8,128)S(1)}, f32[128,256]{1,0:T(8,128)S(1)}, u32[]{:S(2)}, u32[]{:S(2)}) collective-permute-start(f32[128,256]{1,0:T(8,128)S(1)} %get-tuple-element.173.p0.state.n0.refs_3_), channel_id=1, source_target_pairs={{0,4},{4,64},{64,68},{68,0},{1,5},{5,65},{65,69},{69,1},{2,6},{6,6... | collective-permute-start | bytes 393224 | tf_op jit(solution)/shard_map/ppermute | solution.py:37
  55.7 20.2 %collective-permute-start.18 = (f32[4,128,256]{2,1,0:T(8,128)S(1)}, f32[4,128,256]{2,1,0:T(8,128)S(1)}, u32[]{:S(2)}, u32[]{:S(2)}) collective-permute-start(f32[4,128,256]{2,1,0:T(8,128)S(1)} %shard_map.155), channel_id=1, source_target_pairs={{0,32},{32,0},{1,33},{33,1},{2,34},{34,2},{3,35},{35,3},{4,36},{36... | collective-permute-start | bytes 1572872 | tf_op jit(solution)/shard_map/ppermute | solution.py:37
  58.8 15.3 %collective-permute-start.4 = (f32[136,512]{1,0:T(8,128)S(1)}, f32[136,512]{1,0:T(8,128)S(1)}, u32[]{:S(2)}, u32[]{:S(2)}) collective-permute-start(f32[136,512]{1,0:T(8,128)S(1)} %get-tuple-element.150), channel_id=1, source_target_pairs={{0,4},{4,64},{64,68},{68,0},{1,5},{5,65},{65,69},{69,1},{2,6},{6,6... | collective-permute-start | bytes 835592 | tf_op jit(solution)/shard_map/ppermute | solution.py:37
  58.8 15.3 %collective-permute-start.5 = (f32[136,512]{1,0:T(8,128)S(1)}, f32[136,512]{1,0:T(8,128)S(1)}, u32[]{:S(2)}, u32[]{:S(2)}) collective-permute-start(f32[136,512]{1,0:T(8,128)S(1)} %get-tuple-element.151), channel_id=1, source_target_pairs={{0,64},{4,68},{64,0},{68,4},{1,65},{5,69},{65,1},{69,5},{2,66},{6,... | collective-permute-start | bytes 835592 | tf_op jit(solution)/shard_map/ppermute | solution.py:37
  60.7 13.8 %collective-permute-start.6 = (f32[136,512]{1,0:T(8,128)S(1)}, f32[136,512]{1,0:T(8,128)S(1)}, u32[]{:S(2)}, u32[]{:S(2)}) collective-permute-start(f32[136,512]{1,0:T(8,128)S(1)} %get-tuple-element.152), channel_id=1, source_target_pairs={{0,68},{4,0},{64,4},{68,64},{1,69},{5,1},{65,5},{69,65},{2,70},{6,... | collective-permute-start | bytes 835592 | tf_op jit(solution)/shard_map/ppermute | solution.py:37
  78.2 7.8 %collective-permute-start.20 = (f32[128,256]{1,0:T(8,128)S(1)}, f32[128,256]{1,0:T(8,128)S(1)}, u32[]{:S(2)}, u32[]{:S(2)}) collective-permute-start(f32[128,256]{1,0:T(8,128)S(1)} %get-tuple-element.176), channel_id=1, source_target_pairs={{0,16},{8,24},{16,0},{24,8},{1,17},{9,25},{17,1},{25,9},{2,18},{10... | collective-permute-start | bytes 393224 | tf_op jit(solution)/shard_map/ppermute | solution.py:37
  81.1 5.5 %collective-permute-start.21 = (f32[128,256]{1,0:T(8,128)S(1)}, f32[128,256]{1,0:T(8,128)S(1)}, u32[]{:S(2)}, u32[]{:S(2)}) collective-permute-start(f32[128,256]{1,0:T(8,128)S(1)} %get-tuple-element.177), channel_id=1, source_target_pairs={{0,24},{8,0},{16,8},{24,16},{1,25},{9,1},{17,9},{25,17},{2,26},{10... | collective-permute-start | bytes 393224 | tf_op jit(solution)/shard_map/ppermute | solution.py:37
  87.4 6.2 %collective-permute-start.24 = (f32[128,256]{1,0:T(8,128)S(1)}, f32[128,256]{1,0:T(8,128)S(1)}, u32[]{:S(2)}, u32[]{:S(2)}) collective-permute-start(f32[128,256]{1,0:T(8,128)S(1)} %get-tuple-element.180.p0.state.n1.refs_4_), channel_id=1, source_target_pairs={{0,68},{4,0},{64,4},{68,64},{1,69},{5,1},{65,5},{69,65},{2,70},{6,... | collective-permute-start | bytes 393224 | tf_op jit(solution)/shard_map/ppermute | solution.py:37
  90.1 5.4 %collective-permute-start.23 = (f32[128,256]{1,0:T(8,128)S(1)}, f32[128,256]{1,0:T(8,128)S(1)}, u32[]{:S(2)}, u32[]{:S(2)}) collective-permute-start(f32[128,256]{1,0:T(8,128)S(1)} %get-tuple-element.180.p0.state.n1.refs_4_), channel_id=1, source_target_pairs={{0,64},{4,68},{64,0},{68,4},{1,65},{5,69},{65,1},{69,5},{2,66},{6,... | collective-permute-start | bytes 393224 | tf_op jit(solution)/shard_map/ppermute | solution.py:37
  90.3 8.6 %collective-permute-start.22 = (f32[128,256]{1,0:T(8,128)S(1)}, f32[128,256]{1,0:T(8,128)S(1)}, u32[]{:S(2)}, u32[]{:S(2)}) collective-permute-start(f32[128,256]{1,0:T(8,128)S(1)} %get-tuple-element.180.p0.state.n1.refs_4_), channel_id=1, source_target_pairs={{0,4},{4,64},{64,68},{68,0},{1,5},{5,65},{65,69},{69,1},{2,6},{6,6... | collective-permute-start | bytes 393224 | tf_op jit(solution)/shard_map/ppermute | solution.py:37
  103.7 6.0 %collective-permute-start.26 = (f32[128,256]{1,0:T(8,128)S(1)}, f32[128,256]{1,0:T(8,128)S(1)}, u32[]{:S(2)}, u32[]{:S(2)}) collective-permute-start(f32[128,256]{1,0:T(8,128)S(1)} %get-tuple-element.182), channel_id=1, source_target_pairs={{0,8},{8,16},{16,24},{24,0},{1,9},{9,17},{17,25},{25,1},{2,10},{10... | collective-permute-start | bytes 393224 | tf_op jit(solution)/shard_map/ppermute | solution.py:37
  105.6 7.9 %collective-permute-start.27 = (f32[128,256]{1,0:T(8,128)S(1)}, f32[128,256]{1,0:T(8,128)S(1)}, u32[]{:S(2)}, u32[]{:S(2)}) collective-permute-start(f32[128,256]{1,0:T(8,128)S(1)} %get-tuple-element.183), channel_id=1, source_target_pairs={{0,16},{8,24},{16,0},{24,8},{1,17},{9,25},{17,1},{25,9},{2,18},{10... | collective-permute-start | bytes 393224 | tf_op jit(solution)/shard_map/ppermute | solution.py:37
  107.4 6.0 %collective-permute-start.28 = (f32[128,256]{1,0:T(8,128)S(1)}, f32[128,256]{1,0:T(8,128)S(1)}, u32[]{:S(2)}, u32[]{:S(2)}) collective-permute-start(f32[128,256]{1,0:T(8,128)S(1)} %get-tuple-element.184), channel_id=1, source_target_pairs={{0,24},{8,0},{16,8},{24,16},{1,25},{9,1},{17,9},{25,17},{2,26},{10... | collective-permute-start | bytes 393224 | tf_op jit(solution)/shard_map/ppermute | solution.py:37
  114.9 8.9 %collective-permute-start.29 = (f32[128,256]{1,0:T(8,128)S(1)}, f32[128,256]{1,0:T(8,128)S(1)}, u32[]{:S(2)}, u32[]{:S(2)}) collective-permute-start(f32[128,256]{1,0:T(8,128)S(1)} %get-tuple-element.187.state.p0.n2.refs_5_), channel_id=1, source_target_pairs={{0,4},{4,64},{64,68},{68,0},{1,5},{5,65},{65,69},{69,1},{2,6},{6,6... | collective-permute-start | bytes 393224 | tf_op jit(solution)/shard_map/ppermute | solution.py:37
  125.6 9.0 %collective-permute-start.7 = (f32[2,64,256]{2,1,0:T(8,128)S(1)}, f32[2,64,256]{2,1,0:T(8,128)S(1)}, u32[]{:S(2)}, u32[]{:S(2)}) collective-permute-start(f32[2,64,256]{2,1,0:T(8,128)S(1)} %get-tuple-element.156), channel_id=1, source_target_pairs={{0,4},{4,64},{64,68},{68,0},{1,5},{5,65},{65,69},{69,1},{2,6},{6,6... | collective-permute-start | bytes 393224 | tf_op jit(solution)/shard_map/ppermute | solution.py:37
  125.7 11.4 %collective-permute-start.8 = (f32[2,64,256]{2,1,0:T(8,128)S(1)}, f32[2,64,256]{2,1,0:T(8,128)S(1)}, u32[]{:S(2)}, u32[]{:S(2)}) collective-permute-start(f32[2,64,256]{2,1,0:T(8,128)S(1)} %get-tuple-element.157), channel_id=1, source_target_pairs={{0,64},{4,68},{64,0},{68,4},{1,65},{5,69},{65,1},{69,5},{2,66},{6,... | collective-permute-start | bytes 393224 | tf_op jit(solution)/shard_map/ppermute | solution.py:37
  127.3 9.7 %collective-permute-start.9 = (f32[2,64,256]{2,1,0:T(8,128)S(1)}, f32[2,64,256]{2,1,0:T(8,128)S(1)}, u32[]{:S(2)}, u32[]{:S(2)}) collective-permute-start(f32[2,64,256]{2,1,0:T(8,128)S(1)} %get-tuple-element.158), channel_id=1, source_target_pairs={{0,68},{4,0},{64,4},{68,64},{1,69},{5,1},{65,5},{69,65},{2,70},{6,... | collective-permute-start | bytes 393224 | tf_op jit(solution)/shard_map/ppermute | solution.py:37
  129.6 9.0 %collective-permute-start.33 = (f32[128,256]{1,0:T(8,128)S(1)}, f32[128,256]{1,0:T(8,128)S(1)}, u32[]{:S(2)}, u32[]{:S(2)}) collective-permute-start(f32[128,256]{1,0:T(8,128)S(1)} %get-tuple-element.190), channel_id=1, source_target_pairs={{0,8},{8,16},{16,24},{24,0},{1,9},{9,17},{17,25},{25,1},{2,10},{10... | collective-permute-start | bytes 393224 | tf_op jit(solution)/shard_map/ppermute | solution.py:37
  131.1 7.9 %collective-permute-start.34 = (f32[128,256]{1,0:T(8,128)S(1)}, f32[128,256]{1,0:T(8,128)S(1)}, u32[]{:S(2)}, u32[]{:S(2)}) collective-permute-start(f32[128,256]{1,0:T(8,128)S(1)} %get-tuple-element.191), channel_id=1, source_target_pairs={{0,16},{8,24},{16,0},{24,8},{1,17},{9,25},{17,1},{25,9},{2,18},{10... | collective-permute-start | bytes 393224 | tf_op jit(solution)/shard_map/ppermute | solution.py:37
  140.6 5.8 %collective-permute-start.38 = (f32[2,64,256]{2,1,0:T(8,128)S(1)}, f32[2,64,256]{2,1,0:T(8,128)S(1)}, u32[]{:S(2)}, u32[]{:S(2)}) collective-permute-start(f32[2,64,256]{2,1,0:T(8,128)S(1)} %get-tuple-element.195.g0), channel_id=1, source_target_pairs={{0,8},{8,16},{16,24},{24,0},{1,9},{9,17},{17,25},{25,1},{2,10},{10... | collective-permute-start | bytes 393224 | tf_op jit(solution)/shard_map/ppermute | solution.py:37
  141.9 7.7 %collective-permute-start.37 = (f32[2,64,256]{2,1,0:T(8,128)S(1)}, f32[2,64,256]{2,1,0:T(8,128)S(1)}, u32[]{:S(2)}, u32[]{:S(2)}) collective-permute-start(f32[2,64,256]{2,1,0:T(8,128)S(1)} %get-tuple-element.195.g0), channel_id=1, source_target_pairs={{0,16},{8,24},{16,0},{24,8},{1,17},{9,25},{17,1},{25,9},{2,18},{10... | collective-permute-start | bytes 393224 | tf_op jit(solution)/shard_map/ppermute | solution.py:37
  156.3 8.7 %collective-permute-start.40 = (f32[2,64,256]{2,1,0:T(8,128)S(1)}, f32[2,64,256]{2,1,0:T(8,128)S(1)}, u32[]{:S(2)}, u32[]{:S(2)}) collective-permute-start(f32[2,64,256]{2,1,0:T(8,128)S(1)} %get-tuple-element.199), channel_id=1, source_target_pairs={{0,4},{4,64},{64,68},{68,0},{1,5},{5,65},{65,69},{69,1},{2,6},{6,6... | collective-permute-start | bytes 393224 | tf_op jit(solution)/shard_map/ppermute | solution.py:37
  156.4 8.8 %collective-permute-start.41 = (f32[2,64,256]{2,1,0:T(8,128)S(1)}, f32[2,64,256]{2,1,0:T(8,128)S(1)}, u32[]{:S(2)}, u32[]{:S(2)}) collective-permute-start(f32[2,64,256]{2,1,0:T(8,128)S(1)} %get-tuple-element.200), channel_id=1, source_target_pairs={{0,64},{4,68},{64,0},{68,4},{1,65},{5,69},{65,1},{69,5},{2,66},{6,... | collective-permute-start | bytes 393224 | tf_op jit(solution)/shard_map/ppermute | solution.py:37
  157.7 8.1 %collective-permute-start.42 = (f32[2,64,256]{2,1,0:T(8,128)S(1)}, f32[2,64,256]{2,1,0:T(8,128)S(1)}, u32[]{:S(2)}, u32[]{:S(2)}) collective-permute-start(f32[2,64,256]{2,1,0:T(8,128)S(1)} %get-tuple-element.201), channel_id=1, source_target_pairs={{0,68},{4,0},{64,4},{68,64},{1,69},{5,1},{65,5},{69,65},{2,70},{6,... | collective-permute-start | bytes 393224 | tf_op jit(solution)/shard_map/ppermute | solution.py:37
  160.3 10.3 %collective-permute-start.46 = (f32[2,64,256]{2,1,0:T(8,128)S(1)}, f32[2,64,256]{2,1,0:T(8,128)S(1)}, u32[]{:S(2)}, u32[]{:S(2)}) collective-permute-start(f32[2,64,256]{2,1,0:T(8,128)S(1)} %get-tuple-element.210), channel_id=1, source_target_pairs={{0,4},{4,64},{64,68},{68,0},{1,5},{5,65},{65,69},{69,1},{2,6},{6,6... | collective-permute-start | bytes 393224 | tf_op jit(solution)/shard_map/ppermute | solution.py:37
  160.4 12.1 %collective-permute-start.47 = (f32[2,64,256]{2,1,0:T(8,128)S(1)}, f32[2,64,256]{2,1,0:T(8,128)S(1)}, u32[]{:S(2)}, u32[]{:S(2)}) collective-permute-start(f32[2,64,256]{2,1,0:T(8,128)S(1)} %get-tuple-element.211), channel_id=1, source_target_pairs={{0,64},{4,68},{64,0},{68,4},{1,65},{5,69},{65,1},{69,5},{2,66},{6,... | collective-permute-start | bytes 393224 | tf_op jit(solution)/shard_map/ppermute | solution.py:37
  165.0 7.5 %collective-permute-start.48 = (f32[2,64,256]{2,1,0:T(8,128)S(1)}, f32[2,64,256]{2,1,0:T(8,128)S(1)}, u32[]{:S(2)}, u32[]{:S(2)}) collective-permute-start(f32[2,64,256]{2,1,0:T(8,128)S(1)} %get-tuple-element.212), channel_id=1, source_target_pairs={{0,68},{4,0},{64,4},{68,64},{1,69},{5,1},{65,5},{69,65},{2,70},{6,... | collective-permute-start | bytes 393224 | tf_op jit(solution)/shard_map/ppermute | solution.py:37
  166.7 5.8 %collective-permute-start.45 = (f32[2,64,256]{2,1,0:T(8,128)S(1)}, f32[2,64,256]{2,1,0:T(8,128)S(1)}, u32[]{:S(2)}, u32[]{:S(2)}) collective-permute-start(f32[2,64,256]{2,1,0:T(8,128)S(1)} %get-tuple-element.207.g0), channel_id=1, source_target_pairs={{0,8},{8,16},{16,24},{24,0},{1,9},{9,17},{17,25},{25,1},{2,10},{10... | collective-permute-start | bytes 393224 | tf_op jit(solution)/shard_map/ppermute | solution.py:37
  166.8 6.8 %collective-permute-start.44 = (f32[2,64,256]{2,1,0:T(8,128)S(1)}, f32[2,64,256]{2,1,0:T(8,128)S(1)}, u32[]{:S(2)}, u32[]{:S(2)}) collective-permute-start(f32[2,64,256]{2,1,0:T(8,128)S(1)} %get-tuple-element.207.g0), channel_id=1, source_target_pairs={{0,16},{8,24},{16,0},{24,8},{1,17},{9,25},{17,1},{25,9},{2,18},{10... | collective-permute-start | bytes 393224 | tf_op jit(solution)/shard_map/ppermute | solution.py:37
  170.7 5.5 %collective-permute-start.43 = (f32[2,64,256]{2,1,0:T(8,128)S(1)}, f32[2,64,256]{2,1,0:T(8,128)S(1)}, u32[]{:S(2)}, u32[]{:S(2)}) collective-permute-start(f32[2,64,256]{2,1,0:T(8,128)S(1)} %get-tuple-element.207.g0), channel_id=1, source_target_pairs={{0,24},{8,0},{16,8},{24,16},{1,25},{9,1},{17,9},{25,17},{2,26},{10... | collective-permute-start | bytes 393224 | tf_op jit(solution)/shard_map/ppermute | solution.py:37
  182.1 6.8 %collective-permute-start.50 = (f32[2,64,256]{2,1,0:T(8,128)S(1)}, f32[2,64,256]{2,1,0:T(8,128)S(1)}, u32[]{:S(2)}, u32[]{:S(2)}) collective-permute-start(f32[2,64,256]{2,1,0:T(8,128)S(1)} %get-tuple-element.218), channel_id=1, source_target_pairs={{0,4},{4,64},{64,68},{68,0},{1,5},{5,65},{65,69},{69,1},{2,6},{6,6... | collective-permute-start | bytes 393224 | tf_op jit(solution)/shard_map/ppermute | solution.py:37
  183.6 9.0 %collective-permute-start.51 = (f32[2,64,256]{2,1,0:T(8,128)S(1)}, f32[2,64,256]{2,1,0:T(8,128)S(1)}, u32[]{:S(2)}, u32[]{:S(2)}) collective-permute-start(f32[2,64,256]{2,1,0:T(8,128)S(1)} %get-tuple-element.219), channel_id=1, source_target_pairs={{0,64},{4,68},{64,0},{68,4},{1,65},{5,69},{65,1},{69,5},{2,66},{6,... | collective-permute-start | bytes 393224 | tf_op jit(solution)/shard_map/ppermute | solution.py:37
  186.6 6.0 %collective-permute-start.52 = (f32[2,64,256]{2,1,0:T(8,128)S(1)}, f32[2,64,256]{2,1,0:T(8,128)S(1)}, u32[]{:S(2)}, u32[]{:S(2)}) collective-permute-start(f32[2,64,256]{2,1,0:T(8,128)S(1)} %get-tuple-element.220), channel_id=1, source_target_pairs={{0,68},{4,0},{64,4},{68,64},{1,69},{5,1},{65,5},{69,65},{2,70},{6,... | collective-permute-start | bytes 393224 | tf_op jit(solution)/shard_map/ppermute | solution.py:37
  193.9 8.0 %collective-permute-start.54 = (f32[2,64,256]{2,1,0:T(8,128)S(1)}, f32[2,64,256]{2,1,0:T(8,128)S(1)}, u32[]{:S(2)}, u32[]{:S(2)}) collective-permute-start(f32[2,64,256]{2,1,0:T(8,128)S(1)} %get-tuple-element.226.g0), channel_id=1, source_target_pairs={{0,16},{8,24},{16,0},{24,8},{1,17},{9,25},{17,1},{25,9},{2,18},{10... | collective-permute-start | bytes 393224 | tf_op jit(solution)/shard_map/ppermute | solution.py:37
  208.0 6.1 %collective-permute-start.57 = (f32[2,64,256]{2,1,0:T(8,128)S(1)}, f32[2,64,256]{2,1,0:T(8,128)S(1)}, u32[]{:S(2)}, u32[]{:S(2)}) collective-permute-start(f32[2,64,256]{2,1,0:T(8,128)S(1)} %get-tuple-element.230), channel_id=1, source_target_pairs={{0,4},{4,64},{64,68},{68,0},{1,5},{5,65},{65,69},{69,1},{2,6},{6,6... | collective-permute-start | bytes 393224 | tf_op jit(solution)/shard_map/ppermute | solution.py:37
  208.6 9.3 %collective-permute-start.58 = (f32[2,64,256]{2,1,0:T(8,128)S(1)}, f32[2,64,256]{2,1,0:T(8,128)S(1)}, u32[]{:S(2)}, u32[]{:S(2)}) collective-permute-start(f32[2,64,256]{2,1,0:T(8,128)S(1)} %get-tuple-element.231), channel_id=1, source_target_pairs={{0,64},{4,68},{64,0},{68,4},{1,65},{5,69},{65,1},{69,5},{2,66},{6,... | collective-permute-start | bytes 393224 | tf_op jit(solution)/shard_map/ppermute | solution.py:37
  211.9 6.0 %collective-permute-start.59 = (f32[2,64,256]{2,1,0:T(8,128)S(1)}, f32[2,64,256]{2,1,0:T(8,128)S(1)}, u32[]{:S(2)}, u32[]{:S(2)}) collective-permute-start(f32[2,64,256]{2,1,0:T(8,128)S(1)} %get-tuple-element.232), channel_id=1, source_target_pairs={{0,68},{4,0},{64,4},{68,64},{1,69},{5,1},{65,5},{69,65},{2,70},{6,... | collective-permute-start | bytes 393224 | tf_op jit(solution)/shard_map/ppermute | solution.py:37
  262.5 5.6 %collective-permute-start.64 = (f32[16,40,256]{2,1,0:T(8,128)S(1)}, f32[16,40,256]{2,1,0:T(8,128)S(1)}, u32[]{:S(2)}, u32[]{:S(2)}) collective-permute-start(f32[16,40,256]{2,1,0:T(8,128)S(1)} %all_to_all.11), channel_id=1, source_target_pairs={{0,32},{32,0},{1,33},{33,1},{2,34},{34,2},{3,35},{35,3},{4,36},{36... | collective-permute-start | bytes 1966088 | tf_op jit(solution)/shard_map/ppermute | solution.py:37
  (29 other events, 146.1 us)

commit v2 on v1

--- a/solution.py
+++ b/solution.py
@@ -41,11 +41,7 @@
     return along(value, "c", 1)
 
 
-def order(value, after):
-    return lax.optimization_barrier((value, after))[0]
-
-
-def local(kernel, tables, arrays, outs, scratch=(), flops=1_000_000):
+def local(kernel, tables, arrays, outs, scratch=(), flops=1_000_000, arrays_in=pltpu.VMEM, semaphores=()):
     vmem, smem = pl.BlockSpec(memory_space=pltpu.VMEM), pl.BlockSpec(memory_space=pltpu.SMEM)
     size = sum(a.size for a in arrays) + sum(math.prod(o) for o in outs if not isinstance(o, int))
     return pl.pallas_call(
@@ -54,13 +50,13 @@
             jax.ShapeDtypeStruct((o,), jnp.int32) if isinstance(o, int) else jax.ShapeDtypeStruct(o, F32)
             for o in outs
         ],
-        in_specs=[smem] * len(tables) + [vmem] * len(arrays),
+        in_specs=[smem] * len(tables) + [pl.BlockSpec(memory_space=arrays_in)] * len(arrays),
         out_specs=[smem if isinstance(o, int) else vmem for o in outs],
-        scratch_shapes=[pltpu.VMEM(s, F32) for s in scratch],
+        scratch_shapes=[pltpu.VMEM(s, F32) for s in scratch] + list(semaphores),
         cost_estimate=pl.CostEstimate(flops=flops, bytes_accessed=4 * size, transcendentals=0),
         compiler_params=pltpu.CompilerParams(vmem_limit_bytes=VMEM_LIMIT),
         interpret=INTERPRET,
-    )(*tables, *arrays)
+    )(*tables, *(a if arrays_in is pltpu.VMEM or INTERPRET else pltpu.with_memory_space_constraint(a, arrays_in) for a in arrays))
 
 
 def ahead(z, s):
@@ -75,35 +71,51 @@
     return pl.multiple_of(i * step, step)
 
 
-def give_tiles(place, dst, rel, own, init, cot, out, half):
-    c = place[1]
-    rows = own.shape[1] // 8
-    lane = lax.broadcasted_iota(jnp.int32, (8, own.shape[2]), 1) // 128
+def id_codes(place, lane):
     codes = jnp.zeros(lane.shape, F32)
     for j in range(2):
-        codes = jnp.where(lane == 2 * j, dst[j].astype(F32), codes)
-        codes = jnp.where(lane == 2 * j + 1, rel[j].astype(F32), codes)
+        codes = jnp.where(lane == 2 * j, place[4 + j].astype(F32), codes)
+        codes = jnp.where(lane == 2 * j + 1, place[6 + j].astype(F32), codes)
+    return codes
+
+
+def give_tiles(place, own, init, cot, out, half0, half1, sems):
+    c = place[1]
+    rows, width = own.shape[1] // 8, init.shape[1]
+    quarter = half0.shape[0]
+    copies = []
+
+    def copy(source, target):
+        copies.append(pltpu.make_async_copy(source, target, sems.at[len(copies)]))
+        copies[-1].start()
+
     for to in range(4):
+        at = row(to * 2 + 1 - c, rows)
         for j in range(2):
-            out[to, j * rows : (j + 1) * rows, :] = own[j, pl.ds(row(to * 2 + 1 - c, rows), rows), :]
+            copy(own.at[j, pl.ds(at, rows), :], out.at[to, j * rows : (j + 1) * rows, :])
+        for i in range(2):
+            copy(
+                cot.at[pl.ds(row(4 * to + 2 - 2 * c + i, rows // 2), rows // 2), :],
+                out.at[to, 2 * rows + 8 :, i * width : (i + 1) * width],
+            )
+    copy(init.at[pl.ds(row(2 * c, quarter), quarter), :], half0)
+    copy(init.at[pl.ds(row(2 * c + 1, quarter), quarter), :], half1)
+    lane = lax.broadcasted_iota(jnp.int32, (8, own.shape[2]), 1) // 128
+    codes = id_codes(place, lane)
+    for to in range(4):
         out[to, 2 * rows : 2 * rows + 8, :] = codes
-        lines = cot[pl.ds(row(to * 2 + 1 - c, rows), rows), :]
-        out[to, 2 * rows + 8 :, 0 : cot.shape[1]] = lines[0 : rows // 2]
-        out[to, 2 * rows + 8 :, cot.shape[1] :] = lines[rows // 2 :]
-    half[...] = init[pl.ds(row(c, half.shape[0]), half.shape[0]), :]
-
-
-def cut_tiles(core, place, dst, rel, own, got, *outs):
+    for waited in copies:
+        waited.wait()
+
+
+def cut_tiles(core, place, own, got, *outs):
     z, c = place[0], place[1]
     rows = own.shape[1] // 8
     lane = lax.broadcasted_iota(jnp.int32, (8, own.shape[2]), 1) // 128
 
     @pl.when(c == core)
     def _():
-        codes = jnp.zeros(lane.shape, F32)
-        for j in range(2):
-            codes = jnp.where(lane == 2 * j, dst[j].astype(F32), codes)
-            codes = jnp.where(lane == 2 * j + 1, rel[j].astype(F32), codes)
+        codes = id_codes(place, lane)
         for s in range(4):
             to = ahead(z, s)
             for j in range(2):
@@ -154,13 +166,14 @@
     lax.fori_loop(0, 2, step, 0)
 
 
-def spread_first(place, ids, tiles, rel_emb, init, near, far, o0, o1, o2, o3, own, full, slots):
+def spread_first(place, ids, tiles, rel_emb, init, near0, near1, far0, far1, o0, o1, o2, o3, own, full, slots):
     z, c, zl = place[0], place[1], place[2]
-    half = near.shape[0]
+    quarter = near0.shape[0]
     rows = tiles.shape[1] // 2
     full[zl] = init[...]
-    full[1 - zl, pl.ds(row(c, half), half), :] = near[...]
-    full[1 - zl, pl.ds(row(1 - c, half), half), :] = far[...]
+    for i, (near, far) in enumerate(((near0, far0), (near1, far1))):
+        full[1 - zl, pl.ds(row(2 * c + i, quarter), quarter), :] = near[...]
+        full[1 - zl, pl.ds(row(2 - 2 * c + i, quarter), quarter), :] = far[...]
     at = row(z * 2 + c, rows)
     for b in range(2):
         own[b * rows : (b + 1) * rows, :] = full[b, pl.ds(at, rows), :]
@@ -388,17 +401,23 @@
 
     own_tiles, own_cot, init = tiles[0, 0], cotangent[0, 0], init_state[0]
     here = jnp.stack([z, c, zl, y]).astype(jnp.int32)
-    codes = (here, dst_block.reshape(2), rel_id.reshape(2))
+    codes = (jnp.concatenate([here, dst_block.reshape(2), rel_id.reshape(2)]),)
     piece = (2 * rows + 8, tile)
-    give, half = local(give_tiles, codes, (own_tiles, init, own_cot), [(4, piece[0] + rows // 2, tile), (tile // 2, width)])
+    give, half0, half1 = local(
+        give_tiles,
+        codes,
+        (own_tiles, init, own_cot),
+        [(4, piece[0] + rows // 2, tile), (tile // 4, width), (tile // 4, width)],
+        arrays_in=pltpu.HBM,
+        semaphores=[pltpu.SemaphoreType.DMA((18,))],
+    )
     got_tiles = swap(give)
     held, ids = [None] * snaps, [None] * snaps
     part = [local(functools.partial(cut_tiles, core), codes, (own_tiles, got_tiles), [piece] * 4) for core in range(2)]
     ring = [part[0][0]] + [along(part[0][s], Z, s) for s in range(1, 4)]
-    near = along(order(half, part[0][1]), "zl", 1)
-    far = swap(near)
+    near = [along(half0, Z, 1), along(half1, Z, -1)]
+    far = [swap(v) for v in near]
     cut_cot = local(cut_rows, (here,), (own_cot, got_tiles), [pair] * 4)
-    ring, part[1], cut_cot = lax.optimization_barrier((ring, part[1], cut_cot))
 
     def join(core, ring):
         held[core], held[2 + core], ids[core], ids[2 + core] = local(
@@ -414,7 +433,7 @@
             *to_y, state = local(
                 spread_first,
                 (here, ids[0]),
-                (held[0], rel_emb, init, near, far),
+                (held[0], rel_emb, init, *near, *far),
                 [(2 * rows + 8, width)] * 4 + [flat],
                 work,
             )

time: 269 us -> 270 us (level)
  local copies, waits for them, and re-layouts: 6.63 us -> 2.41 us
    unnamed x24 -> x16, local copies, waits for them, and re-layouts: 5.02 us -> 0.05 us
    ppermute x65 -> x67, waiting for transfers between devices: 99.3 us -> 101 us  [along(): lax.ppermute(value, axis, [(i, (i + steps) % count) for i in range(count)])]
    ppermute x65 -> x67, starting transfers between devices: 92.2 us -> 93.7 us  [along(): lax.ppermute(value, axis, [(i, (i + steps) % count) for i in range(count)])]
  transfers between devices with their start and end apart: 65 -> 67, of which waited for: 43 -> 42; matrix products, arithmetic and copies ran while one was open for 0% -> 0% of each run, Pallas kernels for 6% -> 6%
where the time goes in v2:
time: 270 us
  waiting for transfers between devices  101 us (37%)
  starting transfers between devices  93.7 us (35%)
  Pallas kernels  40.5 us (15%)
  blocking collectives  30.8 us (11%)
    ppermute x67, waiting for transfers between devices, along(): lax.ppermute(value, axis, [(i, (i + steps) % count) for i in range(count)])  101 us
    ppermute x67, starting transfers between devices, along(): lax.ppermute(value, axis, [(i, (i + steps) % count) for i in range(count)])  93.7 us
    pallas_call x39, Pallas kernels, local(): pl.pallas_call(kernel, out_shape=[jax.ShapeDtypeStruct((o,), jnp.int32) i...  40.5 us
    all_to_all x1, blocking collectives, on_device(): lax.all_to_all(keep + swap(give), plane, 0, 0, tiled=True)  17.3 us
    all_to_all x1, blocking collectives, on_device(): lax.all_to_all(jnp.broadcast_to(summed[None], size), plane, 0, 0, tiled=T...  13.4 us
  transfers between devices with their start and end apart: 67, of which 42 were waited for; matrix products, arithmetic and copies ran while one was open for 0% of the time, Pallas kernels for 6%

profile of v2, /device:TPU:1, one launch (start us, length us, event | category | flops | bytes accessed | tf_op | source)
XLA Modules:
  0.0 270.2 jit_solution(9599096325901663681)
XLA Ops:
  1.4 2.2 shard_map.145
  5.1 2.8 %collective-permute-done.got = f32[4,168,512]{2,1,0:T(8,128)S(1)} collective-permute-done((f32[4,168,512]{2,1,0:T(8,128)S(1)}, f32[4,168,512]{2,1,0:T(8,128)S(1)}, u32[]{:S(2)}, u32[]{:S(2)}) %collective-permute-start) | collective-permute-done | bytes 1376288 | tf_op jit(solution)/shard_map/ppermute | solution.py:37
  10.3 3.3 %collective-permute-start.2 = (f32[136,512]{1,0:T(8,128)S(1)}, f32[136,512]{1,0:T(8,128)S(1)}, u32[]{:S(2)}, u32[]{:S(2)}) collective-permute-start(f32[136,512]{1,0:T(8,128)S(1)} %get-tuple-element.121), channel_id=1, source_target_pairs={{0,64},{4,68},{64,0},{68,4},{1,65},{5,69},{65,1},{69,5},{2,66},{6,... | collective-permute-start | bytes 835592 | tf_op jit(solution)/shard_map/ppermute | solution.py:37
  15.1 1.9 collective-permute-start.11
  17.0 10.9 %collective-permute-done.10.near0 = f32[128,256]{1,0:T(8,128)S(1)} collective-permute-done((f32[128,256]{1,0:T(8,128)S(1)}, f32[128,256]{1,0:T(8,128)S(1)}, u32[]{:S(2)}, u32[]{:S(2)}) %collective-permute-start.10) | collective-permute-done | bytes 131104 | tf_op jit(solution)/shard_map/ppermute | solution.py:37
  34.1 2.6 collective-permute-start.15
  39.4 4.1 %collective-permute-done.15.a2.l2 = f32[136,256]{1,0:T(8,128)S(1)} collective-permute-done((f32[136,256]{1,0:T(8,128)S(1)}, f32[136,256]{1,0:T(8,128)S(1)}, u32[]{:S(2)}, u32[]{:S(2)}) %collective-permute-start.15) | collective-permute-done | bytes 139296 | tf_op jit(solution)/shard_map/ppermute | solution.py:37
  44.3 2.4 collective-permute-start.19
  47.6 2.0 collective-permute-done.19.p3
  49.6 2.5 collective-permute-done.18.p2
  52.1 3.8 %collective-permute-done.17.p1 = f32[128,256]{1,0:T(8,128)S(1)} collective-permute-done((f32[128,256]{1,0:T(8,128)S(1)}, f32[128,256]{1,0:T(8,128)S(1)}, u32[]{:S(2)}, u32[]{:S(2)}) %collective-permute-start.17) | collective-permute-done | bytes 131104 | tf_op jit(solution)/shard_map/ppermute | solution.py:37
  61.2 12.4 %collective-permute-done.4.p1 = f32[136,512]{1,0:T(8,128)S(1)} collective-permute-done((f32[136,512]{1,0:T(8,128)S(1)}, f32[136,512]{1,0:T(8,128)S(1)}, u32[]{:S(2)}, u32[]{:S(2)}) %collective-permute-start.4) | collective-permute-done | bytes 278560 | tf_op jit(solution)/shard_map/ppermute | solution.py:37
  77.2 2.6 collective-permute-start.22
  81.8 3.0 %collective-permute-done.22.a2 = f32[128,256]{1,0:T(8,128)S(1)} collective-permute-done((f32[128,256]{1,0:T(8,128)S(1)}, f32[128,256]{1,0:T(8,128)S(1)}, u32[]{:S(2)}, u32[]{:S(2)}) %collective-permute-start.22) | collective-permute-done | bytes 131104 | tf_op jit(solution)/shard_map/ppermute | solution.py:37
  85.7 3.9 %collective-permute-start.26 = (f32[128,256]{1,0:T(8,128)S(1)}, f32[128,256]{1,0:T(8,128)S(1)}, u32[]{:S(2)}, u32[]{:S(2)}) collective-permute-start(f32[128,256]{1,0:T(8,128)S(1)} %get-tuple-element.156.p0.state.n1.refs_4_), channel_id=1, source_target_pairs={{0,68},{4,0},{64,4},{68,64},{1,69},{5,1},{65,5},{69,65},{2,70},{6,... | collective-permute-start | bytes 393224 | tf_op jit(solution)/shard_map/ppermute | solution.py:37
  90.3 2.3 collective-permute-done.26.p3
  92.5 2.5 collective-permute-done.25.p2
  95.0 3.3 %collective-permute-done.24.p1 = f32[128,256]{1,0:T(8,128)S(1)} collective-permute-done((f32[128,256]{1,0:T(8,128)S(1)}, f32[128,256]{1,0:T(8,128)S(1)}, u32[]{:S(2)}, u32[]{:S(2)}) %collective-permute-start.24) | collective-permute-done | bytes 131104 | tf_op jit(solution)/shard_map/ppermute | solution.py:37
  103.0 2.5 collective-permute-start.28
  109.4 3.7 %collective-permute-done.29.a2 = f32[128,256]{1,0:T(8,128)S(1)} collective-permute-done((f32[128,256]{1,0:T(8,128)S(1)}, f32[128,256]{1,0:T(8,128)S(1)}, u32[]{:S(2)}, u32[]{:S(2)}) %collective-permute-start.29) | collective-permute-done | bytes 131104 | tf_op jit(solution)/shard_map/ppermute | solution.py:37
  115.5 2.3 collective-permute-done.33.p3
  117.9 2.2 collective-permute-done.32.p2
  120.1 3.7 %collective-permute-done.31.p1 = f32[128,256]{1,0:T(8,128)S(1)} collective-permute-done((f32[128,256]{1,0:T(8,128)S(1)}, f32[128,256]{1,0:T(8,128)S(1)}, u32[]{:S(2)}, u32[]{:S(2)}) %collective-permute-start.31) | collective-permute-done | bytes 131104 | tf_op jit(solution)/shard_map/ppermute | solution.py:37
  131.7 2.2 collective-permute-start.36
  135.3 2.5 collective-permute-start.37
  142.6 3.5 %collective-permute-start.39 = (f32[2,64,256]{2,1,0:T(8,128)S(1)}, f32[2,64,256]{2,1,0:T(8,128)S(1)}, u32[]{:S(2)}, u32[]{:S(2)}) collective-permute-start(f32[2,64,256]{2,1,0:T(8,128)S(1)} %get-tuple-element.171.g0), channel_id=1, source_target_pairs={{0,16},{8,24},{16,0},{24,8},{1,17},{9,25},{17,1},{25,9},{2,18},{10... | collective-permute-start | bytes 393224 | tf_op jit(solution)/shard_map/ppermute | solution.py:37
  147.2 3.2 %collective-permute-done.39.g2 = f32[2,64,256]{2,1,0:T(8,128)S(1)} collective-permute-done((f32[2,64,256]{2,1,0:T(8,128)S(1)}, f32[2,64,256]{2,1,0:T(8,128)S(1)}, u32[]{:S(2)}, u32[]{:S(2)}) %collective-permute-start.39) | collective-permute-done | bytes 131104 | tf_op jit(solution)/shard_map/ppermute | solution.py:37
  152.5 2.4 collective-permute-start.41
  158.3 2.0 collective-permute-start.44
  163.9 2.0 collective-permute-done.42.d1
  167.6 2.9 %collective-permute-start.46 = (f32[2,64,256]{2,1,0:T(8,128)S(1)}, f32[2,64,256]{2,1,0:T(8,128)S(1)}, u32[]{:S(2)}, u32[]{:S(2)}) collective-permute-start(f32[2,64,256]{2,1,0:T(8,128)S(1)} %get-tuple-element.183.g0), channel_id=1, source_target_pairs={{0,16},{8,24},{16,0},{24,8},{1,17},{9,25},{17,1},{25,9},{2,18},{10... | collective-permute-start | bytes 393224 | tf_op jit(solution)/shard_map/ppermute | solution.py:37
  174.4 2.5 collective-permute-done.45.g1
  178.4 2.0 collective-permute-start.51
  180.4 1.9 collective-permute-done.51.got
  184.4 3.0 %collective-permute-start.53 = (f32[2,64,256]{2,1,0:T(8,128)S(1)}, f32[2,64,256]{2,1,0:T(8,128)S(1)}, u32[]{:S(2)}, u32[]{:S(2)}) collective-permute-start(f32[2,64,256]{2,1,0:T(8,128)S(1)} %get-tuple-element.195), channel_id=1, source_target_pairs={{0,64},{4,68},{64,0},{68,4},{1,65},{5,69},{65,1},{69,5},{2,66},{6,... | collective-permute-start | bytes 393224 | tf_op jit(solution)/shard_map/ppermute | solution.py:37
  189.7 3.7 %collective-permute-done.53.d2 = f32[2,64,256]{2,1,0:T(8,128)S(1)} collective-permute-done((f32[2,64,256]{2,1,0:T(8,128)S(1)}, f32[2,64,256]{2,1,0:T(8,128)S(1)}, u32[]{:S(2)}, u32[]{:S(2)}) %collective-permute-start.53) | collective-permute-done | bytes 131104 | tf_op jit(solution)/shard_map/ppermute | solution.py:37
  194.8 3.1 %collective-permute-start.56 = (f32[2,64,256]{2,1,0:T(8,128)S(1)}, f32[2,64,256]{2,1,0:T(8,128)S(1)}, u32[]{:S(2)}, u32[]{:S(2)}) collective-permute-start(f32[2,64,256]{2,1,0:T(8,128)S(1)} %get-tuple-element.202.g0), channel_id=1, source_target_pairs={{0,16},{8,24},{16,0},{24,8},{1,17},{9,25},{17,1},{25,9},{2,18},{10... | collective-permute-start | bytes 393224 | tf_op jit(solution)/shard_map/ppermute | solution.py:37
  199.3 3.3 %collective-permute-done.56.g2 = f32[2,64,256]{2,1,0:T(8,128)S(1)} collective-permute-done((f32[2,64,256]{2,1,0:T(8,128)S(1)}, f32[2,64,256]{2,1,0:T(8,128)S(1)}, u32[]{:S(2)}, u32[]{:S(2)}) %collective-permute-start.56) | collective-permute-done | bytes 131104 | tf_op jit(solution)/shard_map/ppermute | solution.py:37
  204.2 2.4 collective-permute-start.58
  209.7 3.1 %collective-permute-start.60 = (f32[2,64,256]{2,1,0:T(8,128)S(1)}, f32[2,64,256]{2,1,0:T(8,128)S(1)}, u32[]{:S(2)}, u32[]{:S(2)}) collective-permute-start(f32[2,64,256]{2,1,0:T(8,128)S(1)} %get-tuple-element.207), channel_id=1, source_target_pairs={{0,64},{4,68},{64,0},{68,4},{1,65},{5,69},{65,1},{69,5},{2,66},{6,... | collective-permute-start | bytes 393224 | tf_op jit(solution)/shard_map/ppermute | solution.py:37
  212.8 2.3 shard_map.182
  215.1 3.7 %collective-permute-done.60.d2 = f32[2,64,256]{2,1,0:T(8,128)S(1)} collective-permute-done((f32[2,64,256]{2,1,0:T(8,128)S(1)}, f32[2,64,256]{2,1,0:T(8,128)S(1)}, u32[]{:S(2)}, u32[]{:S(2)}) %collective-permute-start.60) | collective-permute-done | bytes 131104 | tf_op jit(solution)/shard_map/ppermute | solution.py:37
  220.2 2.2 shard_map.183
  225.6 17.3 %all_to_all.10 = f32[16,40,256]{2,1,0:T(8,128)S(1)} all-to-all(f32[16,40,256]{2,1,0:T(8,128)S(1)} %add.16), channel_id=1, replica_groups=mesh['zh'=2,'c'=2,'y'=4,'zl'=2,'b'=4] {'zh','zl','y'}, dimensions={0} | all-to-all | bytes 1310720 | tf_op jit(solution)/shard_map/all_to_all | solution.py:513
  243.0 2.5 collective-permute-start.65
  247.2 2.8 %collective-permute-done.64 = f32[40,256]{1,0:T(8,128)S(1)} collective-permute-done((f32[40,256]{1,0:T(8,128)S(1)}, f32[40,256]{1,0:T(8,128)S(1)}, u32[]{:S(2)}, u32[]{:S(2)}) %collective-permute-start.64) | collective-permute-done | bytes 40992 | tf_op jit(solution)/shard_map/ppermute | solution.py:37
  250.1 13.4 %all_to_all.11 = f32[16,40,256]{2,1,0:T(8,128)S(1)} all-to-all(f32[16,40,256]{2,1,0:T(8,128)S(1)} %broadcast_in_dim.2), channel_id=1, replica_groups=mesh['zh'=2,'c'=2,'y'=4,'zl'=2,'b'=4] {'zh','zl','y'}, dimensions={0} | all-to-all | bytes 1310720 | tf_op jit(solution)/shard_map/all_to_all | solution.py:515
  263.5 3.6 %collective-permute-start.66 = (f32[16,40,256]{2,1,0:T(8,128)S(1)}, f32[16,40,256]{2,1,0:T(8,128)S(1)}, u32[]{:S(2)}, u32[]{:S(2)}) collective-permute-start(f32[16,40,256]{2,1,0:T(8,128)S(1)} %all_to_all.11), channel_id=1, source_target_pairs={{0,32},{32,0},{1,33},{33,1},{2,34},{34,2},{3,35},{35,3},{4,36},{36... | collective-permute-start | bytes 1966088 | tf_op jit(solution)/shard_map/ppermute | solution.py:37
  (152 shorter events, 92.3 us)
Async XLA Ops:
  8.5 21.1 %collective-permute-start.1 = (f32[136,512]{1,0:T(8,128)S(1)}, f32[136,512]{1,0:T(8,128)S(1)}, u32[]{:S(2)}, u32[]{:S(2)}) collective-permute-start(f32[136,512]{1,0:T(8,128)S(1)} %get-tuple-element.120), channel_id=1, source_target_pairs={{0,4},{4,64},{64,68},{68,0},{1,5},{5,65},{65,69},{69,1},{2,6},{6,6... | collective-permute-start | bytes 835592 | tf_op jit(solution)/shard_map/ppermute | solution.py:37
  10.3 19.3 %collective-permute-start.2 = (f32[136,512]{1,0:T(8,128)S(1)}, f32[136,512]{1,0:T(8,128)S(1)}, u32[]{:S(2)}, u32[]{:S(2)}) collective-permute-start(f32[136,512]{1,0:T(8,128)S(1)} %get-tuple-element.121), channel_id=1, source_target_pairs={{0,64},{4,68},{64,0},{68,4},{1,65},{5,69},{65,1},{69,5},{2,66},{6,... | collective-permute-start | bytes 835592 | tf_op jit(solution)/shard_map/ppermute | solution.py:37
  13.6 16.0 %collective-permute-start.3 = (f32[136,512]{1,0:T(8,128)S(1)}, f32[136,512]{1,0:T(8,128)S(1)}, u32[]{:S(2)}, u32[]{:S(2)}) collective-permute-start(f32[136,512]{1,0:T(8,128)S(1)} %get-tuple-element.122), channel_id=1, source_target_pairs={{0,68},{4,0},{64,4},{68,64},{1,69},{5,1},{65,5},{69,65},{2,70},{6,... | collective-permute-start | bytes 835592 | tf_op jit(solution)/shard_map/ppermute | solution.py:37
  14.4 13.5 %collective-permute-start.10 = (f32[128,256]{1,0:T(8,128)S(1)}, f32[128,256]{1,0:T(8,128)S(1)}, u32[]{:S(2)}, u32[]{:S(2)}) collective-permute-start(f32[128,256]{1,0:T(8,128)S(1)} %get-tuple-element.140), channel_id=1, source_target_pairs={{0,4},{4,64},{64,68},{68,0},{1,5},{5,65},{65,69},{69,1},{2,6},{6,6... | collective-permute-start | bytes 393224 | tf_op jit(solution)/shard_map/ppermute | solution.py:37
  15.1 13.7 %collective-permute-start.11 = (f32[128,256]{1,0:T(8,128)S(1)}, f32[128,256]{1,0:T(8,128)S(1)}, u32[]{:S(2)}, u32[]{:S(2)}) collective-permute-start(f32[128,256]{1,0:T(8,128)S(1)} %get-tuple-element.141), channel_id=1, source_target_pairs={{0,68},{4,0},{64,4},{68,64},{1,69},{5,1},{65,5},{69,65},{2,70},{6,... | collective-permute-start | bytes 393224 | tf_op jit(solution)/shard_map/ppermute | solution.py:37
  32.8 6.6 %collective-permute-start.14 = (f32[136,256]{1,0:T(8,128)S(1)}, f32[136,256]{1,0:T(8,128)S(1)}, u32[]{:S(2)}, u32[]{:S(2)}) collective-permute-start(f32[136,256]{1,0:T(8,128)S(1)} %get-tuple-element.143), channel_id=1, source_target_pairs={{0,8},{8,16},{16,24},{24,0},{1,9},{9,17},{17,25},{25,1},{2,10},{10... | collective-permute-start | bytes 417800 | tf_op jit(solution)/shard_map/ppermute | solution.py:37
  34.1 9.4 %collective-permute-start.15 = (f32[136,256]{1,0:T(8,128)S(1)}, f32[136,256]{1,0:T(8,128)S(1)}, u32[]{:S(2)}, u32[]{:S(2)}) collective-permute-start(f32[136,256]{1,0:T(8,128)S(1)} %get-tuple-element.144), channel_id=1, source_target_pairs={{0,16},{8,24},{16,0},{24,8},{1,17},{9,25},{17,1},{25,9},{2,18},{10... | collective-permute-start | bytes 417800 | tf_op jit(solution)/shard_map/ppermute | solution.py:37
  36.7 6.7 %collective-permute-start.16 = (f32[136,256]{1,0:T(8,128)S(1)}, f32[136,256]{1,0:T(8,128)S(1)}, u32[]{:S(2)}, u32[]{:S(2)}) collective-permute-start(f32[136,256]{1,0:T(8,128)S(1)} %get-tuple-element.145), channel_id=1, source_target_pairs={{0,24},{8,0},{16,8},{24,16},{1,25},{9,1},{17,9},{25,17},{2,26},{10... | collective-permute-start | bytes 417800 | tf_op jit(solution)/shard_map/ppermute | solution.py:37
  44.3 5.4 %collective-permute-start.19 = (f32[128,256]{1,0:T(8,128)S(1)}, f32[128,256]{1,0:T(8,128)S(1)}, u32[]{:S(2)}, u32[]{:S(2)}) collective-permute-start(f32[128,256]{1,0:T(8,128)S(1)} %get-tuple-element.149.p0.state.n0.refs_3_), channel_id=1, source_target_pairs={{0,68},{4,0},{64,4},{68,64},{1,69},{5,1},{65,5},{69,65},{2,70},{6,... | collective-permute-start | bytes 393224 | tf_op jit(solution)/shard_map/ppermute | solution.py:37
  46.7 5.4 %collective-permute-start.18 = (f32[128,256]{1,0:T(8,128)S(1)}, f32[128,256]{1,0:T(8,128)S(1)}, u32[]{:S(2)}, u32[]{:S(2)}) collective-permute-start(f32[128,256]{1,0:T(8,128)S(1)} %get-tuple-element.149.p0.state.n0.refs_3_), channel_id=1, source_target_pairs={{0,64},{4,68},{64,0},{68,4},{1,65},{5,69},{65,1},{69,5},{2,66},{6,... | collective-permute-start | bytes 393224 | tf_op jit(solution)/shard_map/ppermute | solution.py:37
  47.5 8.3 %collective-permute-start.17 = (f32[128,256]{1,0:T(8,128)S(1)}, f32[128,256]{1,0:T(8,128)S(1)}, u32[]{:S(2)}, u32[]{:S(2)}) collective-permute-start(f32[128,256]{1,0:T(8,128)S(1)} %get-tuple-element.149.p0.state.n0.refs_3_), channel_id=1, source_target_pairs={{0,4},{4,64},{64,68},{68,0},{1,5},{5,65},{65,69},{69,1},{2,6},{6,6... | collective-permute-start | bytes 393224 | tf_op jit(solution)/shard_map/ppermute | solution.py:37
  56.4 18.9 %collective-permute-start.20 = (f32[4,128,256]{2,1,0:T(8,128)S(1)}, f32[4,128,256]{2,1,0:T(8,128)S(1)}, u32[]{:S(2)}, u32[]{:S(2)}) collective-permute-start(f32[4,128,256]{2,1,0:T(8,128)S(1)} %shard_map.155), channel_id=1, source_target_pairs={{0,32},{32,0},{1,33},{33,1},{2,34},{34,2},{3,35},{35,3},{4,36},{36... | collective-permute-start | bytes 1572872 | tf_op jit(solution)/shard_map/ppermute | solution.py:37
  58.2 15.4 %collective-permute-start.4 = (f32[136,512]{1,0:T(8,128)S(1)}, f32[136,512]{1,0:T(8,128)S(1)}, u32[]{:S(2)}, u32[]{:S(2)}) collective-permute-start(f32[136,512]{1,0:T(8,128)S(1)} %get-tuple-element.126), channel_id=1, source_target_pairs={{0,4},{4,64},{64,68},{68,0},{1,5},{5,65},{65,69},{69,1},{2,6},{6,6... | collective-permute-start | bytes 835592 | tf_op jit(solution)/shard_map/ppermute | solution.py:37
  58.3 15.4 %collective-permute-start.5 = (f32[136,512]{1,0:T(8,128)S(1)}, f32[136,512]{1,0:T(8,128)S(1)}, u32[]{:S(2)}, u32[]{:S(2)}) collective-permute-start(f32[136,512]{1,0:T(8,128)S(1)} %get-tuple-element.127), channel_id=1, source_target_pairs={{0,64},{4,68},{64,0},{68,4},{1,65},{5,69},{65,1},{69,5},{2,66},{6,... | collective-permute-start | bytes 835592 | tf_op jit(solution)/shard_map/ppermute | solution.py:37
  59.7 14.3 %collective-permute-start.6 = (f32[136,512]{1,0:T(8,128)S(1)}, f32[136,512]{1,0:T(8,128)S(1)}, u32[]{:S(2)}, u32[]{:S(2)}) collective-permute-start(f32[136,512]{1,0:T(8,128)S(1)} %get-tuple-element.128), channel_id=1, source_target_pairs={{0,68},{4,0},{64,4},{68,64},{1,69},{5,1},{65,5},{69,65},{2,70},{6,... | collective-permute-start | bytes 835592 | tf_op jit(solution)/shard_map/ppermute | solution.py:37
  77.2 7.6 %collective-permute-start.22 = (f32[128,256]{1,0:T(8,128)S(1)}, f32[128,256]{1,0:T(8,128)S(1)}, u32[]{:S(2)}, u32[]{:S(2)}) collective-permute-start(f32[128,256]{1,0:T(8,128)S(1)} %get-tuple-element.152), channel_id=1, source_target_pairs={{0,16},{8,24},{16,0},{24,8},{1,17},{9,25},{17,1},{25,9},{2,18},{10... | collective-permute-start | bytes 393224 | tf_op jit(solution)/shard_map/ppermute | solution.py:37
  85.7 6.8 %collective-permute-start.26 = (f32[128,256]{1,0:T(8,128)S(1)}, f32[128,256]{1,0:T(8,128)S(1)}, u32[]{:S(2)}, u32[]{:S(2)}) collective-permute-start(f32[128,256]{1,0:T(8,128)S(1)} %get-tuple-element.156.p0.state.n1.refs_4_), channel_id=1, source_target_pairs={{0,68},{4,0},{64,4},{68,64},{1,69},{5,1},{65,5},{69,65},{2,70},{6,... | collective-permute-start | bytes 393224 | tf_op jit(solution)/shard_map/ppermute | solution.py:37
  89.6 5.4 %collective-permute-start.25 = (f32[128,256]{1,0:T(8,128)S(1)}, f32[128,256]{1,0:T(8,128)S(1)}, u32[]{:S(2)}, u32[]{:S(2)}) collective-permute-start(f32[128,256]{1,0:T(8,128)S(1)} %get-tuple-element.156.p0.state.n1.refs_4_), channel_id=1, source_target_pairs={{0,64},{4,68},{64,0},{68,4},{1,65},{5,69},{65,1},{69,5},{2,66},{6,... | collective-permute-start | bytes 393224 | tf_op jit(solution)/shard_map/ppermute | solution.py:37
  89.6 8.7 %collective-permute-start.24 = (f32[128,256]{1,0:T(8,128)S(1)}, f32[128,256]{1,0:T(8,128)S(1)}, u32[]{:S(2)}, u32[]{:S(2)}) collective-permute-start(f32[128,256]{1,0:T(8,128)S(1)} %get-tuple-element.156.p0.state.n1.refs_4_), channel_id=1, source_target_pairs={{0,4},{4,64},{64,68},{68,0},{1,5},{5,65},{65,69},{69,1},{2,6},{6,6... | collective-permute-start | bytes 393224 | tf_op jit(solution)/shard_map/ppermute | solution.py:37
  103.0 6.4 %collective-permute-start.28 = (f32[128,256]{1,0:T(8,128)S(1)}, f32[128,256]{1,0:T(8,128)S(1)}, u32[]{:S(2)}, u32[]{:S(2)}) collective-permute-start(f32[128,256]{1,0:T(8,128)S(1)} %get-tuple-element.158), channel_id=1, source_target_pairs={{0,8},{8,16},{16,24},{24,0},{1,9},{9,17},{17,25},{25,1},{2,10},{10... | collective-permute-start | bytes 393224 | tf_op jit(solution)/shard_map/ppermute | solution.py:37
  105.4 7.7 %collective-permute-start.29 = (f32[128,256]{1,0:T(8,128)S(1)}, f32[128,256]{1,0:T(8,128)S(1)}, u32[]{:S(2)}, u32[]{:S(2)}) collective-permute-start(f32[128,256]{1,0:T(8,128)S(1)} %get-tuple-element.159), channel_id=1, source_target_pairs={{0,16},{8,24},{16,0},{24,8},{1,17},{9,25},{17,1},{25,9},{2,18},{10... | collective-permute-start | bytes 393224 | tf_op jit(solution)/shard_map/ppermute | solution.py:37
  107.2 6.0 %collective-permute-start.30 = (f32[128,256]{1,0:T(8,128)S(1)}, f32[128,256]{1,0:T(8,128)S(1)}, u32[]{:S(2)}, u32[]{:S(2)}) collective-permute-start(f32[128,256]{1,0:T(8,128)S(1)} %get-tuple-element.160), channel_id=1, source_target_pairs={{0,24},{8,0},{16,8},{24,16},{1,25},{9,1},{17,9},{25,17},{2,26},{10... | collective-permute-start | bytes 393224 | tf_op jit(solution)/shard_map/ppermute | solution.py:37
  114.7 5.4 %collective-permute-start.32 = (f32[128,256]{1,0:T(8,128)S(1)}, f32[128,256]{1,0:T(8,128)S(1)}, u32[]{:S(2)}, u32[]{:S(2)}) collective-permute-start(f32[128,256]{1,0:T(8,128)S(1)} %get-tuple-element.163.state.p0.n2.refs_5_), channel_id=1, source_target_pairs={{0,64},{4,68},{64,0},{68,4},{1,65},{5,69},{65,1},{69,5},{2,66},{6,... | collective-permute-start | bytes 393224 | tf_op jit(solution)/shard_map/ppermute | solution.py:37
  114.7 9.1 %collective-permute-start.31 = (f32[128,256]{1,0:T(8,128)S(1)}, f32[128,256]{1,0:T(8,128)S(1)}, u32[]{:S(2)}, u32[]{:S(2)}) collective-permute-start(f32[128,256]{1,0:T(8,128)S(1)} %get-tuple-element.163.state.p0.n2.refs_5_), channel_id=1, source_target_pairs={{0,4},{4,64},{64,68},{68,0},{1,5},{5,65},{65,69},{69,1},{2,6},{6,6... | collective-permute-start | bytes 393224 | tf_op jit(solution)/shard_map/ppermute | solution.py:37
  126.1 9.1 %collective-permute-start.7 = (f32[2,64,256]{2,1,0:T(8,128)S(1)}, f32[2,64,256]{2,1,0:T(8,128)S(1)}, u32[]{:S(2)}, u32[]{:S(2)}) collective-permute-start(f32[2,64,256]{2,1,0:T(8,128)S(1)} %get-tuple-element.132), channel_id=1, source_target_pairs={{0,4},{4,64},{64,68},{68,0},{1,5},{5,65},{65,69},{69,1},{2,6},{6,6... | collective-permute-start | bytes 393224 | tf_op jit(solution)/shard_map/ppermute | solution.py:37
  126.2 11.6 %collective-permute-start.8 = (f32[2,64,256]{2,1,0:T(8,128)S(1)}, f32[2,64,256]{2,1,0:T(8,128)S(1)}, u32[]{:S(2)}, u32[]{:S(2)}) collective-permute-start(f32[2,64,256]{2,1,0:T(8,128)S(1)} %get-tuple-element.133), channel_id=1, source_target_pairs={{0,64},{4,68},{64,0},{68,4},{1,65},{5,69},{65,1},{69,5},{2,66},{6,... | collective-permute-start | bytes 393224 | tf_op jit(solution)/shard_map/ppermute | solution.py:37
  127.7 10.1 %collective-permute-start.9 = (f32[2,64,256]{2,1,0:T(8,128)S(1)}, f32[2,64,256]{2,1,0:T(8,128)S(1)}, u32[]{:S(2)}, u32[]{:S(2)}) collective-permute-start(f32[2,64,256]{2,1,0:T(8,128)S(1)} %get-tuple-element.134), channel_id=1, source_target_pairs={{0,68},{4,0},{64,4},{68,64},{1,69},{5,1},{65,5},{69,65},{2,70},{6,... | collective-permute-start | bytes 393224 | tf_op jit(solution)/shard_map/ppermute | solution.py:37
  130.2 9.1 %collective-permute-start.35 = (f32[128,256]{1,0:T(8,128)S(1)}, f32[128,256]{1,0:T(8,128)S(1)}, u32[]{:S(2)}, u32[]{:S(2)}) collective-permute-start(f32[128,256]{1,0:T(8,128)S(1)} %get-tuple-element.166), channel_id=1, source_target_pairs={{0,8},{8,16},{16,24},{24,0},{1,9},{9,17},{17,25},{25,1},{2,10},{10... | collective-permute-start | bytes 393224 | tf_op jit(solution)/shard_map/ppermute | solution.py:37
  131.7 8.1 %collective-permute-start.36 = (f32[128,256]{1,0:T(8,128)S(1)}, f32[128,256]{1,0:T(8,128)S(1)}, u32[]{:S(2)}, u32[]{:S(2)}) collective-permute-start(f32[128,256]{1,0:T(8,128)S(1)} %get-tuple-element.167), channel_id=1, source_target_pairs={{0,16},{8,24},{16,0},{24,8},{1,17},{9,25},{17,1},{25,9},{2,18},{10... | collective-permute-start | bytes 393224 | tf_op jit(solution)/shard_map/ppermute | solution.py:37
  141.4 5.8 %collective-permute-start.40 = (f32[2,64,256]{2,1,0:T(8,128)S(1)}, f32[2,64,256]{2,1,0:T(8,128)S(1)}, u32[]{:S(2)}, u32[]{:S(2)}) collective-permute-start(f32[2,64,256]{2,1,0:T(8,128)S(1)} %get-tuple-element.171.g0), channel_id=1, source_target_pairs={{0,8},{8,16},{16,24},{24,0},{1,9},{9,17},{17,25},{25,1},{2,10},{10... | collective-permute-start | bytes 393224 | tf_op jit(solution)/shard_map/ppermute | solution.py:37
  142.6 7.8 %collective-permute-start.39 = (f32[2,64,256]{2,1,0:T(8,128)S(1)}, f32[2,64,256]{2,1,0:T(8,128)S(1)}, u32[]{:S(2)}, u32[]{:S(2)}) collective-permute-start(f32[2,64,256]{2,1,0:T(8,128)S(1)} %get-tuple-element.171.g0), channel_id=1, source_target_pairs={{0,16},{8,24},{16,0},{24,8},{1,17},{9,25},{17,1},{25,9},{2,18},{10... | collective-permute-start | bytes 393224 | tf_op jit(solution)/shard_map/ppermute | solution.py:37
  157.1 8.8 %collective-permute-start.42 = (f32[2,64,256]{2,1,0:T(8,128)S(1)}, f32[2,64,256]{2,1,0:T(8,128)S(1)}, u32[]{:S(2)}, u32[]{:S(2)}) collective-permute-start(f32[2,64,256]{2,1,0:T(8,128)S(1)} %get-tuple-element.175), channel_id=1, source_target_pairs={{0,4},{4,64},{64,68},{68,0},{1,5},{5,65},{65,69},{69,1},{2,6},{6,6... | collective-permute-start | bytes 393224 | tf_op jit(solution)/shard_map/ppermute | solution.py:37
  157.1 8.8 %collective-permute-start.43 = (f32[2,64,256]{2,1,0:T(8,128)S(1)}, f32[2,64,256]{2,1,0:T(8,128)S(1)}, u32[]{:S(2)}, u32[]{:S(2)}) collective-permute-start(f32[2,64,256]{2,1,0:T(8,128)S(1)} %get-tuple-element.176), channel_id=1, source_target_pairs={{0,64},{4,68},{64,0},{68,4},{1,65},{5,69},{65,1},{69,5},{2,66},{6,... | collective-permute-start | bytes 393224 | tf_op jit(solution)/shard_map/ppermute | solution.py:37
  158.3 8.3 %collective-permute-start.44 = (f32[2,64,256]{2,1,0:T(8,128)S(1)}, f32[2,64,256]{2,1,0:T(8,128)S(1)}, u32[]{:S(2)}, u32[]{:S(2)}) collective-permute-start(f32[2,64,256]{2,1,0:T(8,128)S(1)} %get-tuple-element.177), channel_id=1, source_target_pairs={{0,68},{4,0},{64,4},{68,64},{1,69},{5,1},{65,5},{69,65},{2,70},{6,... | collective-permute-start | bytes 393224 | tf_op jit(solution)/shard_map/ppermute | solution.py:37
  160.9 10.6 %collective-permute-start.48 = (f32[2,64,256]{2,1,0:T(8,128)S(1)}, f32[2,64,256]{2,1,0:T(8,128)S(1)}, u32[]{:S(2)}, u32[]{:S(2)}) collective-permute-start(f32[2,64,256]{2,1,0:T(8,128)S(1)} %get-tuple-element.186), channel_id=1, source_target_pairs={{0,4},{4,64},{64,68},{68,0},{1,5},{5,65},{65,69},{69,1},{2,6},{6,6... | collective-permute-start | bytes 393224 | tf_op jit(solution)/shard_map/ppermute | solution.py:37
  161.1 12.2 %collective-permute-start.49 = (f32[2,64,256]{2,1,0:T(8,128)S(1)}, f32[2,64,256]{2,1,0:T(8,128)S(1)}, u32[]{:S(2)}, u32[]{:S(2)}) collective-permute-start(f32[2,64,256]{2,1,0:T(8,128)S(1)} %get-tuple-element.187), channel_id=1, source_target_pairs={{0,64},{4,68},{64,0},{68,4},{1,65},{5,69},{65,1},{69,5},{2,66},{6,... | collective-permute-start | bytes 393224 | tf_op jit(solution)/shard_map/ppermute | solution.py:37
  165.9 7.4 %collective-permute-start.50 = (f32[2,64,256]{2,1,0:T(8,128)S(1)}, f32[2,64,256]{2,1,0:T(8,128)S(1)}, u32[]{:S(2)}, u32[]{:S(2)}) collective-permute-start(f32[2,64,256]{2,1,0:T(8,128)S(1)} %get-tuple-element.188), channel_id=1, source_target_pairs={{0,68},{4,0},{64,4},{68,64},{1,69},{5,1},{65,5},{69,65},{2,70},{6,... | collective-permute-start | bytes 393224 | tf_op jit(solution)/shard_map/ppermute | solution.py:37
  167.5 5.8 %collective-permute-start.47 = (f32[2,64,256]{2,1,0:T(8,128)S(1)}, f32[2,64,256]{2,1,0:T(8,128)S(1)}, u32[]{:S(2)}, u32[]{:S(2)}) collective-permute-start(f32[2,64,256]{2,1,0:T(8,128)S(1)} %get-tuple-element.183.g0), channel_id=1, source_target_pairs={{0,8},{8,16},{16,24},{24,0},{1,9},{9,17},{17,25},{25,1},{2,10},{10... | collective-permute-start | bytes 393224 | tf_op jit(solution)/shard_map/ppermute | solution.py:37
  167.6 6.8 %collective-permute-start.46 = (f32[2,64,256]{2,1,0:T(8,128)S(1)}, f32[2,64,256]{2,1,0:T(8,128)S(1)}, u32[]{:S(2)}, u32[]{:S(2)}) collective-permute-start(f32[2,64,256]{2,1,0:T(8,128)S(1)} %get-tuple-element.183.g0), channel_id=1, source_target_pairs={{0,16},{8,24},{16,0},{24,8},{1,17},{9,25},{17,1},{25,9},{2,18},{10... | collective-permute-start | bytes 393224 | tf_op jit(solution)/shard_map/ppermute | solution.py:37
  171.5 5.4 %collective-permute-start.45 = (f32[2,64,256]{2,1,0:T(8,128)S(1)}, f32[2,64,256]{2,1,0:T(8,128)S(1)}, u32[]{:S(2)}, u32[]{:S(2)}) collective-permute-start(f32[2,64,256]{2,1,0:T(8,128)S(1)} %get-tuple-element.183.g0), channel_id=1, source_target_pairs={{0,24},{8,0},{16,8},{24,16},{1,25},{9,1},{17,9},{25,17},{2,26},{10... | collective-permute-start | bytes 393224 | tf_op jit(solution)/shard_map/ppermute | solution.py:37
  182.9 6.8 %collective-permute-start.52 = (f32[2,64,256]{2,1,0:T(8,128)S(1)}, f32[2,64,256]{2,1,0:T(8,128)S(1)}, u32[]{:S(2)}, u32[]{:S(2)}) collective-permute-start(f32[2,64,256]{2,1,0:T(8,128)S(1)} %get-tuple-element.194), channel_id=1, source_target_pairs={{0,4},{4,64},{64,68},{68,0},{1,5},{5,65},{65,69},{69,1},{2,6},{6,6... | collective-permute-start | bytes 393224 | tf_op jit(solution)/shard_map/ppermute | solution.py:37
  184.4 9.0 %collective-permute-start.53 = (f32[2,64,256]{2,1,0:T(8,128)S(1)}, f32[2,64,256]{2,1,0:T(8,128)S(1)}, u32[]{:S(2)}, u32[]{:S(2)}) collective-permute-start(f32[2,64,256]{2,1,0:T(8,128)S(1)} %get-tuple-element.195), channel_id=1, source_target_pairs={{0,64},{4,68},{64,0},{68,4},{1,65},{5,69},{65,1},{69,5},{2,66},{6,... | collective-permute-start | bytes 393224 | tf_op jit(solution)/shard_map/ppermute | solution.py:37
  187.4 6.0 %collective-permute-start.54 = (f32[2,64,256]{2,1,0:T(8,128)S(1)}, f32[2,64,256]{2,1,0:T(8,128)S(1)}, u32[]{:S(2)}, u32[]{:S(2)}) collective-permute-start(f32[2,64,256]{2,1,0:T(8,128)S(1)} %get-tuple-element.196), channel_id=1, source_target_pairs={{0,68},{4,0},{64,4},{68,64},{1,69},{5,1},{65,5},{69,65},{2,70},{6,... | collective-permute-start | bytes 393224 | tf_op jit(solution)/shard_map/ppermute | solution.py:37
  194.8 7.9 %collective-permute-start.56 = (f32[2,64,256]{2,1,0:T(8,128)S(1)}, f32[2,64,256]{2,1,0:T(8,128)S(1)}, u32[]{:S(2)}, u32[]{:S(2)}) collective-permute-start(f32[2,64,256]{2,1,0:T(8,128)S(1)} %get-tuple-element.202.g0), channel_id=1, source_target_pairs={{0,16},{8,24},{16,0},{24,8},{1,17},{9,25},{17,1},{25,9},{2,18},{10... | collective-permute-start | bytes 393224 | tf_op jit(solution)/shard_map/ppermute | solution.py:37
  208.8 6.3 %collective-permute-start.59 = (f32[2,64,256]{2,1,0:T(8,128)S(1)}, f32[2,64,256]{2,1,0:T(8,128)S(1)}, u32[]{:S(2)}, u32[]{:S(2)}) collective-permute-start(f32[2,64,256]{2,1,0:T(8,128)S(1)} %get-tuple-element.206), channel_id=1, source_target_pairs={{0,4},{4,64},{64,68},{68,0},{1,5},{5,65},{65,69},{69,1},{2,6},{6,6... | collective-permute-start | bytes 393224 | tf_op jit(solution)/shard_map/ppermute | solution.py:37
  209.7 9.2 %collective-permute-start.60 = (f32[2,64,256]{2,1,0:T(8,128)S(1)}, f32[2,64,256]{2,1,0:T(8,128)S(1)}, u32[]{:S(2)}, u32[]{:S(2)}) collective-permute-start(f32[2,64,256]{2,1,0:T(8,128)S(1)} %get-tuple-element.207), channel_id=1, source_target_pairs={{0,64},{4,68},{64,0},{68,4},{1,65},{5,69},{65,1},{69,5},{2,66},{6,... | collective-permute-start | bytes 393224 | tf_op jit(solution)/shard_map/ppermute | solution.py:37
  212.8 6.0 %collective-permute-start.61 = (f32[2,64,256]{2,1,0:T(8,128)S(1)}, f32[2,64,256]{2,1,0:T(8,128)S(1)}, u32[]{:S(2)}, u32[]{:S(2)}) collective-permute-start(f32[2,64,256]{2,1,0:T(8,128)S(1)} %get-tuple-element.208), channel_id=1, source_target_pairs={{0,68},{4,0},{64,4},{68,64},{1,69},{5,1},{65,5},{69,65},{2,70},{6,... | collective-permute-start | bytes 393224 | tf_op jit(solution)/shard_map/ppermute | solution.py:37
  263.5 5.6 %collective-permute-start.66 = (f32[16,40,256]{2,1,0:T(8,128)S(1)}, f32[16,40,256]{2,1,0:T(8,128)S(1)}, u32[]{:S(2)}, u32[]{:S(2)}) collective-permute-start(f32[16,40,256]{2,1,0:T(8,128)S(1)} %all_to_all.11), channel_id=1, source_target_pairs={{0,32},{32,0},{1,33},{33,1},{2,34},{34,2},{3,35},{35,3},{4,36},{36... | collective-permute-start | bytes 1966088 | tf_op jit(solution)/shard_map/ppermute | solution.py:37
  (27 other events, 190.6 us)

commit v3 on v2

--- a/solution.py
+++ b/solution.py
@@ -39,6 +39,12 @@
 
 def swap(value):
     return along(value, "c", 1)
+
+
+def ring(pieces, axis, sign=1):
+    far = along(pieces[2], axis, 2 * sign)
+    one, three = along(pieces[1], axis, sign), along(pieces[3], axis, 3 * sign)
+    return [pieces[0], one, far, three]
 
 
 def local(kernel, tables, arrays, outs, scratch=(), flops=1_000_000, arrays_in=pltpu.VMEM, semaphores=()):
@@ -414,17 +420,17 @@
     got_tiles = swap(give)
     held, ids = [None] * snaps, [None] * snaps
     part = [local(functools.partial(cut_tiles, core), codes, (own_tiles, got_tiles), [piece] * 4) for core in range(2)]
-    ring = [part[0][0]] + [along(part[0][s], Z, s) for s in range(1, 4)]
+    tiles_ring = ring(part[0], Z)
     near = [along(half0, Z, 1), along(half1, Z, -1)]
     far = [swap(v) for v in near]
     cut_cot = local(cut_rows, (here,), (own_cot, got_tiles), [pair] * 4)
 
-    def join(core, ring):
+    def join(core, came):
         held[core], held[2 + core], ids[core], ids[2 + core] = local(
-            join_tiles, (here,), ring, [(2, 2 * rows, tile)] * 2 + [8, 8]
+            join_tiles, (here,), came, [(2, 2 * rows, tile)] * 2 + [8, 8]
         )
 
-    join(0, ring)
+    join(0, tiles_ring)
     work = [(2, tile, width), (8, rows, width)]
     stored, states = [], []
     state = lines = None
@@ -438,26 +444,24 @@
                 work,
             )
         else:
-            ring = [state] + [along(state, Z, s) for s in range(1, 4)]
-            (packed,) = local(pack_ring, (here,), ring, [(4, *flat)])
-            to_y = local(spread_next, (here, ids[t]), [held[t], rel_emb] + ring + [swap(packed)], [flat] * 4, work)
-        came_y = [to_y[0]] + [along(to_y[s], "y", s) for s in range(1, 4)]
+            came_z = ring([state] * 4, Z)
+            (packed,) = local(pack_ring, (here,), came_z, [(4, *flat)])
+            to_y = local(spread_next, (here, ids[t]), [held[t], rel_emb] + came_z + [swap(packed)], [flat] * 4, work)
+        came_y = ring(to_y, "y")
         if t == 0:
             lines = came_y
-            late = [along(part[1][s], Z, s) for s in range(1, 4)]
-            join(1, [part[1][0]] + late)
+            join(1, ring(part[1], Z))
         update, self_part = local(gates, (here,), (state, w_self, w_gate, bias_row), [flat] * 2)
         terms = came_y + [state, update, self_part, w_neigh]
         if t == 1:
-            ring = [cut_cot[0]] + [along(cut_cot[s], Z, s) for s in range(1, 4)]
-            cots = local(join_rows, (here,), ring, [pair] * 4, [(4, 2, rows, width)])
+            cots = local(join_rows, (here,), ring(cut_cot, Z), [pair] * 4, [(4, 2, rows, width)])
         new, agg, candidate = local(advance, (here,), terms, [flat] * 3)
         stored.append((state, agg, update, candidate))
         states.append(new)
         state = new
 
     cut = local(cut_states, (here,), states, [pair] * 4, [(4, 2, rows, width)])
-    cut = [cut[0]] + [along(cut[s], Z, s) for s in range(1, 4)]
+    cut = ring(cut, Z)
 
     d_prev = d_in = None
     pres, gates_in, rel_lines = [None] * snaps, [None] * snaps, []
@@ -472,7 +476,7 @@
         pres[t], gates_in[t] = d_pre, d_gate
         if t == 0:
             break
-        pieces = [d_agg] + [along(d_agg, "y", -s) for s in range(1, 4)]
+        pieces = ring([d_agg] * 4, "y", -1)
         (d_prev,) = local(before, (here,), (d_keep, d_pre, d_gate, w_self, w_gate), [flat])
         second = t == snaps - 2
         other, mine_rows, rel_rows, *mine_states = local(
@@ -501,7 +505,7 @@
                 flops=20_000_000_000,
             )
         parts = local(add_pairs, (here,), (mine_rows, got), [pair] * 4)
-        d_in = [parts[0]] + [along(parts[s], Z, s) for s in range(1, 4)]
+        d_in = ring(parts, Z)
 
     parts = 16
     chunk = 2 * width // parts
@@ -511,7 +515,8 @@
     )
     plane = ("zh", "zl", "y")
     summed = jnp.sum(lax.all_to_all(keep + swap(give), plane, 0, 0, tiled=True), axis=0)
-    summed = (summed + along(summed, "b", 2)) + (along(summed, "b", 1) + along(summed, "b", 3))
+    came_x = ring([summed] * 4, "b")
+    summed = (came_x[0] + came_x[2]) + (came_x[1] + came_x[3])
     mine_sum = lax.all_to_all(jnp.broadcast_to(summed[None], size), plane, 0, 0, tiled=True)
     other_sum = swap(mine_sum)
     halves = (jnp.where(c == 0, mine_sum, other_sum), jnp.where(c == 0, other_sum, mine_sum))

time: 270 us -> 270 us (level)
  no operation moved by 1% of the time
where the time goes in v3:
time: 270 us
  waiting for transfers between devices  101 us (37%)
  starting transfers between devices  93.7 us (35%)
  Pallas kernels  40.5 us (15%)
  blocking collectives  30.8 us (11%)
    ppermute x67, waiting for transfers between devices, along(): lax.ppermute(value, axis, [(i, (i + steps) % count) for i in range(count)])  101 us
    ppermute x67, starting transfers between devices, along(): lax.ppermute(value, axis, [(i, (i + steps) % count) for i in range(count)])  93.7 us
    pallas_call x39, Pallas kernels, local(): pl.pallas_call(kernel, out_shape=[jax.ShapeDtypeStruct((o,), jnp.int32) i...  40.5 us
    all_to_all x1, blocking collectives, on_device(): lax.all_to_all(keep + swap(give), plane, 0, 0, tiled=True)  17.3 us
    all_to_all x1, blocking collectives, on_device(): lax.all_to_all(jnp.broadcast_to(summed[None], size), plane, 0, 0, tiled=T...  13.4 us
  transfers between devices with their start and end apart: 67, of which 42 were waited for; matrix products, arithmetic and copies ran while one was open for 0% of the time, Pallas kernels for 6%

profile of v3, /device:TPU:1, one launch (start us, length us, event | category | flops | bytes accessed | tf_op | source)
XLA Modules:
  0.0 270.2 jit_solution(9599096325901663681)
XLA Ops:
  1.4 2.2 shard_map.145
  5.1 2.8 %collective-permute-done.got = f32[4,168,512]{2,1,0:T(8,128)S(1)} collective-permute-done((f32[4,168,512]{2,1,0:T(8,128)S(1)}, f32[4,168,512]{2,1,0:T(8,128)S(1)}, u32[]{:S(2)}, u32[]{:S(2)}) %collective-permute-start) | collective-permute-done | bytes 1376288 | tf_op jit(solution)/shard_map/ppermute | solution.py:37
  10.3 3.3 %collective-permute-start.2 = (f32[136,512]{1,0:T(8,128)S(1)}, f32[136,512]{1,0:T(8,128)S(1)}, u32[]{:S(2)}, u32[]{:S(2)}) collective-permute-start(f32[136,512]{1,0:T(8,128)S(1)} %get-tuple-element.121), channel_id=1, source_target_pairs={{0,64},{4,68},{64,0},{68,4},{1,65},{5,69},{65,1},{69,5},{2,66},{6,... | collective-permute-start | bytes 835592 | tf_op jit(solution)/shard_map/ppermute | solution.py:37
  15.1 1.9 collective-permute-start.11
  17.0 10.9 %collective-permute-done.10.near0 = f32[128,256]{1,0:T(8,128)S(1)} collective-permute-done((f32[128,256]{1,0:T(8,128)S(1)}, f32[128,256]{1,0:T(8,128)S(1)}, u32[]{:S(2)}, u32[]{:S(2)}) %collective-permute-start.10) | collective-permute-done | bytes 131104 | tf_op jit(solution)/shard_map/ppermute | solution.py:37
  34.1 2.6 collective-permute-start.15
  39.4 4.1 %collective-permute-done.15.a2.l2 = f32[136,256]{1,0:T(8,128)S(1)} collective-permute-done((f32[136,256]{1,0:T(8,128)S(1)}, f32[136,256]{1,0:T(8,128)S(1)}, u32[]{:S(2)}, u32[]{:S(2)}) %collective-permute-start.15) | collective-permute-done | bytes 139296 | tf_op jit(solution)/shard_map/ppermute | solution.py:37
  44.3 2.4 collective-permute-start.19
  47.6 2.0 collective-permute-done.19.p3
  49.6 2.5 collective-permute-done.18.p2
  52.1 3.8 %collective-permute-done.17.p1 = f32[128,256]{1,0:T(8,128)S(1)} collective-permute-done((f32[128,256]{1,0:T(8,128)S(1)}, f32[128,256]{1,0:T(8,128)S(1)}, u32[]{:S(2)}, u32[]{:S(2)}) %collective-permute-start.17) | collective-permute-done | bytes 131104 | tf_op jit(solution)/shard_map/ppermute | solution.py:37
  61.2 12.4 %collective-permute-done.4.p1 = f32[136,512]{1,0:T(8,128)S(1)} collective-permute-done((f32[136,512]{1,0:T(8,128)S(1)}, f32[136,512]{1,0:T(8,128)S(1)}, u32[]{:S(2)}, u32[]{:S(2)}) %collective-permute-start.4) | collective-permute-done | bytes 278560 | tf_op jit(solution)/shard_map/ppermute | solution.py:37
  77.2 2.6 collective-permute-start.22
  81.8 3.0 %collective-permute-done.22.a2 = f32[128,256]{1,0:T(8,128)S(1)} collective-permute-done((f32[128,256]{1,0:T(8,128)S(1)}, f32[128,256]{1,0:T(8,128)S(1)}, u32[]{:S(2)}, u32[]{:S(2)}) %collective-permute-start.22) | collective-permute-done | bytes 131104 | tf_op jit(solution)/shard_map/ppermute | solution.py:37
  85.7 3.9 %collective-permute-start.26 = (f32[128,256]{1,0:T(8,128)S(1)}, f32[128,256]{1,0:T(8,128)S(1)}, u32[]{:S(2)}, u32[]{:S(2)}) collective-permute-start(f32[128,256]{1,0:T(8,128)S(1)} %get-tuple-element.156.p0.state.n1.refs_4_), channel_id=1, source_target_pairs={{0,68},{4,0},{64,4},{68,64},{1,69},{5,1},{65,5},{69,65},{2,70},{6,... | collective-permute-start | bytes 393224 | tf_op jit(solution)/shard_map/ppermute | solution.py:37
  90.3 2.3 collective-permute-done.26.p3
  92.5 2.5 collective-permute-done.25.p2
  95.0 3.3 %collective-permute-done.24.p1 = f32[128,256]{1,0:T(8,128)S(1)} collective-permute-done((f32[128,256]{1,0:T(8,128)S(1)}, f32[128,256]{1,0:T(8,128)S(1)}, u32[]{:S(2)}, u32[]{:S(2)}) %collective-permute-start.24) | collective-permute-done | bytes 131104 | tf_op jit(solution)/shard_map/ppermute | solution.py:37
  103.0 2.5 collective-permute-start.28
  109.4 3.7 %collective-permute-done.29.a2 = f32[128,256]{1,0:T(8,128)S(1)} collective-permute-done((f32[128,256]{1,0:T(8,128)S(1)}, f32[128,256]{1,0:T(8,128)S(1)}, u32[]{:S(2)}, u32[]{:S(2)}) %collective-permute-start.29) | collective-permute-done | bytes 131104 | tf_op jit(solution)/shard_map/ppermute | solution.py:37
  115.5 2.3 collective-permute-done.33.p3
  117.9 2.2 collective-permute-done.32.p2
  120.1 3.7 %collective-permute-done.31.p1 = f32[128,256]{1,0:T(8,128)S(1)} collective-permute-done((f32[128,256]{1,0:T(8,128)S(1)}, f32[128,256]{1,0:T(8,128)S(1)}, u32[]{:S(2)}, u32[]{:S(2)}) %collective-permute-start.31) | collective-permute-done | bytes 131104 | tf_op jit(solution)/shard_map/ppermute | solution.py:37
  131.7 2.2 collective-permute-start.36
  135.3 2.5 collective-permute-start.37
  142.6 3.5 %collective-permute-start.39 = (f32[2,64,256]{2,1,0:T(8,128)S(1)}, f32[2,64,256]{2,1,0:T(8,128)S(1)}, u32[]{:S(2)}, u32[]{:S(2)}) collective-permute-start(f32[2,64,256]{2,1,0:T(8,128)S(1)} %get-tuple-element.171.g0), channel_id=1, source_target_pairs={{0,16},{8,24},{16,0},{24,8},{1,17},{9,25},{17,1},{25,9},{2,18},{10... | collective-permute-start | bytes 393224 | tf_op jit(solution)/shard_map/ppermute | solution.py:37
  147.2 3.2 %collective-permute-done.39.g2 = f32[2,64,256]{2,1,0:T(8,128)S(1)} collective-permute-done((f32[2,64,256]{2,1,0:T(8,128)S(1)}, f32[2,64,256]{2,1,0:T(8,128)S(1)}, u32[]{:S(2)}, u32[]{:S(2)}) %collective-permute-start.39) | collective-permute-done | bytes 131104 | tf_op jit(solution)/shard_map/ppermute | solution.py:37
  152.5 2.4 collective-permute-start.41
  158.3 2.0 collective-permute-start.44
  163.9 2.0 collective-permute-done.42.d1
  167.6 2.9 %collective-permute-start.46 = (f32[2,64,256]{2,1,0:T(8,128)S(1)}, f32[2,64,256]{2,1,0:T(8,128)S(1)}, u32[]{:S(2)}, u32[]{:S(2)}) collective-permute-start(f32[2,64,256]{2,1,0:T(8,128)S(1)} %get-tuple-element.183.g0), channel_id=1, source_target_pairs={{0,16},{8,24},{16,0},{24,8},{1,17},{9,25},{17,1},{25,9},{2,18},{10... | collective-permute-start | bytes 393224 | tf_op jit(solution)/shard_map/ppermute | solution.py:37
  174.4 2.5 collective-permute-done.45.g1
  178.4 2.0 collective-permute-start.51
  180.4 1.9 collective-permute-done.51.got
  184.4 3.0 %collective-permute-start.53 = (f32[2,64,256]{2,1,0:T(8,128)S(1)}, f32[2,64,256]{2,1,0:T(8,128)S(1)}, u32[]{:S(2)}, u32[]{:S(2)}) collective-permute-start(f32[2,64,256]{2,1,0:T(8,128)S(1)} %get-tuple-element.195), channel_id=1, source_target_pairs={{0,64},{4,68},{64,0},{68,4},{1,65},{5,69},{65,1},{69,5},{2,66},{6,... | collective-permute-start | bytes 393224 | tf_op jit(solution)/shard_map/ppermute | solution.py:37
  189.7 3.7 %collective-permute-done.53.d2 = f32[2,64,256]{2,1,0:T(8,128)S(1)} collective-permute-done((f32[2,64,256]{2,1,0:T(8,128)S(1)}, f32[2,64,256]{2,1,0:T(8,128)S(1)}, u32[]{:S(2)}, u32[]{:S(2)}) %collective-permute-start.53) | collective-permute-done | bytes 131104 | tf_op jit(solution)/shard_map/ppermute | solution.py:37
  194.8 3.1 %collective-permute-start.56 = (f32[2,64,256]{2,1,0:T(8,128)S(1)}, f32[2,64,256]{2,1,0:T(8,128)S(1)}, u32[]{:S(2)}, u32[]{:S(2)}) collective-permute-start(f32[2,64,256]{2,1,0:T(8,128)S(1)} %get-tuple-element.202.g0), channel_id=1, source_target_pairs={{0,16},{8,24},{16,0},{24,8},{1,17},{9,25},{17,1},{25,9},{2,18},{10... | collective-permute-start | bytes 393224 | tf_op jit(solution)/shard_map/ppermute | solution.py:37
  199.3 3.3 %collective-permute-done.56.g2 = f32[2,64,256]{2,1,0:T(8,128)S(1)} collective-permute-done((f32[2,64,256]{2,1,0:T(8,128)S(1)}, f32[2,64,256]{2,1,0:T(8,128)S(1)}, u32[]{:S(2)}, u32[]{:S(2)}) %collective-permute-start.56) | collective-permute-done | bytes 131104 | tf_op jit(solution)/shard_map/ppermute | solution.py:37
  204.2 2.4 collective-permute-start.58
  209.7 3.1 %collective-permute-start.60 = (f32[2,64,256]{2,1,0:T(8,128)S(1)}, f32[2,64,256]{2,1,0:T(8,128)S(1)}, u32[]{:S(2)}, u32[]{:S(2)}) collective-permute-start(f32[2,64,256]{2,1,0:T(8,128)S(1)} %get-tuple-element.207), channel_id=1, source_target_pairs={{0,64},{4,68},{64,0},{68,4},{1,65},{5,69},{65,1},{69,5},{2,66},{6,... | collective-permute-start | bytes 393224 | tf_op jit(solution)/shard_map/ppermute | solution.py:37
  212.8 2.3 shard_map.182
  215.1 3.7 %collective-permute-done.60.d2 = f32[2,64,256]{2,1,0:T(8,128)S(1)} collective-permute-done((f32[2,64,256]{2,1,0:T(8,128)S(1)}, f32[2,64,256]{2,1,0:T(8,128)S(1)}, u32[]{:S(2)}, u32[]{:S(2)}) %collective-permute-start.60) | collective-permute-done | bytes 131104 | tf_op jit(solution)/shard_map/ppermute | solution.py:37
  220.2 2.2 shard_map.183
  225.6 17.3 %all_to_all.10 = f32[16,40,256]{2,1,0:T(8,128)S(1)} all-to-all(f32[16,40,256]{2,1,0:T(8,128)S(1)} %add.16), channel_id=1, replica_groups=mesh['zh'=2,'c'=2,'y'=4,'zl'=2,'b'=4] {'zh','zl','y'}, dimensions={0} | all-to-all | bytes 1310720 | tf_op jit(solution)/shard_map/all_to_all | solution.py:517
  243.0 2.5 collective-permute-start.65
  247.2 2.8 %collective-permute-done.64 = f32[40,256]{1,0:T(8,128)S(1)} collective-permute-done((f32[40,256]{1,0:T(8,128)S(1)}, f32[40,256]{1,0:T(8,128)S(1)}, u32[]{:S(2)}, u32[]{:S(2)}) %collective-permute-start.64) | collective-permute-done | bytes 40992 | tf_op jit(solution)/shard_map/ppermute | solution.py:37
  250.1 13.4 %all_to_all.11 = f32[16,40,256]{2,1,0:T(8,128)S(1)} all-to-all(f32[16,40,256]{2,1,0:T(8,128)S(1)} %broadcast_in_dim.2), channel_id=1, replica_groups=mesh['zh'=2,'c'=2,'y'=4,'zl'=2,'b'=4] {'zh','zl','y'}, dimensions={0} | all-to-all | bytes 1310720 | tf_op jit(solution)/shard_map/all_to_all | solution.py:520
  263.5 3.6 %collective-permute-start.66 = (f32[16,40,256]{2,1,0:T(8,128)S(1)}, f32[16,40,256]{2,1,0:T(8,128)S(1)}, u32[]{:S(2)}, u32[]{:S(2)}) collective-permute-start(f32[16,40,256]{2,1,0:T(8,128)S(1)} %all_to_all.11), channel_id=1, source_target_pairs={{0,32},{32,0},{1,33},{33,1},{2,34},{34,2},{3,35},{35,3},{4,36},{36... | collective-permute-start | bytes 1966088 | tf_op jit(solution)/shard_map/ppermute | solution.py:37
  (152 shorter events, 92.3 us)
Async XLA Ops:
  8.5 21.1 %collective-permute-start.1 = (f32[136,512]{1,0:T(8,128)S(1)}, f32[136,512]{1,0:T(8,128)S(1)}, u32[]{:S(2)}, u32[]{:S(2)}) collective-permute-start(f32[136,512]{1,0:T(8,128)S(1)} %get-tuple-element.120), channel_id=1, source_target_pairs={{0,4},{4,64},{64,68},{68,0},{1,5},{5,65},{65,69},{69,1},{2,6},{6,6... | collective-permute-start | bytes 835592 | tf_op jit(solution)/shard_map/ppermute | solution.py:37
  10.3 19.3 %collective-permute-start.2 = (f32[136,512]{1,0:T(8,128)S(1)}, f32[136,512]{1,0:T(8,128)S(1)}, u32[]{:S(2)}, u32[]{:S(2)}) collective-permute-start(f32[136,512]{1,0:T(8,128)S(1)} %get-tuple-element.121), channel_id=1, source_target_pairs={{0,64},{4,68},{64,0},{68,4},{1,65},{5,69},{65,1},{69,5},{2,66},{6,... | collective-permute-start | bytes 835592 | tf_op jit(solution)/shard_map/ppermute | solution.py:37
  13.6 16.0 %collective-permute-start.3 = (f32[136,512]{1,0:T(8,128)S(1)}, f32[136,512]{1,0:T(8,128)S(1)}, u32[]{:S(2)}, u32[]{:S(2)}) collective-permute-start(f32[136,512]{1,0:T(8,128)S(1)} %get-tuple-element.122), channel_id=1, source_target_pairs={{0,68},{4,0},{64,4},{68,64},{1,69},{5,1},{65,5},{69,65},{2,70},{6,... | collective-permute-start | bytes 835592 | tf_op jit(solution)/shard_map/ppermute | solution.py:37
  14.4 13.5 %collective-permute-start.10 = (f32[128,256]{1,0:T(8,128)S(1)}, f32[128,256]{1,0:T(8,128)S(1)}, u32[]{:S(2)}, u32[]{:S(2)}) collective-permute-start(f32[128,256]{1,0:T(8,128)S(1)} %get-tuple-element.140), channel_id=1, source_target_pairs={{0,4},{4,64},{64,68},{68,0},{1,5},{5,65},{65,69},{69,1},{2,6},{6,6... | collective-permute-start | bytes 393224 | tf_op jit(solution)/shard_map/ppermute | solution.py:37
  15.1 13.7 %collective-permute-start.11 = (f32[128,256]{1,0:T(8,128)S(1)}, f32[128,256]{1,0:T(8,128)S(1)}, u32[]{:S(2)}, u32[]{:S(2)}) collective-permute-start(f32[128,256]{1,0:T(8,128)S(1)} %get-tuple-element.141), channel_id=1, source_target_pairs={{0,68},{4,0},{64,4},{68,64},{1,69},{5,1},{65,5},{69,65},{2,70},{6,... | collective-permute-start | bytes 393224 | tf_op jit(solution)/shard_map/ppermute | solution.py:37
  32.8 6.6 %collective-permute-start.14 = (f32[136,256]{1,0:T(8,128)S(1)}, f32[136,256]{1,0:T(8,128)S(1)}, u32[]{:S(2)}, u32[]{:S(2)}) collective-permute-start(f32[136,256]{1,0:T(8,128)S(1)} %get-tuple-element.143), channel_id=1, source_target_pairs={{0,8},{8,16},{16,24},{24,0},{1,9},{9,17},{17,25},{25,1},{2,10},{10... | collective-permute-start | bytes 417800 | tf_op jit(solution)/shard_map/ppermute | solution.py:37
  34.1 9.4 %collective-permute-start.15 = (f32[136,256]{1,0:T(8,128)S(1)}, f32[136,256]{1,0:T(8,128)S(1)}, u32[]{:S(2)}, u32[]{:S(2)}) collective-permute-start(f32[136,256]{1,0:T(8,128)S(1)} %get-tuple-element.144), channel_id=1, source_target_pairs={{0,16},{8,24},{16,0},{24,8},{1,17},{9,25},{17,1},{25,9},{2,18},{10... | collective-permute-start | bytes 417800 | tf_op jit(solution)/shard_map/ppermute | solution.py:37
  36.7 6.7 %collective-permute-start.16 = (f32[136,256]{1,0:T(8,128)S(1)}, f32[136,256]{1,0:T(8,128)S(1)}, u32[]{:S(2)}, u32[]{:S(2)}) collective-permute-start(f32[136,256]{1,0:T(8,128)S(1)} %get-tuple-element.145), channel_id=1, source_target_pairs={{0,24},{8,0},{16,8},{24,16},{1,25},{9,1},{17,9},{25,17},{2,26},{10... | collective-permute-start | bytes 417800 | tf_op jit(solution)/shard_map/ppermute | solution.py:37
  44.3 5.4 %collective-permute-start.19 = (f32[128,256]{1,0:T(8,128)S(1)}, f32[128,256]{1,0:T(8,128)S(1)}, u32[]{:S(2)}, u32[]{:S(2)}) collective-permute-start(f32[128,256]{1,0:T(8,128)S(1)} %get-tuple-element.149.p0.state.n0.refs_3_), channel_id=1, source_target_pairs={{0,68},{4,0},{64,4},{68,64},{1,69},{5,1},{65,5},{69,65},{2,70},{6,... | collective-permute-start | bytes 393224 | tf_op jit(solution)/shard_map/ppermute | solution.py:37
  46.7 5.4 %collective-permute-start.18 = (f32[128,256]{1,0:T(8,128)S(1)}, f32[128,256]{1,0:T(8,128)S(1)}, u32[]{:S(2)}, u32[]{:S(2)}) collective-permute-start(f32[128,256]{1,0:T(8,128)S(1)} %get-tuple-element.149.p0.state.n0.refs_3_), channel_id=1, source_target_pairs={{0,64},{4,68},{64,0},{68,4},{1,65},{5,69},{65,1},{69,5},{2,66},{6,... | collective-permute-start | bytes 393224 | tf_op jit(solution)/shard_map/ppermute | solution.py:37
  47.5 8.3 %collective-permute-start.17 = (f32[128,256]{1,0:T(8,128)S(1)}, f32[128,256]{1,0:T(8,128)S(1)}, u32[]{:S(2)}, u32[]{:S(2)}) collective-permute-start(f32[128,256]{1,0:T(8,128)S(1)} %get-tuple-element.149.p0.state.n0.refs_3_), channel_id=1, source_target_pairs={{0,4},{4,64},{64,68},{68,0},{1,5},{5,65},{65,69},{69,1},{2,6},{6,6... | collective-permute-start | bytes 393224 | tf_op jit(solution)/shard_map/ppermute | solution.py:37
  56.4 18.9 %collective-permute-start.20 = (f32[4,128,256]{2,1,0:T(8,128)S(1)}, f32[4,128,256]{2,1,0:T(8,128)S(1)}, u32[]{:S(2)}, u32[]{:S(2)}) collective-permute-start(f32[4,128,256]{2,1,0:T(8,128)S(1)} %shard_map.155), channel_id=1, source_target_pairs={{0,32},{32,0},{1,33},{33,1},{2,34},{34,2},{3,35},{35,3},{4,36},{36... | collective-permute-start | bytes 1572872 | tf_op jit(solution)/shard_map/ppermute | solution.py:37
  58.2 15.4 %collective-permute-start.4 = (f32[136,512]{1,0:T(8,128)S(1)}, f32[136,512]{1,0:T(8,128)S(1)}, u32[]{:S(2)}, u32[]{:S(2)}) collective-permute-start(f32[136,512]{1,0:T(8,128)S(1)} %get-tuple-element.126), channel_id=1, source_target_pairs={{0,4},{4,64},{64,68},{68,0},{1,5},{5,65},{65,69},{69,1},{2,6},{6,6... | collective-permute-start | bytes 835592 | tf_op jit(solution)/shard_map/ppermute | solution.py:37
  58.3 15.4 %collective-permute-start.5 = (f32[136,512]{1,0:T(8,128)S(1)}, f32[136,512]{1,0:T(8,128)S(1)}, u32[]{:S(2)}, u32[]{:S(2)}) collective-permute-start(f32[136,512]{1,0:T(8,128)S(1)} %get-tuple-element.127), channel_id=1, source_target_pairs={{0,64},{4,68},{64,0},{68,4},{1,65},{5,69},{65,1},{69,5},{2,66},{6,... | collective-permute-start | bytes 835592 | tf_op jit(solution)/shard_map/ppermute | solution.py:37
  59.7 14.3 %collective-permute-start.6 = (f32[136,512]{1,0:T(8,128)S(1)}, f32[136,512]{1,0:T(8,128)S(1)}, u32[]{:S(2)}, u32[]{:S(2)}) collective-permute-start(f32[136,512]{1,0:T(8,128)S(1)} %get-tuple-element.128), channel_id=1, source_target_pairs={{0,68},{4,0},{64,4},{68,64},{1,69},{5,1},{65,5},{69,65},{2,70},{6,... | collective-permute-start | bytes 835592 | tf_op jit(solution)/shard_map/ppermute | solution.py:37
  77.2 7.6 %collective-permute-start.22 = (f32[128,256]{1,0:T(8,128)S(1)}, f32[128,256]{1,0:T(8,128)S(1)}, u32[]{:S(2)}, u32[]{:S(2)}) collective-permute-start(f32[128,256]{1,0:T(8,128)S(1)} %get-tuple-element.152), channel_id=1, source_target_pairs={{0,16},{8,24},{16,0},{24,8},{1,17},{9,25},{17,1},{25,9},{2,18},{10... | collective-permute-start | bytes 393224 | tf_op jit(solution)/shard_map/ppermute | solution.py:37
  85.7 6.8 %collective-permute-start.26 = (f32[128,256]{1,0:T(8,128)S(1)}, f32[128,256]{1,0:T(8,128)S(1)}, u32[]{:S(2)}, u32[]{:S(2)}) collective-permute-start(f32[128,256]{1,0:T(8,128)S(1)} %get-tuple-element.156.p0.state.n1.refs_4_), channel_id=1, source_target_pairs={{0,68},{4,0},{64,4},{68,64},{1,69},{5,1},{65,5},{69,65},{2,70},{6,... | collective-permute-start | bytes 393224 | tf_op jit(solution)/shard_map/ppermute | solution.py:37
  89.6 5.4 %collective-permute-start.25 = (f32[128,256]{1,0:T(8,128)S(1)}, f32[128,256]{1,0:T(8,128)S(1)}, u32[]{:S(2)}, u32[]{:S(2)}) collective-permute-start(f32[128,256]{1,0:T(8,128)S(1)} %get-tuple-element.156.p0.state.n1.refs_4_), channel_id=1, source_target_pairs={{0,64},{4,68},{64,0},{68,4},{1,65},{5,69},{65,1},{69,5},{2,66},{6,... | collective-permute-start | bytes 393224 | tf_op jit(solution)/shard_map/ppermute | solution.py:37
  89.6 8.7 %collective-permute-start.24 = (f32[128,256]{1,0:T(8,128)S(1)}, f32[128,256]{1,0:T(8,128)S(1)}, u32[]{:S(2)}, u32[]{:S(2)}) collective-permute-start(f32[128,256]{1,0:T(8,128)S(1)} %get-tuple-element.156.p0.state.n1.refs_4_), channel_id=1, source_target_pairs={{0,4},{4,64},{64,68},{68,0},{1,5},{5,65},{65,69},{69,1},{2,6},{6,6... | collective-permute-start | bytes 393224 | tf_op jit(solution)/shard_map/ppermute | solution.py:37
  103.0 6.4 %collective-permute-start.28 = (f32[128,256]{1,0:T(8,128)S(1)}, f32[128,256]{1,0:T(8,128)S(1)}, u32[]{:S(2)}, u32[]{:S(2)}) collective-permute-start(f32[128,256]{1,0:T(8,128)S(1)} %get-tuple-element.158), channel_id=1, source_target_pairs={{0,8},{8,16},{16,24},{24,0},{1,9},{9,17},{17,25},{25,1},{2,10},{10... | collective-permute-start | bytes 393224 | tf_op jit(solution)/shard_map/ppermute | solution.py:37
  105.4 7.7 %collective-permute-start.29 = (f32[128,256]{1,0:T(8,128)S(1)}, f32[128,256]{1,0:T(8,128)S(1)}, u32[]{:S(2)}, u32[]{:S(2)}) collective-permute-start(f32[128,256]{1,0:T(8,128)S(1)} %get-tuple-element.159), channel_id=1, source_target_pairs={{0,16},{8,24},{16,0},{24,8},{1,17},{9,25},{17,1},{25,9},{2,18},{10... | collective-permute-start | bytes 393224 | tf_op jit(solution)/shard_map/ppermute | solution.py:37
  107.2 6.0 %collective-permute-start.30 = (f32[128,256]{1,0:T(8,128)S(1)}, f32[128,256]{1,0:T(8,128)S(1)}, u32[]{:S(2)}, u32[]{:S(2)}) collective-permute-start(f32[128,256]{1,0:T(8,128)S(1)} %get-tuple-element.160), channel_id=1, source_target_pairs={{0,24},{8,0},{16,8},{24,16},{1,25},{9,1},{17,9},{25,17},{2,26},{10... | collective-permute-start | bytes 393224 | tf_op jit(solution)/shard_map/ppermute | solution.py:37
  114.7 5.4 %collective-permute-start.32 = (f32[128,256]{1,0:T(8,128)S(1)}, f32[128,256]{1,0:T(8,128)S(1)}, u32[]{:S(2)}, u32[]{:S(2)}) collective-permute-start(f32[128,256]{1,0:T(8,128)S(1)} %get-tuple-element.163.state.p0.n2.refs_5_), channel_id=1, source_target_pairs={{0,64},{4,68},{64,0},{68,4},{1,65},{5,69},{65,1},{69,5},{2,66},{6,... | collective-permute-start | bytes 393224 | tf_op jit(solution)/shard_map/ppermute | solution.py:37
  114.7 9.1 %collective-permute-start.31 = (f32[128,256]{1,0:T(8,128)S(1)}, f32[128,256]{1,0:T(8,128)S(1)}, u32[]{:S(2)}, u32[]{:S(2)}) collective-permute-start(f32[128,256]{1,0:T(8,128)S(1)} %get-tuple-element.163.state.p0.n2.refs_5_), channel_id=1, source_target_pairs={{0,4},{4,64},{64,68},{68,0},{1,5},{5,65},{65,69},{69,1},{2,6},{6,6... | collective-permute-start | bytes 393224 | tf_op jit(solution)/shard_map/ppermute | solution.py:37
  126.1 9.1 %collective-permute-start.7 = (f32[2,64,256]{2,1,0:T(8,128)S(1)}, f32[2,64,256]{2,1,0:T(8,128)S(1)}, u32[]{:S(2)}, u32[]{:S(2)}) collective-permute-start(f32[2,64,256]{2,1,0:T(8,128)S(1)} %get-tuple-element.132), channel_id=1, source_target_pairs={{0,4},{4,64},{64,68},{68,0},{1,5},{5,65},{65,69},{69,1},{2,6},{6,6... | collective-permute-start | bytes 393224 | tf_op jit(solution)/shard_map/ppermute | solution.py:37
  126.2 11.6 %collective-permute-start.8 = (f32[2,64,256]{2,1,0:T(8,128)S(1)}, f32[2,64,256]{2,1,0:T(8,128)S(1)}, u32[]{:S(2)}, u32[]{:S(2)}) collective-permute-start(f32[2,64,256]{2,1,0:T(8,128)S(1)} %get-tuple-element.133), channel_id=1, source_target_pairs={{0,64},{4,68},{64,0},{68,4},{1,65},{5,69},{65,1},{69,5},{2,66},{6,... | collective-permute-start | bytes 393224 | tf_op jit(solution)/shard_map/ppermute | solution.py:37
  127.7 10.1 %collective-permute-start.9 = (f32[2,64,256]{2,1,0:T(8,128)S(1)}, f32[2,64,256]{2,1,0:T(8,128)S(1)}, u32[]{:S(2)}, u32[]{:S(2)}) collective-permute-start(f32[2,64,256]{2,1,0:T(8,128)S(1)} %get-tuple-element.134), channel_id=1, source_target_pairs={{0,68},{4,0},{64,4},{68,64},{1,69},{5,1},{65,5},{69,65},{2,70},{6,... | collective-permute-start | bytes 393224 | tf_op jit(solution)/shard_map/ppermute | solution.py:37
  130.2 9.1 %collective-permute-start.35 = (f32[128,256]{1,0:T(8,128)S(1)}, f32[128,256]{1,0:T(8,128)S(1)}, u32[]{:S(2)}, u32[]{:S(2)}) collective-permute-start(f32[128,256]{1,0:T(8,128)S(1)} %get-tuple-element.166), channel_id=1, source_target_pairs={{0,8},{8,16},{16,24},{24,0},{1,9},{9,17},{17,25},{25,1},{2,10},{10... | collective-permute-start | bytes 393224 | tf_op jit(solution)/shard_map/ppermute | solution.py:37
  131.7 8.1 %collective-permute-start.36 = (f32[128,256]{1,0:T(8,128)S(1)}, f32[128,256]{1,0:T(8,128)S(1)}, u32[]{:S(2)}, u32[]{:S(2)}) collective-permute-start(f32[128,256]{1,0:T(8,128)S(1)} %get-tuple-element.167), channel_id=1, source_target_pairs={{0,16},{8,24},{16,0},{24,8},{1,17},{9,25},{17,1},{25,9},{2,18},{10... | collective-permute-start | bytes 393224 | tf_op jit(solution)/shard_map/ppermute | solution.py:37
  141.4 5.8 %collective-permute-start.40 = (f32[2,64,256]{2,1,0:T(8,128)S(1)}, f32[2,64,256]{2,1,0:T(8,128)S(1)}, u32[]{:S(2)}, u32[]{:S(2)}) collective-permute-start(f32[2,64,256]{2,1,0:T(8,128)S(1)} %get-tuple-element.171.g0), channel_id=1, source_target_pairs={{0,8},{8,16},{16,24},{24,0},{1,9},{9,17},{17,25},{25,1},{2,10},{10... | collective-permute-start | bytes 393224 | tf_op jit(solution)/shard_map/ppermute | solution.py:37
  142.6 7.8 %collective-permute-start.39 = (f32[2,64,256]{2,1,0:T(8,128)S(1)}, f32[2,64,256]{2,1,0:T(8,128)S(1)}, u32[]{:S(2)}, u32[]{:S(2)}) collective-permute-start(f32[2,64,256]{2,1,0:T(8,128)S(1)} %get-tuple-element.171.g0), channel_id=1, source_target_pairs={{0,16},{8,24},{16,0},{24,8},{1,17},{9,25},{17,1},{25,9},{2,18},{10... | collective-permute-start | bytes 393224 | tf_op jit(solution)/shard_map/ppermute | solution.py:37
  157.1 8.8 %collective-permute-start.42 = (f32[2,64,256]{2,1,0:T(8,128)S(1)}, f32[2,64,256]{2,1,0:T(8,128)S(1)}, u32[]{:S(2)}, u32[]{:S(2)}) collective-permute-start(f32[2,64,256]{2,1,0:T(8,128)S(1)} %get-tuple-element.175), channel_id=1, source_target_pairs={{0,4},{4,64},{64,68},{68,0},{1,5},{5,65},{65,69},{69,1},{2,6},{6,6... | collective-permute-start | bytes 393224 | tf_op jit(solution)/shard_map/ppermute | solution.py:37
  157.1 8.8 %collective-permute-start.43 = (f32[2,64,256]{2,1,0:T(8,128)S(1)}, f32[2,64,256]{2,1,0:T(8,128)S(1)}, u32[]{:S(2)}, u32[]{:S(2)}) collective-permute-start(f32[2,64,256]{2,1,0:T(8,128)S(1)} %get-tuple-element.176), channel_id=1, source_target_pairs={{0,64},{4,68},{64,0},{68,4},{1,65},{5,69},{65,1},{69,5},{2,66},{6,... | collective-permute-start | bytes 393224 | tf_op jit(solution)/shard_map/ppermute | solution.py:37
  158.3 8.3 %collective-permute-start.44 = (f32[2,64,256]{2,1,0:T(8,128)S(1)}, f32[2,64,256]{2,1,0:T(8,128)S(1)}, u32[]{:S(2)}, u32[]{:S(2)}) collective-permute-start(f32[2,64,256]{2,1,0:T(8,128)S(1)} %get-tuple-element.177), channel_id=1, source_target_pairs={{0,68},{4,0},{64,4},{68,64},{1,69},{5,1},{65,5},{69,65},{2,70},{6,... | collective-permute-start | bytes 393224 | tf_op jit(solution)/shard_map/ppermute | solution.py:37
  160.9 10.6 %collective-permute-start.48 = (f32[2,64,256]{2,1,0:T(8,128)S(1)}, f32[2,64,256]{2,1,0:T(8,128)S(1)}, u32[]{:S(2)}, u32[]{:S(2)}) collective-permute-start(f32[2,64,256]{2,1,0:T(8,128)S(1)} %get-tuple-element.186), channel_id=1, source_target_pairs={{0,4},{4,64},{64,68},{68,0},{1,5},{5,65},{65,69},{69,1},{2,6},{6,6... | collective-permute-start | bytes 393224 | tf_op jit(solution)/shard_map/ppermute | solution.py:37
  161.1 12.2 %collective-permute-start.49 = (f32[2,64,256]{2,1,0:T(8,128)S(1)}, f32[2,64,256]{2,1,0:T(8,128)S(1)}, u32[]{:S(2)}, u32[]{:S(2)}) collective-permute-start(f32[2,64,256]{2,1,0:T(8,128)S(1)} %get-tuple-element.187), channel_id=1, source_target_pairs={{0,64},{4,68},{64,0},{68,4},{1,65},{5,69},{65,1},{69,5},{2,66},{6,... | collective-permute-start | bytes 393224 | tf_op jit(solution)/shard_map/ppermute | solution.py:37
  165.9 7.4 %collective-permute-start.50 = (f32[2,64,256]{2,1,0:T(8,128)S(1)}, f32[2,64,256]{2,1,0:T(8,128)S(1)}, u32[]{:S(2)}, u32[]{:S(2)}) collective-permute-start(f32[2,64,256]{2,1,0:T(8,128)S(1)} %get-tuple-element.188), channel_id=1, source_target_pairs={{0,68},{4,0},{64,4},{68,64},{1,69},{5,1},{65,5},{69,65},{2,70},{6,... | collective-permute-start | bytes 393224 | tf_op jit(solution)/shard_map/ppermute | solution.py:37
  167.5 5.8 %collective-permute-start.47 = (f32[2,64,256]{2,1,0:T(8,128)S(1)}, f32[2,64,256]{2,1,0:T(8,128)S(1)}, u32[]{:S(2)}, u32[]{:S(2)}) collective-permute-start(f32[2,64,256]{2,1,0:T(8,128)S(1)} %get-tuple-element.183.g0), channel_id=1, source_target_pairs={{0,8},{8,16},{16,24},{24,0},{1,9},{9,17},{17,25},{25,1},{2,10},{10... | collective-permute-start | bytes 393224 | tf_op jit(solution)/shard_map/ppermute | solution.py:37
  167.6 6.8 %collective-permute-start.46 = (f32[2,64,256]{2,1,0:T(8,128)S(1)}, f32[2,64,256]{2,1,0:T(8,128)S(1)}, u32[]{:S(2)}, u32[]{:S(2)}) collective-permute-start(f32[2,64,256]{2,1,0:T(8,128)S(1)} %get-tuple-element.183.g0), channel_id=1, source_target_pairs={{0,16},{8,24},{16,0},{24,8},{1,17},{9,25},{17,1},{25,9},{2,18},{10... | collective-permute-start | bytes 393224 | tf_op jit(solution)/shard_map/ppermute | solution.py:37
  171.5 5.4 %collective-permute-start.45 = (f32[2,64,256]{2,1,0:T(8,128)S(1)}, f32[2,64,256]{2,1,0:T(8,128)S(1)}, u32[]{:S(2)}, u32[]{:S(2)}) collective-permute-start(f32[2,64,256]{2,1,0:T(8,128)S(1)} %get-tuple-element.183.g0), channel_id=1, source_target_pairs={{0,24},{8,0},{16,8},{24,16},{1,25},{9,1},{17,9},{25,17},{2,26},{10... | collective-permute-start | bytes 393224 | tf_op jit(solution)/shard_map/ppermute | solution.py:37
  182.9 6.8 %collective-permute-start.52 = (f32[2,64,256]{2,1,0:T(8,128)S(1)}, f32[2,64,256]{2,1,0:T(8,128)S(1)}, u32[]{:S(2)}, u32[]{:S(2)}) collective-permute-start(f32[2,64,256]{2,1,0:T(8,128)S(1)} %get-tuple-element.194), channel_id=1, source_target_pairs={{0,4},{4,64},{64,68},{68,0},{1,5},{5,65},{65,69},{69,1},{2,6},{6,6... | collective-permute-start | bytes 393224 | tf_op jit(solution)/shard_map/ppermute | solution.py:37
  184.4 9.0 %collective-permute-start.53 = (f32[2,64,256]{2,1,0:T(8,128)S(1)}, f32[2,64,256]{2,1,0:T(8,128)S(1)}, u32[]{:S(2)}, u32[]{:S(2)}) collective-permute-start(f32[2,64,256]{2,1,0:T(8,128)S(1)} %get-tuple-element.195), channel_id=1, source_target_pairs={{0,64},{4,68},{64,0},{68,4},{1,65},{5,69},{65,1},{69,5},{2,66},{6,... | collective-permute-start | bytes 393224 | tf_op jit(solution)/shard_map/ppermute | solution.py:37
  187.4 6.0 %collective-permute-start.54 = (f32[2,64,256]{2,1,0:T(8,128)S(1)}, f32[2,64,256]{2,1,0:T(8,128)S(1)}, u32[]{:S(2)}, u32[]{:S(2)}) collective-permute-start(f32[2,64,256]{2,1,0:T(8,128)S(1)} %get-tuple-element.196), channel_id=1, source_target_pairs={{0,68},{4,0},{64,4},{68,64},{1,69},{5,1},{65,5},{69,65},{2,70},{6,... | collective-permute-start | bytes 393224 | tf_op jit(solution)/shard_map/ppermute | solution.py:37
  194.8 7.9 %collective-permute-start.56 = (f32[2,64,256]{2,1,0:T(8,128)S(1)}, f32[2,64,256]{2,1,0:T(8,128)S(1)}, u32[]{:S(2)}, u32[]{:S(2)}) collective-permute-start(f32[2,64,256]{2,1,0:T(8,128)S(1)} %get-tuple-element.202.g0), channel_id=1, source_target_pairs={{0,16},{8,24},{16,0},{24,8},{1,17},{9,25},{17,1},{25,9},{2,18},{10... | collective-permute-start | bytes 393224 | tf_op jit(solution)/shard_map/ppermute | solution.py:37
  208.8 6.3 %collective-permute-start.59 = (f32[2,64,256]{2,1,0:T(8,128)S(1)}, f32[2,64,256]{2,1,0:T(8,128)S(1)}, u32[]{:S(2)}, u32[]{:S(2)}) collective-permute-start(f32[2,64,256]{2,1,0:T(8,128)S(1)} %get-tuple-element.206), channel_id=1, source_target_pairs={{0,4},{4,64},{64,68},{68,0},{1,5},{5,65},{65,69},{69,1},{2,6},{6,6... | collective-permute-start | bytes 393224 | tf_op jit(solution)/shard_map/ppermute | solution.py:37
  209.7 9.2 %collective-permute-start.60 = (f32[2,64,256]{2,1,0:T(8,128)S(1)}, f32[2,64,256]{2,1,0:T(8,128)S(1)}, u32[]{:S(2)}, u32[]{:S(2)}) collective-permute-start(f32[2,64,256]{2,1,0:T(8,128)S(1)} %get-tuple-element.207), channel_id=1, source_target_pairs={{0,64},{4,68},{64,0},{68,4},{1,65},{5,69},{65,1},{69,5},{2,66},{6,... | collective-permute-start | bytes 393224 | tf_op jit(solution)/shard_map/ppermute | solution.py:37
  212.8 6.0 %collective-permute-start.61 = (f32[2,64,256]{2,1,0:T(8,128)S(1)}, f32[2,64,256]{2,1,0:T(8,128)S(1)}, u32[]{:S(2)}, u32[]{:S(2)}) collective-permute-start(f32[2,64,256]{2,1,0:T(8,128)S(1)} %get-tuple-element.208), channel_id=1, source_target_pairs={{0,68},{4,0},{64,4},{68,64},{1,69},{5,1},{65,5},{69,65},{2,70},{6,... | collective-permute-start | bytes 393224 | tf_op jit(solution)/shard_map/ppermute | solution.py:37
  263.5 5.6 %collective-permute-start.66 = (f32[16,40,256]{2,1,0:T(8,128)S(1)}, f32[16,40,256]{2,1,0:T(8,128)S(1)}, u32[]{:S(2)}, u32[]{:S(2)}) collective-permute-start(f32[16,40,256]{2,1,0:T(8,128)S(1)} %all_to_all.11), channel_id=1, source_target_pairs={{0,32},{32,0},{1,33},{33,1},{2,34},{34,2},{3,35},{35,3},{4,36},{36... | collective-permute-start | bytes 1966088 | tf_op jit(solution)/shard_map/ppermute | solution.py:37
  (27 other events, 190.6 us)

commit v4 on v3

--- a/solution.py
+++ b/solution.py
@@ -246,7 +246,7 @@
         d_keep[...] = d_new * rest
 
 
-def retreat_last(place, cot, state, update, candidate, w_neigh, d_pre, d_gate, d_agg, d_keep):
+def retreat_last(cot, state, update, candidate, w_neigh, d_pre, d_gate, d_agg, d_keep):
     d_new = cot[...].reshape(state.shape)
     retreat_math(d_new, state, update, candidate, w_neigh, d_pre, d_gate, d_agg, d_keep)
 
@@ -254,6 +254,11 @@
 def retreat(place, d0, d1, d2, d3, d_prev, cot, state, update, candidate, w_neigh, d_pre, d_gate, d_agg, d_keep):
     came = ((d0[0:2] + d1[0:2]) + (d2[0:2] + d3[0:2]) + cot[...]).reshape(state.shape)
     retreat_math(came + d_prev[...], state, update, candidate, w_neigh, d_pre, d_gate, d_agg, d_keep)
+
+
+def turn(place, a0, a1, a2, a3, state, update, self_part, w_neigh, cot, new, agg, cand, d_pre, d_gate, d_agg, d_keep):
+    advance(place, a0, a1, a2, a3, state, update, self_part, w_neigh, new, agg, cand)
+    retreat_last(cot, state, update, cand, w_neigh, d_pre, d_gate, d_agg, d_keep)
 
 
 def before(place, d_keep, d_pre, d_gate, w_self, w_gate, d_prev):
@@ -392,6 +397,12 @@
             out[i * parts // 2 : (i + 1) * parts // 2, 0:chunk, :] = value.reshape(parts // 2, chunk, width)
         out[:, chunk:, :] = jnp.zeros((parts, out.shape[1] - chunk, width), F32)
         out[0, chunk : chunk + 1, :] = bias
+
+
+def finish(place, *refs):
+    ins, (agg, *lines_later), (keep, give), kept = refs[:10], refs[10:20], refs[20:22], refs[22:]
+    retreat(place, *ins, *kept)
+    weight_grads(place, ins[6], agg, *kept[:3], *lines_later, keep, give)
 
 
 def on_device(
@@ -455,7 +466,10 @@
         terms = came_y + [state, update, self_part, w_neigh]
         if t == 1:
             cots = local(join_rows, (here,), ring(cut_cot, Z), [pair] * 4, [(4, 2, rows, width)])
-        new, agg, candidate = local(advance, (here,), terms, [flat] * 3)
+        if t + 1 < snaps:
+            new, agg, candidate = local(advance, (here,), terms, [flat] * 3)
+        else:
+            new, agg, candidate, *turned = local(turn, (here,), terms + [cots[t]], [flat] * 5 + [pair, flat])
         stored.append((state, agg, update, candidate))
         states.append(new)
         state = new
@@ -469,13 +483,13 @@
         held_state, agg, update, candidate = stored[t]
         tail = (cots[t], held_state, update, candidate, w_neigh)
         outs = [flat, flat, pair, flat]
+        if t == 0:
+            break
         if d_in is None:
-            d_pre, d_gate, d_agg, d_keep = local(retreat_last, (here,), tail, outs)
+            d_pre, d_gate, d_agg, d_keep = turned
         else:
             d_pre, d_gate, d_agg, d_keep = local(retreat, (here,), (*d_in, d_prev, *tail), outs)
         pres[t], gates_in[t] = d_pre, d_gate
-        if t == 0:
-            break
         pieces = ring([d_agg] * 4, "y", -1)
         (d_prev,) = local(before, (here,), (d_keep, d_pre, d_gate, w_self, w_gate), [flat])
         second = t == snaps - 2
@@ -511,7 +525,7 @@
     chunk = 2 * width // parts
     size = (parts, chunk + 8, width)
     keep, give = local(
-        weight_grads, (here,), (stored[0][0], stored[0][1], d_pre, d_gate, d_agg, *lines, *later), [size] * 2
+        finish, (here,), (*d_in, d_prev, *tail, stored[0][1], *lines, *later), [size] * 2, [flat, flat, pair, flat]
     )
     plane = ("zh", "zl", "y")
     summed = jnp.sum(lax.all_to_all(keep + swap(give), plane, 0, 0, tiled=True), axis=0)

time: 270 us -> 269 us (level)
    pallas_call x39 -> x37, Pallas kernels: 40.5 us -> 39.3 us  [local(): pl.pallas_call(kernel, out_shape=[jax.ShapeDtypeStruct((o,), jnp.int32) i...]
where the time goes in v4:
time: 269 us
  waiting for transfers between devices  102 us (38%)
  starting transfers between devices  93.3 us (35%)
  Pallas kernels  39.3 us (15%)
  blocking collectives  30.9 us (11%)
    ppermute x67, waiting for transfers between devices, along(): lax.ppermute(value, axis, [(i, (i + steps) % count) for i in range(count)])  102 us
    ppermute x67, starting transfers between devices, along(): lax.ppermute(value, axis, [(i, (i + steps) % count) for i in range(count)])  93.3 us
    pallas_call x37, Pallas kernels, local(): pl.pallas_call(kernel, out_shape=[jax.ShapeDtypeStruct((o,), jnp.int32) i...  39.3 us
    all_to_all x1, blocking collectives, on_device(): lax.all_to_all(keep + swap(give), plane, 0, 0, tiled=True)  17.5 us
    all_to_all x1, blocking collectives, on_device(): lax.all_to_all(jnp.broadcast_to(summed[None], size), plane, 0, 0, tiled=T...  13.4 us
  transfers between devices with their start and end apart: 67, of which 42 were waited for; matrix products, arithmetic and copies ran while one was open for 0% of the time, Pallas kernels for 6%

profile of v4, /device:TPU:1, one launch (start us, length us, event | category | flops | bytes accessed | tf_op | source)
XLA Modules:
  0.0 268.9 jit_solution(2706601273658575618)
XLA Ops:
  1.4 2.2 shard_map.145
  5.1 2.8 %collective-permute-done.got = f32[4,168,512]{2,1,0:T(8,128)S(1)} collective-permute-done((f32[4,168,512]{2,1,0:T(8,128)S(1)}, f32[4,168,512]{2,1,0:T(8,128)S(1)}, u32[]{:S(2)}, u32[]{:S(2)}) %collective-permute-start) | collective-permute-done | bytes 1376288 | tf_op jit(solution)/shard_map/ppermute | solution.py:37
  10.3 3.3 %collective-permute-start.2 = (f32[136,512]{1,0:T(8,128)S(1)}, f32[136,512]{1,0:T(8,128)S(1)}, u32[]{:S(2)}, u32[]{:S(2)}) collective-permute-start(f32[136,512]{1,0:T(8,128)S(1)} %get-tuple-element.117), channel_id=1, source_target_pairs={{0,64},{4,68},{64,0},{68,4},{1,65},{5,69},{65,1},{69,5},{2,66},{6,... | collective-permute-start | bytes 835592 | tf_op jit(solution)/shard_map/ppermute | solution.py:37
  15.1 1.9 collective-permute-start.8
  17.0 10.9 %collective-permute-done.7.near0 = f32[128,256]{1,0:T(8,128)S(1)} collective-permute-done((f32[128,256]{1,0:T(8,128)S(1)}, f32[128,256]{1,0:T(8,128)S(1)}, u32[]{:S(2)}, u32[]{:S(2)}) %collective-permute-start.7) | collective-permute-done | bytes 131104 | tf_op jit(solution)/shard_map/ppermute | solution.py:37
  34.1 2.6 collective-permute-start.12
  39.4 4.1 %collective-permute-done.12.a2.refs_13_ = f32[136,256]{1,0:T(8,128)S(1)} collective-permute-done((f32[136,256]{1,0:T(8,128)S(1)}, f32[136,256]{1,0:T(8,128)S(1)}, u32[]{:S(2)}, u32[]{:S(2)}) %collective-permute-start.12) | collective-permute-done | bytes 139296 | tf_op jit(solution)/shard_map/ppermute | solution.py:37
  44.3 2.4 collective-permute-start.16
  47.6 2.0 collective-permute-done.16.p3
  49.6 2.5 collective-permute-done.15.p2
  52.1 3.8 %collective-permute-done.14.p1 = f32[128,256]{1,0:T(8,128)S(1)} collective-permute-done((f32[128,256]{1,0:T(8,128)S(1)}, f32[128,256]{1,0:T(8,128)S(1)}, u32[]{:S(2)}, u32[]{:S(2)}) %collective-permute-start.14) | collective-permute-done | bytes 131104 | tf_op jit(solution)/shard_map/ppermute | solution.py:37
  61.2 12.4 %collective-permute-done.4.p1 = f32[136,512]{1,0:T(8,128)S(1)} collective-permute-done((f32[136,512]{1,0:T(8,128)S(1)}, f32[136,512]{1,0:T(8,128)S(1)}, u32[]{:S(2)}, u32[]{:S(2)}) %collective-permute-start.4) | collective-permute-done | bytes 278560 | tf_op jit(solution)/shard_map/ppermute | solution.py:37
  77.2 2.6 collective-permute-start.19
  81.8 3.0 %collective-permute-done.19.a2 = f32[128,256]{1,0:T(8,128)S(1)} collective-permute-done((f32[128,256]{1,0:T(8,128)S(1)}, f32[128,256]{1,0:T(8,128)S(1)}, u32[]{:S(2)}, u32[]{:S(2)}) %collective-permute-start.19) | collective-permute-done | bytes 131104 | tf_op jit(solution)/shard_map/ppermute | solution.py:37
  85.7 3.9 %collective-permute-start.23 = (f32[128,256]{1,0:T(8,128)S(1)}, f32[128,256]{1,0:T(8,128)S(1)}, u32[]{:S(2)}, u32[]{:S(2)}) collective-permute-start(f32[128,256]{1,0:T(8,128)S(1)} %get-tuple-element.147.p0.state.n1.refs_4_), channel_id=1, source_target_pairs={{0,68},{4,0},{64,4},{68,64},{1,69},{5,1},{65,5},{69,65},{2,70},{6,... | collective-permute-start | bytes 393224 | tf_op jit(solution)/shard_map/ppermute | solution.py:37
  90.3 2.2 collective-permute-done.23.p3
  92.5 2.5 collective-permute-done.22.p2
  95.0 3.3 %collective-permute-done.21.p1 = f32[128,256]{1,0:T(8,128)S(1)} collective-permute-done((f32[128,256]{1,0:T(8,128)S(1)}, f32[128,256]{1,0:T(8,128)S(1)}, u32[]{:S(2)}, u32[]{:S(2)}) %collective-permute-start.21) | collective-permute-done | bytes 131104 | tf_op jit(solution)/shard_map/ppermute | solution.py:37
  103.0 2.5 collective-permute-start.25
  109.4 3.7 %collective-permute-done.26.a2 = f32[128,256]{1,0:T(8,128)S(1)} collective-permute-done((f32[128,256]{1,0:T(8,128)S(1)}, f32[128,256]{1,0:T(8,128)S(1)}, u32[]{:S(2)}, u32[]{:S(2)}) %collective-permute-start.26) | collective-permute-done | bytes 131104 | tf_op jit(solution)/shard_map/ppermute | solution.py:37
  115.5 2.3 collective-permute-done.30.p3
  117.9 2.2 collective-permute-done.29.p2
  120.1 3.7 %collective-permute-done.28.p1 = f32[128,256]{1,0:T(8,128)S(1)} collective-permute-done((f32[128,256]{1,0:T(8,128)S(1)}, f32[128,256]{1,0:T(8,128)S(1)}, u32[]{:S(2)}, u32[]{:S(2)}) %collective-permute-start.28) | collective-permute-done | bytes 131104 | tf_op jit(solution)/shard_map/ppermute | solution.py:37
  131.7 2.2 collective-permute-start.33
  135.3 2.5 collective-permute-start.34
  142.4 3.5 %collective-permute-start.39 = (f32[2,64,256]{2,1,0:T(8,128)S(1)}, f32[2,64,256]{2,1,0:T(8,128)S(1)}, u32[]{:S(2)}, u32[]{:S(2)}) collective-permute-start(f32[2,64,256]{2,1,0:T(8,128)S(1)} %get-tuple-element.166.g0), channel_id=1, source_target_pairs={{0,16},{8,24},{16,0},{24,8},{1,17},{9,25},{17,1},{25,9},{2,18},{10... | collective-permute-start | bytes 393224 | tf_op jit(solution)/shard_map/ppermute | solution.py:37
  147.1 3.2 %collective-permute-done.39.g2 = f32[2,64,256]{2,1,0:T(8,128)S(1)} collective-permute-done((f32[2,64,256]{2,1,0:T(8,128)S(1)}, f32[2,64,256]{2,1,0:T(8,128)S(1)}, u32[]{:S(2)}, u32[]{:S(2)}) %collective-permute-start.39) | collective-permute-done | bytes 131104 | tf_op jit(solution)/shard_map/ppermute | solution.py:37
  152.4 2.3 collective-permute-start.41
  158.2 2.0 collective-permute-start.44
  163.7 2.0 collective-permute-done.42.d1
  167.4 2.7 %collective-permute-start.46 = (f32[2,64,256]{2,1,0:T(8,128)S(1)}, f32[2,64,256]{2,1,0:T(8,128)S(1)}, u32[]{:S(2)}, u32[]{:S(2)}) collective-permute-start(f32[2,64,256]{2,1,0:T(8,128)S(1)} %get-tuple-element.178.g0), channel_id=1, source_target_pairs={{0,16},{8,24},{16,0},{24,8},{1,17},{9,25},{17,1},{25,9},{2,18},{10... | collective-permute-start | bytes 393224 | tf_op jit(solution)/shard_map/ppermute | solution.py:37
  174.0 2.6 collective-permute-done.45.g1
  178.1 2.1 collective-permute-start.51
  180.2 1.9 collective-permute-done.51.got
  184.3 2.9 %collective-permute-start.53 = (f32[2,64,256]{2,1,0:T(8,128)S(1)}, f32[2,64,256]{2,1,0:T(8,128)S(1)}, u32[]{:S(2)}, u32[]{:S(2)}) collective-permute-start(f32[2,64,256]{2,1,0:T(8,128)S(1)} %get-tuple-element.189), channel_id=1, source_target_pairs={{0,64},{4,68},{64,0},{68,4},{1,65},{5,69},{65,1},{69,5},{2,66},{6,... | collective-permute-start | bytes 393224 | tf_op jit(solution)/shard_map/ppermute | solution.py:37
  189.5 3.7 %collective-permute-done.53.d2 = f32[2,64,256]{2,1,0:T(8,128)S(1)} collective-permute-done((f32[2,64,256]{2,1,0:T(8,128)S(1)}, f32[2,64,256]{2,1,0:T(8,128)S(1)}, u32[]{:S(2)}, u32[]{:S(2)}) %collective-permute-start.53) | collective-permute-done | bytes 131104 | tf_op jit(solution)/shard_map/ppermute | solution.py:37
  194.4 3.0 %collective-permute-start.56 = (f32[2,64,256]{2,1,0:T(8,128)S(1)}, f32[2,64,256]{2,1,0:T(8,128)S(1)}, u32[]{:S(2)}, u32[]{:S(2)}) collective-permute-start(f32[2,64,256]{2,1,0:T(8,128)S(1)} %get-tuple-element.196.g0), channel_id=1, source_target_pairs={{0,16},{8,24},{16,0},{24,8},{1,17},{9,25},{17,1},{25,9},{2,18},{10... | collective-permute-start | bytes 393224 | tf_op jit(solution)/shard_map/ppermute | solution.py:37
  199.2 3.2 %collective-permute-done.56.g2 = f32[2,64,256]{2,1,0:T(8,128)S(1)} collective-permute-done((f32[2,64,256]{2,1,0:T(8,128)S(1)}, f32[2,64,256]{2,1,0:T(8,128)S(1)}, u32[]{:S(2)}, u32[]{:S(2)}) %collective-permute-start.56) | collective-permute-done | bytes 131104 | tf_op jit(solution)/shard_map/ppermute | solution.py:37
  203.9 2.4 collective-permute-start.58
  209.5 3.0 %collective-permute-start.60 = (f32[2,64,256]{2,1,0:T(8,128)S(1)}, f32[2,64,256]{2,1,0:T(8,128)S(1)}, u32[]{:S(2)}, u32[]{:S(2)}) collective-permute-start(f32[2,64,256]{2,1,0:T(8,128)S(1)} %get-tuple-element.201), channel_id=1, source_target_pairs={{0,64},{4,68},{64,0},{68,4},{1,65},{5,69},{65,1},{69,5},{2,66},{6,... | collective-permute-start | bytes 393224 | tf_op jit(solution)/shard_map/ppermute | solution.py:37
  212.5 2.3 shard_map.180
  214.8 3.7 %collective-permute-done.60.refs_2_ = f32[2,64,256]{2,1,0:T(8,128)S(1)} collective-permute-done((f32[2,64,256]{2,1,0:T(8,128)S(1)}, f32[2,64,256]{2,1,0:T(8,128)S(1)}, u32[]{:S(2)}, u32[]{:S(2)}) %collective-permute-start.60) | collective-permute-done | bytes 131104 | tf_op jit(solution)/shard_map/ppermute | solution.py:37
  218.5 2.4 shard_map.181
  224.1 17.5 %all_to_all.10 = f32[16,40,256]{2,1,0:T(8,128)S(1)} all-to-all(f32[16,40,256]{2,1,0:T(8,128)S(1)} %add.16), channel_id=1, replica_groups=mesh['zh'=2,'c'=2,'y'=4,'zl'=2,'b'=4] {'zh','zl','y'}, dimensions={0} | all-to-all | bytes 1310720 | tf_op jit(solution)/shard_map/all_to_all | solution.py:531
  241.6 2.6 collective-permute-start.65
  245.9 2.8 %collective-permute-done.64 = f32[40,256]{1,0:T(8,128)S(1)} collective-permute-done((f32[40,256]{1,0:T(8,128)S(1)}, f32[40,256]{1,0:T(8,128)S(1)}, u32[]{:S(2)}, u32[]{:S(2)}) %collective-permute-start.64) | collective-permute-done | bytes 40992 | tf_op jit(solution)/shard_map/ppermute | solution.py:37
  248.8 13.4 %all_to_all.11 = f32[16,40,256]{2,1,0:T(8,128)S(1)} all-to-all(f32[16,40,256]{2,1,0:T(8,128)S(1)} %broadcast_in_dim.2), channel_id=1, replica_groups=mesh['zh'=2,'c'=2,'y'=4,'zl'=2,'b'=4] {'zh','zl','y'}, dimensions={0} | all-to-all | bytes 1310720 | tf_op jit(solution)/shard_map/all_to_all | solution.py:534
  262.2 3.6 %collective-permute-start.66 = (f32[16,40,256]{2,1,0:T(8,128)S(1)}, f32[16,40,256]{2,1,0:T(8,128)S(1)}, u32[]{:S(2)}, u32[]{:S(2)}) collective-permute-start(f32[16,40,256]{2,1,0:T(8,128)S(1)} %all_to_all.11), channel_id=1, source_target_pairs={{0,32},{32,0},{1,33},{33,1},{2,34},{34,2},{3,35},{35,3},{4,36},{36... | collective-permute-start | bytes 1966088 | tf_op jit(solution)/shard_map/ppermute | solution.py:37
  (150 shorter events, 91.1 us)
Async XLA Ops:
  8.5 21.1 %collective-permute-start.1 = (f32[136,512]{1,0:T(8,128)S(1)}, f32[136,512]{1,0:T(8,128)S(1)}, u32[]{:S(2)}, u32[]{:S(2)}) collective-permute-start(f32[136,512]{1,0:T(8,128)S(1)} %get-tuple-element.116), channel_id=1, source_target_pairs={{0,4},{4,64},{64,68},{68,0},{1,5},{5,65},{65,69},{69,1},{2,6},{6,6... | collective-permute-start | bytes 835592 | tf_op jit(solution)/shard_map/ppermute | solution.py:37
  10.3 19.3 %collective-permute-start.2 = (f32[136,512]{1,0:T(8,128)S(1)}, f32[136,512]{1,0:T(8,128)S(1)}, u32[]{:S(2)}, u32[]{:S(2)}) collective-permute-start(f32[136,512]{1,0:T(8,128)S(1)} %get-tuple-element.117), channel_id=1, source_target_pairs={{0,64},{4,68},{64,0},{68,4},{1,65},{5,69},{65,1},{69,5},{2,66},{6,... | collective-permute-start | bytes 835592 | tf_op jit(solution)/shard_map/ppermute | solution.py:37
  13.6 16.0 %collective-permute-start.3 = (f32[136,512]{1,0:T(8,128)S(1)}, f32[136,512]{1,0:T(8,128)S(1)}, u32[]{:S(2)}, u32[]{:S(2)}) collective-permute-start(f32[136,512]{1,0:T(8,128)S(1)} %get-tuple-element.118), channel_id=1, source_target_pairs={{0,68},{4,0},{64,4},{68,64},{1,69},{5,1},{65,5},{69,65},{2,70},{6,... | collective-permute-start | bytes 835592 | tf_op jit(solution)/shard_map/ppermute | solution.py:37
  14.4 13.5 %collective-permute-start.7 = (f32[128,256]{1,0:T(8,128)S(1)}, f32[128,256]{1,0:T(8,128)S(1)}, u32[]{:S(2)}, u32[]{:S(2)}) collective-permute-start(f32[128,256]{1,0:T(8,128)S(1)} %get-tuple-element.131), channel_id=1, source_target_pairs={{0,4},{4,64},{64,68},{68,0},{1,5},{5,65},{65,69},{69,1},{2,6},{6,6... | collective-permute-start | bytes 393224 | tf_op jit(solution)/shard_map/ppermute | solution.py:37
  15.1 13.7 %collective-permute-start.8 = (f32[128,256]{1,0:T(8,128)S(1)}, f32[128,256]{1,0:T(8,128)S(1)}, u32[]{:S(2)}, u32[]{:S(2)}) collective-permute-start(f32[128,256]{1,0:T(8,128)S(1)} %get-tuple-element.132), channel_id=1, source_target_pairs={{0,68},{4,0},{64,4},{68,64},{1,69},{5,1},{65,5},{69,65},{2,70},{6,... | collective-permute-start | bytes 393224 | tf_op jit(solution)/shard_map/ppermute | solution.py:37
  32.8 6.6 %collective-permute-start.11 = (f32[136,256]{1,0:T(8,128)S(1)}, f32[136,256]{1,0:T(8,128)S(1)}, u32[]{:S(2)}, u32[]{:S(2)}) collective-permute-start(f32[136,256]{1,0:T(8,128)S(1)} %get-tuple-element.134), channel_id=1, source_target_pairs={{0,8},{8,16},{16,24},{24,0},{1,9},{9,17},{17,25},{25,1},{2,10},{10... | collective-permute-start | bytes 417800 | tf_op jit(solution)/shard_map/ppermute | solution.py:37
  34.1 9.4 %collective-permute-start.12 = (f32[136,256]{1,0:T(8,128)S(1)}, f32[136,256]{1,0:T(8,128)S(1)}, u32[]{:S(2)}, u32[]{:S(2)}) collective-permute-start(f32[136,256]{1,0:T(8,128)S(1)} %get-tuple-element.135), channel_id=1, source_target_pairs={{0,16},{8,24},{16,0},{24,8},{1,17},{9,25},{17,1},{25,9},{2,18},{10... | collective-permute-start | bytes 417800 | tf_op jit(solution)/shard_map/ppermute | solution.py:37
  36.7 6.7 %collective-permute-start.13 = (f32[136,256]{1,0:T(8,128)S(1)}, f32[136,256]{1,0:T(8,128)S(1)}, u32[]{:S(2)}, u32[]{:S(2)}) collective-permute-start(f32[136,256]{1,0:T(8,128)S(1)} %get-tuple-element.136), channel_id=1, source_target_pairs={{0,24},{8,0},{16,8},{24,16},{1,25},{9,1},{17,9},{25,17},{2,26},{10... | collective-permute-start | bytes 417800 | tf_op jit(solution)/shard_map/ppermute | solution.py:37
  44.3 5.4 %collective-permute-start.16 = (f32[128,256]{1,0:T(8,128)S(1)}, f32[128,256]{1,0:T(8,128)S(1)}, u32[]{:S(2)}, u32[]{:S(2)}) collective-permute-start(f32[128,256]{1,0:T(8,128)S(1)} %get-tuple-element.140.p0.state.n0.refs_3_), channel_id=1, source_target_pairs={{0,68},{4,0},{64,4},{68,64},{1,69},{5,1},{65,5},{69,65},{2,70},{6,... | collective-permute-start | bytes 393224 | tf_op jit(solution)/shard_map/ppermute | solution.py:37
  46.7 5.4 %collective-permute-start.15 = (f32[128,256]{1,0:T(8,128)S(1)}, f32[128,256]{1,0:T(8,128)S(1)}, u32[]{:S(2)}, u32[]{:S(2)}) collective-permute-start(f32[128,256]{1,0:T(8,128)S(1)} %get-tuple-element.140.p0.state.n0.refs_3_), channel_id=1, source_target_pairs={{0,64},{4,68},{64,0},{68,4},{1,65},{5,69},{65,1},{69,5},{2,66},{6,... | collective-permute-start | bytes 393224 | tf_op jit(solution)/shard_map/ppermute | solution.py:37
  47.5 8.3 %collective-permute-start.14 = (f32[128,256]{1,0:T(8,128)S(1)}, f32[128,256]{1,0:T(8,128)S(1)}, u32[]{:S(2)}, u32[]{:S(2)}) collective-permute-start(f32[128,256]{1,0:T(8,128)S(1)} %get-tuple-element.140.p0.state.n0.refs_3_), channel_id=1, source_target_pairs={{0,4},{4,64},{64,68},{68,0},{1,5},{5,65},{65,69},{69,1},{2,6},{6,6... | collective-permute-start | bytes 393224 | tf_op jit(solution)/shard_map/ppermute | solution.py:37
  56.4 18.9 %collective-permute-start.17 = (f32[4,128,256]{2,1,0:T(8,128)S(1)}, f32[4,128,256]{2,1,0:T(8,128)S(1)}, u32[]{:S(2)}, u32[]{:S(2)}) collective-permute-start(f32[4,128,256]{2,1,0:T(8,128)S(1)} %shard_map.153), channel_id=1, source_target_pairs={{0,32},{32,0},{1,33},{33,1},{2,34},{34,2},{3,35},{35,3},{4,36},{36... | collective-permute-start | bytes 1572872 | tf_op jit(solution)/shard_map/ppermute | solution.py:37
  58.2 15.4 %collective-permute-start.4 = (f32[136,512]{1,0:T(8,128)S(1)}, f32[136,512]{1,0:T(8,128)S(1)}, u32[]{:S(2)}, u32[]{:S(2)}) collective-permute-start(f32[136,512]{1,0:T(8,128)S(1)} %get-tuple-element.122), channel_id=1, source_target_pairs={{0,4},{4,64},{64,68},{68,0},{1,5},{5,65},{65,69},{69,1},{2,6},{6,6... | collective-permute-start | bytes 835592 | tf_op jit(solution)/shard_map/ppermute | solution.py:37
  58.3 15.4 %collective-permute-start.5 = (f32[136,512]{1,0:T(8,128)S(1)}, f32[136,512]{1,0:T(8,128)S(1)}, u32[]{:S(2)}, u32[]{:S(2)}) collective-permute-start(f32[136,512]{1,0:T(8,128)S(1)} %get-tuple-element.123), channel_id=1, source_target_pairs={{0,64},{4,68},{64,0},{68,4},{1,65},{5,69},{65,1},{69,5},{2,66},{6,... | collective-permute-start | bytes 835592 | tf_op jit(solution)/shard_map/ppermute | solution.py:37
  59.7 14.3 %collective-permute-start.6 = (f32[136,512]{1,0:T(8,128)S(1)}, f32[136,512]{1,0:T(8,128)S(1)}, u32[]{:S(2)}, u32[]{:S(2)}) collective-permute-start(f32[136,512]{1,0:T(8,128)S(1)} %get-tuple-element.124), channel_id=1, source_target_pairs={{0,68},{4,0},{64,4},{68,64},{1,69},{5,1},{65,5},{69,65},{2,70},{6,... | collective-permute-start | bytes 835592 | tf_op jit(solution)/shard_map/ppermute | solution.py:37
  77.2 7.6 %collective-permute-start.19 = (f32[128,256]{1,0:T(8,128)S(1)}, f32[128,256]{1,0:T(8,128)S(1)}, u32[]{:S(2)}, u32[]{:S(2)}) collective-permute-start(f32[128,256]{1,0:T(8,128)S(1)} %get-tuple-element.143), channel_id=1, source_target_pairs={{0,16},{8,24},{16,0},{24,8},{1,17},{9,25},{17,1},{25,9},{2,18},{10... | collective-permute-start | bytes 393224 | tf_op jit(solution)/shard_map/ppermute | solution.py:37
  85.7 6.8 %collective-permute-start.23 = (f32[128,256]{1,0:T(8,128)S(1)}, f32[128,256]{1,0:T(8,128)S(1)}, u32[]{:S(2)}, u32[]{:S(2)}) collective-permute-start(f32[128,256]{1,0:T(8,128)S(1)} %get-tuple-element.147.p0.state.n1.refs_4_), channel_id=1, source_target_pairs={{0,68},{4,0},{64,4},{68,64},{1,69},{5,1},{65,5},{69,65},{2,70},{6,... | collective-permute-start | bytes 393224 | tf_op jit(solution)/shard_map/ppermute | solution.py:37
  89.6 5.4 %collective-permute-start.22 = (f32[128,256]{1,0:T(8,128)S(1)}, f32[128,256]{1,0:T(8,128)S(1)}, u32[]{:S(2)}, u32[]{:S(2)}) collective-permute-start(f32[128,256]{1,0:T(8,128)S(1)} %get-tuple-element.147.p0.state.n1.refs_4_), channel_id=1, source_target_pairs={{0,64},{4,68},{64,0},{68,4},{1,65},{5,69},{65,1},{69,5},{2,66},{6,... | collective-permute-start | bytes 393224 | tf_op jit(solution)/shard_map/ppermute | solution.py:37
  89.6 8.7 %collective-permute-start.21 = (f32[128,256]{1,0:T(8,128)S(1)}, f32[128,256]{1,0:T(8,128)S(1)}, u32[]{:S(2)}, u32[]{:S(2)}) collective-permute-start(f32[128,256]{1,0:T(8,128)S(1)} %get-tuple-element.147.p0.state.n1.refs_4_), channel_id=1, source_target_pairs={{0,4},{4,64},{64,68},{68,0},{1,5},{5,65},{65,69},{69,1},{2,6},{6,6... | collective-permute-start | bytes 393224 | tf_op jit(solution)/shard_map/ppermute | solution.py:37
  103.0 6.5 %collective-permute-start.25 = (f32[128,256]{1,0:T(8,128)S(1)}, f32[128,256]{1,0:T(8,128)S(1)}, u32[]{:S(2)}, u32[]{:S(2)}) collective-permute-start(f32[128,256]{1,0:T(8,128)S(1)} %get-tuple-element.149), channel_id=1, source_target_pairs={{0,8},{8,16},{16,24},{24,0},{1,9},{9,17},{17,25},{25,1},{2,10},{10... | collective-permute-start | bytes 393224 | tf_op jit(solution)/shard_map/ppermute | solution.py:37
  105.4 7.7 %collective-permute-start.26 = (f32[128,256]{1,0:T(8,128)S(1)}, f32[128,256]{1,0:T(8,128)S(1)}, u32[]{:S(2)}, u32[]{:S(2)}) collective-permute-start(f32[128,256]{1,0:T(8,128)S(1)} %get-tuple-element.150), channel_id=1, source_target_pairs={{0,16},{8,24},{16,0},{24,8},{1,17},{9,25},{17,1},{25,9},{2,18},{10... | collective-permute-start | bytes 393224 | tf_op jit(solution)/shard_map/ppermute | solution.py:37
  107.2 6.0 %collective-permute-start.27 = (f32[128,256]{1,0:T(8,128)S(1)}, f32[128,256]{1,0:T(8,128)S(1)}, u32[]{:S(2)}, u32[]{:S(2)}) collective-permute-start(f32[128,256]{1,0:T(8,128)S(1)} %get-tuple-element.151), channel_id=1, source_target_pairs={{0,24},{8,0},{16,8},{24,16},{1,25},{9,1},{17,9},{25,17},{2,26},{10... | collective-permute-start | bytes 393224 | tf_op jit(solution)/shard_map/ppermute | solution.py:37
  114.7 5.4 %collective-permute-start.29 = (f32[128,256]{1,0:T(8,128)S(1)}, f32[128,256]{1,0:T(8,128)S(1)}, u32[]{:S(2)}, u32[]{:S(2)}) collective-permute-start(f32[128,256]{1,0:T(8,128)S(1)} %get-tuple-element.154.p0.state.n2.refs_5_), channel_id=1, source_target_pairs={{0,64},{4,68},{64,0},{68,4},{1,65},{5,69},{65,1},{69,5},{2,66},{6,... | collective-permute-start | bytes 393224 | tf_op jit(solution)/shard_map/ppermute | solution.py:37
  114.7 9.1 %collective-permute-start.28 = (f32[128,256]{1,0:T(8,128)S(1)}, f32[128,256]{1,0:T(8,128)S(1)}, u32[]{:S(2)}, u32[]{:S(2)}) collective-permute-start(f32[128,256]{1,0:T(8,128)S(1)} %get-tuple-element.154.p0.state.n2.refs_5_), channel_id=1, source_target_pairs={{0,4},{4,64},{64,68},{68,0},{1,5},{5,65},{65,69},{69,1},{2,6},{6,6... | collective-permute-start | bytes 393224 | tf_op jit(solution)/shard_map/ppermute | solution.py:37
  126.1 9.1 %collective-permute-start.35 = (f32[2,64,256]{2,1,0:T(8,128)S(1)}, f32[2,64,256]{2,1,0:T(8,128)S(1)}, u32[]{:S(2)}, u32[]{:S(2)}) collective-permute-start(f32[2,64,256]{2,1,0:T(8,128)S(1)} %get-tuple-element.162), channel_id=1, source_target_pairs={{0,4},{4,64},{64,68},{68,0},{1,5},{5,65},{65,69},{69,1},{2,6},{6,6... | collective-permute-start | bytes 393224 | tf_op jit(solution)/shard_map/ppermute | solution.py:37
  126.2 11.6 %collective-permute-start.36 = (f32[2,64,256]{2,1,0:T(8,128)S(1)}, f32[2,64,256]{2,1,0:T(8,128)S(1)}, u32[]{:S(2)}, u32[]{:S(2)}) collective-permute-start(f32[2,64,256]{2,1,0:T(8,128)S(1)} %get-tuple-element.163), channel_id=1, source_target_pairs={{0,64},{4,68},{64,0},{68,4},{1,65},{5,69},{65,1},{69,5},{2,66},{6,... | collective-permute-start | bytes 393224 | tf_op jit(solution)/shard_map/ppermute | solution.py:37
  127.7 10.1 %collective-permute-start.37 = (f32[2,64,256]{2,1,0:T(8,128)S(1)}, f32[2,64,256]{2,1,0:T(8,128)S(1)}, u32[]{:S(2)}, u32[]{:S(2)}) collective-permute-start(f32[2,64,256]{2,1,0:T(8,128)S(1)} %get-tuple-element.164), channel_id=1, source_target_pairs={{0,68},{4,0},{64,4},{68,64},{1,69},{5,1},{65,5},{69,65},{2,70},{6,... | collective-permute-start | bytes 393224 | tf_op jit(solution)/shard_map/ppermute | solution.py:37
  130.2 9.1 %collective-permute-start.32 = (f32[128,256]{1,0:T(8,128)S(1)}, f32[128,256]{1,0:T(8,128)S(1)}, u32[]{:S(2)}, u32[]{:S(2)}) collective-permute-start(f32[128,256]{1,0:T(8,128)S(1)} %get-tuple-element.156), channel_id=1, source_target_pairs={{0,8},{8,16},{16,24},{24,0},{1,9},{9,17},{17,25},{25,1},{2,10},{10... | collective-permute-start | bytes 393224 | tf_op jit(solution)/shard_map/ppermute | solution.py:37
  131.7 8.1 %collective-permute-start.33 = (f32[128,256]{1,0:T(8,128)S(1)}, f32[128,256]{1,0:T(8,128)S(1)}, u32[]{:S(2)}, u32[]{:S(2)}) collective-permute-start(f32[128,256]{1,0:T(8,128)S(1)} %get-tuple-element.157), channel_id=1, source_target_pairs={{0,16},{8,24},{16,0},{24,8},{1,17},{9,25},{17,1},{25,9},{2,18},{10... | collective-permute-start | bytes 393224 | tf_op jit(solution)/shard_map/ppermute | solution.py:37
  141.3 5.8 %collective-permute-start.40 = (f32[2,64,256]{2,1,0:T(8,128)S(1)}, f32[2,64,256]{2,1,0:T(8,128)S(1)}, u32[]{:S(2)}, u32[]{:S(2)}) collective-permute-start(f32[2,64,256]{2,1,0:T(8,128)S(1)} %get-tuple-element.166.g0), channel_id=1, source_target_pairs={{0,8},{8,16},{16,24},{24,0},{1,9},{9,17},{17,25},{25,1},{2,10},{10... | collective-permute-start | bytes 393224 | tf_op jit(solution)/shard_map/ppermute | solution.py:37
  142.4 7.8 %collective-permute-start.39 = (f32[2,64,256]{2,1,0:T(8,128)S(1)}, f32[2,64,256]{2,1,0:T(8,128)S(1)}, u32[]{:S(2)}, u32[]{:S(2)}) collective-permute-start(f32[2,64,256]{2,1,0:T(8,128)S(1)} %get-tuple-element.166.g0), channel_id=1, source_target_pairs={{0,16},{8,24},{16,0},{24,8},{1,17},{9,25},{17,1},{25,9},{2,18},{10... | collective-permute-start | bytes 393224 | tf_op jit(solution)/shard_map/ppermute | solution.py:37
  156.9 8.8 %collective-permute-start.42 = (f32[2,64,256]{2,1,0:T(8,128)S(1)}, f32[2,64,256]{2,1,0:T(8,128)S(1)}, u32[]{:S(2)}, u32[]{:S(2)}) collective-permute-start(f32[2,64,256]{2,1,0:T(8,128)S(1)} %get-tuple-element.170), channel_id=1, source_target_pairs={{0,4},{4,64},{64,68},{68,0},{1,5},{5,65},{65,69},{69,1},{2,6},{6,6... | collective-permute-start | bytes 393224 | tf_op jit(solution)/shard_map/ppermute | solution.py:37
  157.0 8.8 %collective-permute-start.43 = (f32[2,64,256]{2,1,0:T(8,128)S(1)}, f32[2,64,256]{2,1,0:T(8,128)S(1)}, u32[]{:S(2)}, u32[]{:S(2)}) collective-permute-start(f32[2,64,256]{2,1,0:T(8,128)S(1)} %get-tuple-element.171), channel_id=1, source_target_pairs={{0,64},{4,68},{64,0},{68,4},{1,65},{5,69},{65,1},{69,5},{2,66},{6,... | collective-permute-start | bytes 393224 | tf_op jit(solution)/shard_map/ppermute | solution.py:37
  158.2 8.3 %collective-permute-start.44 = (f32[2,64,256]{2,1,0:T(8,128)S(1)}, f32[2,64,256]{2,1,0:T(8,128)S(1)}, u32[]{:S(2)}, u32[]{:S(2)}) collective-permute-start(f32[2,64,256]{2,1,0:T(8,128)S(1)} %get-tuple-element.172), channel_id=1, source_target_pairs={{0,68},{4,0},{64,4},{68,64},{1,69},{5,1},{65,5},{69,65},{2,70},{6,... | collective-permute-start | bytes 393224 | tf_op jit(solution)/shard_map/ppermute | solution.py:37
  160.7 10.6 %collective-permute-start.48 = (f32[2,64,256]{2,1,0:T(8,128)S(1)}, f32[2,64,256]{2,1,0:T(8,128)S(1)}, u32[]{:S(2)}, u32[]{:S(2)}) collective-permute-start(f32[2,64,256]{2,1,0:T(8,128)S(1)} %get-tuple-element.181), channel_id=1, source_target_pairs={{0,4},{4,64},{64,68},{68,0},{1,5},{5,65},{65,69},{69,1},{2,6},{6,6... | collective-permute-start | bytes 393224 | tf_op jit(solution)/shard_map/ppermute | solution.py:37
  160.9 12.1 %collective-permute-start.49 = (f32[2,64,256]{2,1,0:T(8,128)S(1)}, f32[2,64,256]{2,1,0:T(8,128)S(1)}, u32[]{:S(2)}, u32[]{:S(2)}) collective-permute-start(f32[2,64,256]{2,1,0:T(8,128)S(1)} %get-tuple-element.182), channel_id=1, source_target_pairs={{0,64},{4,68},{64,0},{68,4},{1,65},{5,69},{65,1},{69,5},{2,66},{6,... | collective-permute-start | bytes 393224 | tf_op jit(solution)/shard_map/ppermute | solution.py:37
  165.7 7.3 %collective-permute-start.50 = (f32[2,64,256]{2,1,0:T(8,128)S(1)}, f32[2,64,256]{2,1,0:T(8,128)S(1)}, u32[]{:S(2)}, u32[]{:S(2)}) collective-permute-start(f32[2,64,256]{2,1,0:T(8,128)S(1)} %get-tuple-element.183), channel_id=1, source_target_pairs={{0,68},{4,0},{64,4},{68,64},{1,69},{5,1},{65,5},{69,65},{2,70},{6,... | collective-permute-start | bytes 393224 | tf_op jit(solution)/shard_map/ppermute | solution.py:37
  167.3 5.7 %collective-permute-start.47 = (f32[2,64,256]{2,1,0:T(8,128)S(1)}, f32[2,64,256]{2,1,0:T(8,128)S(1)}, u32[]{:S(2)}, u32[]{:S(2)}) collective-permute-start(f32[2,64,256]{2,1,0:T(8,128)S(1)} %get-tuple-element.178.g0), channel_id=1, source_target_pairs={{0,8},{8,16},{16,24},{24,0},{1,9},{9,17},{17,25},{25,1},{2,10},{10... | collective-permute-start | bytes 393224 | tf_op jit(solution)/shard_map/ppermute | solution.py:37
  167.4 6.6 %collective-permute-start.46 = (f32[2,64,256]{2,1,0:T(8,128)S(1)}, f32[2,64,256]{2,1,0:T(8,128)S(1)}, u32[]{:S(2)}, u32[]{:S(2)}) collective-permute-start(f32[2,64,256]{2,1,0:T(8,128)S(1)} %get-tuple-element.178.g0), channel_id=1, source_target_pairs={{0,16},{8,24},{16,0},{24,8},{1,17},{9,25},{17,1},{25,9},{2,18},{10... | collective-permute-start | bytes 393224 | tf_op jit(solution)/shard_map/ppermute | solution.py:37
  171.3 5.3 %collective-permute-start.45 = (f32[2,64,256]{2,1,0:T(8,128)S(1)}, f32[2,64,256]{2,1,0:T(8,128)S(1)}, u32[]{:S(2)}, u32[]{:S(2)}) collective-permute-start(f32[2,64,256]{2,1,0:T(8,128)S(1)} %get-tuple-element.178.g0), channel_id=1, source_target_pairs={{0,24},{8,0},{16,8},{24,16},{1,25},{9,1},{17,9},{25,17},{2,26},{10... | collective-permute-start | bytes 393224 | tf_op jit(solution)/shard_map/ppermute | solution.py:37
  182.8 6.8 %collective-permute-start.52 = (f32[2,64,256]{2,1,0:T(8,128)S(1)}, f32[2,64,256]{2,1,0:T(8,128)S(1)}, u32[]{:S(2)}, u32[]{:S(2)}) collective-permute-start(f32[2,64,256]{2,1,0:T(8,128)S(1)} %get-tuple-element.188), channel_id=1, source_target_pairs={{0,4},{4,64},{64,68},{68,0},{1,5},{5,65},{65,69},{69,1},{2,6},{6,6... | collective-permute-start | bytes 393224 | tf_op jit(solution)/shard_map/ppermute | solution.py:37
  184.3 9.0 %collective-permute-start.53 = (f32[2,64,256]{2,1,0:T(8,128)S(1)}, f32[2,64,256]{2,1,0:T(8,128)S(1)}, u32[]{:S(2)}, u32[]{:S(2)}) collective-permute-start(f32[2,64,256]{2,1,0:T(8,128)S(1)} %get-tuple-element.189), channel_id=1, source_target_pairs={{0,64},{4,68},{64,0},{68,4},{1,65},{5,69},{65,1},{69,5},{2,66},{6,... | collective-permute-start | bytes 393224 | tf_op jit(solution)/shard_map/ppermute | solution.py:37
  187.2 6.0 %collective-permute-start.54 = (f32[2,64,256]{2,1,0:T(8,128)S(1)}, f32[2,64,256]{2,1,0:T(8,128)S(1)}, u32[]{:S(2)}, u32[]{:S(2)}) collective-permute-start(f32[2,64,256]{2,1,0:T(8,128)S(1)} %get-tuple-element.190), channel_id=1, source_target_pairs={{0,68},{4,0},{64,4},{68,64},{1,69},{5,1},{65,5},{69,65},{2,70},{6,... | collective-permute-start | bytes 393224 | tf_op jit(solution)/shard_map/ppermute | solution.py:37
  194.4 7.9 %collective-permute-start.56 = (f32[2,64,256]{2,1,0:T(8,128)S(1)}, f32[2,64,256]{2,1,0:T(8,128)S(1)}, u32[]{:S(2)}, u32[]{:S(2)}) collective-permute-start(f32[2,64,256]{2,1,0:T(8,128)S(1)} %get-tuple-element.196.g0), channel_id=1, source_target_pairs={{0,16},{8,24},{16,0},{24,8},{1,17},{9,25},{17,1},{25,9},{2,18},{10... | collective-permute-start | bytes 393224 | tf_op jit(solution)/shard_map/ppermute | solution.py:37
  208.5 6.3 %collective-permute-start.59 = (f32[2,64,256]{2,1,0:T(8,128)S(1)}, f32[2,64,256]{2,1,0:T(8,128)S(1)}, u32[]{:S(2)}, u32[]{:S(2)}) collective-permute-start(f32[2,64,256]{2,1,0:T(8,128)S(1)} %get-tuple-element.200), channel_id=1, source_target_pairs={{0,4},{4,64},{64,68},{68,0},{1,5},{5,65},{65,69},{69,1},{2,6},{6,6... | collective-permute-start | bytes 393224 | tf_op jit(solution)/shard_map/ppermute | solution.py:37
  209.5 9.0 %collective-permute-start.60 = (f32[2,64,256]{2,1,0:T(8,128)S(1)}, f32[2,64,256]{2,1,0:T(8,128)S(1)}, u32[]{:S(2)}, u32[]{:S(2)}) collective-permute-start(f32[2,64,256]{2,1,0:T(8,128)S(1)} %get-tuple-element.201), channel_id=1, source_target_pairs={{0,64},{4,68},{64,0},{68,4},{1,65},{5,69},{65,1},{69,5},{2,66},{6,... | collective-permute-start | bytes 393224 | tf_op jit(solution)/shard_map/ppermute | solution.py:37
  212.5 6.0 %collective-permute-start.61 = (f32[2,64,256]{2,1,0:T(8,128)S(1)}, f32[2,64,256]{2,1,0:T(8,128)S(1)}, u32[]{:S(2)}, u32[]{:S(2)}) collective-permute-start(f32[2,64,256]{2,1,0:T(8,128)S(1)} %get-tuple-element.202), channel_id=1, source_target_pairs={{0,68},{4,0},{64,4},{68,64},{1,69},{5,1},{65,5},{69,65},{2,70},{6,... | collective-permute-start | bytes 393224 | tf_op jit(solution)/shard_map/ppermute | solution.py:37
  262.2 5.6 %collective-permute-start.66 = (f32[16,40,256]{2,1,0:T(8,128)S(1)}, f32[16,40,256]{2,1,0:T(8,128)S(1)}, u32[]{:S(2)}, u32[]{:S(2)}) collective-permute-start(f32[16,40,256]{2,1,0:T(8,128)S(1)} %all_to_all.11), channel_id=1, source_target_pairs={{0,32},{32,0},{1,33},{33,1},{2,34},{34,2},{3,35},{35,3},{4,36},{36... | collective-permute-start | bytes 1966088 | tf_op jit(solution)/shard_map/ppermute | solution.py:37
  (27 other events, 190.7 us)
